TPU v7x, 32 devices: a whole 2x2x4 slice. The times are simulated.
32 devices in a mesh: dom: 16 (over z, x, core), feat: 2 (over y).
Axes of the slice: x: 2, y: 2, z: 4, core: 2. Of those that a mesh axis runs over, the one named last changes fastest.
Arguments:
- features: bfloat16 [512, 49152], P('feat', 'dom'), may hold values from -6 to 6
- weights: bfloat16 [2, 512, 512], replicated, may hold values from -0.1875 to 0.1875
- tile_values: bfloat16 [1152, 128, 128], P('dom'), may hold values from 0 to 0.099609375
- tile_blocks: int32 [1152, 2], P('dom'), may hold values from 0 to 25
- tile_counts: int32 [16], P('dom'), may hold values from 36 to 72
- replica: int32 [16, 16, 16], P('dom'), may hold values from -1 to 3071, as said below
- cotangent: bfloat16 [512, 49152], P(None, ('dom', 'feat')), may hold values from -6 to 6
Outputs:
- output: bfloat16 [512, 49152], P(None, ('dom', 'feat'))
- feature_grad: bfloat16 [512, 49152], P('feat', 'dom')
- weight_grad: float32 [2, 512, 512], P(None, 'feat')
Inputs may be any that keep to these rules, and one draw needn't show every extreme that they name: `tile_blocks`: column 0 names a tile's source block and column 1 its destination block. replica[q, p, k] is the master slot on partition q of the vertex in mirror slot q * 16 + k of partition p, or -1 for an unused slot; the used slots of a pair (q, p) come first; no partition mirrors its own masters; each master partition fills all 16 slots toward at least one partition.
All inputs are finite; a program needn't handle non-finite values.
Results may differ from a plain program's by a relative error of at most 0.0058.
Values may be sent and summed in bfloat16 or wider, within the bound.
No kernel may reach another device: no remote copies, remote signals or barrier semaphores. Data moves between devices by JAX's collectives and lax.ppermute only.
A program may use at most 64 MiB of HBM per device.

v0:
```python
import functools

import jax
import jax.numpy as jnp
from jax import lax
from jax.experimental import pallas as pl
from jax.experimental.pallas import tpu as pltpu
from jax.sharding import PartitionSpec as P

BF = jnp.bfloat16
F32 = jnp.float32
GROUP = 8


def dot(a, b, ca=1, cb=0):
    return lax.dot_general(a, b, (((ca,), (cb,)), ((), ())), preferred_element_type=F32)


def eye(n):
    rows = lax.broadcasted_iota(jnp.int32, (n, n), 0)
    cols = lax.broadcasted_iota(jnp.int32, (n, n), 1)
    return jnp.where(rows == cols, 1.0, 0.0).astype(BF)


def picks(slots, start, height):
    rows = lax.broadcasted_iota(jnp.int32, (height, slots.shape[1]), 0) + start
    return jnp.where(rows == slots, 1.0, 0.0).astype(BF)


def flip(x):
    return dot(eye(x.shape[1]), x, 1, 1).astype(BF)


SMEM = pl.BlockSpec(memory_space=pltpu.SMEM)
ANY = pl.BlockSpec(memory_space=pl.ANY)


def full(x):
    zeros = (0,) * len(x.shape)
    return pl.BlockSpec(x.shape, lambda *_: zeros)


def cost(flops, nbytes):
    return pl.CostEstimate(flops=int(flops), bytes_accessed=int(nbytes), transcendentals=0)


def block_of(n):
    return next(b for b in (512, 256, 128) if n % b == 0)


def list_tiles(blocks, count, lists, source_col, trash):
    tiles, sources, targets = lists

    def step(t, _):
        tiles[t] = t
        sources[t] = blocks[source_col, t]
        targets[t] = blocks[1 - source_col, t]
        return 0

    lax.fori_loop(0, count, step, 0)
    for u in range(GROUP):
        tiles[count + u] = 0
        sources[count + u] = 0
        targets[count + u] = trash


def run_tiles(n, lists, values, tile_dim, x_all, acc, tile):
    tiles, sources, targets = lists

    def step(g, _):
        for u in range(GROUP):
            at = g * GROUP + u
            picked = column(x_all, sources[at], tile)
            part = dot(picked, values[tiles[at]], 1, tile_dim)
            col = pl.ds(pl.multiple_of(targets[at] * tile, tile), tile)
            acc[:, col] += part
        return 0

    lax.fori_loop(0, (n + GROUP - 1) // GROUP, step, 0)


def column(ref, block, tile):
    at = pl.multiple_of(block * tile, tile)
    return ref[:, pl.ds(at, tile)]


def prep_kernel(nf, x_ref, rep_ref, pull_ref, *halves):
    h = lax.axis_index("feat")
    _, masters = x_ref.shape
    width = halves[0].shape[1]
    step = block_of(masters)
    total = None
    for at in range(0, masters, step):
        part = dot(x_ref[:, at : at + step], picks(rep_ref[...], at, step))
        total = part if total is None else total + part
    pull_ref[...] = flip(total.astype(BF)).reshape(pull_ref.shape)
    for j in range(nf):
        at = pl.multiple_of(lax.rem(h + j, nf) * width, 128)
        halves[j][...] = x_ref[:, pl.ds(at, width)]


def spread_kernel(nf, nc, tile, blocks, count, mirrors, x_ref, values_ref, *rest):
    own_ref, push_ref = rest[:2]
    rest = rest[2:]
    sends = rest[: (nf - 1) * nc]
    acc, x_all, values, tiles, sources, targets, sems = rest[(nf - 1) * nc :]
    lists = (tiles, sources, targets)
    h = lax.axis_index("feat")
    feats, masters = x_ref.shape
    width = own_ref.shape[1]
    slots = x_all.shape[1] - masters
    copies = [
        pltpu.make_async_copy(x_ref, x_all.at[:, :masters], sems.at[0]),
        pltpu.make_async_copy(values_ref, values, sems.at[1]),
    ]
    for copy in copies:
        copy.start()
    acc[...] = jnp.zeros_like(acc)
    x_all[:, masters:] = flip(mirrors[...].reshape(slots, feats))
    list_tiles(blocks, count[0], lists, 0, acc.shape[1] // tile - 1)
    for copy in copies:
        copy.wait()
    run_tiles(count[0], lists, values, 0, x_all, acc, tile)
    part = width // nc
    for j in range(1, nf):
        for c in range(nc):
            at = pl.multiple_of(lax.rem(h + j, nf) * width + c * part, 128)
            sends[(j - 1) * nc + c][...] = acc[:, pl.ds(at, part)].astype(BF)
    push = flip(acc[:, masters : masters + slots].astype(BF))
    push = push.reshape(push_ref.shape[0], push_ref.shape[2], feats)
    for f in range(nf):
        push_ref[:, f] = push
    own_ref[...] = acc[:, pl.ds(pl.multiple_of(h * width, 128), width)].astype(BF)


def dense_kernel(nf, nc, c, *refs):
    rep_ref, wt_ref, w_ref, inc_ref, cot_ref = refs[:5]
    xs, parts = refs[5 : 5 + nf], refs[5 + nf : 5 + 2 * nf]
    refs = refs[5 + 2 * nf :]
    if c:
        pay_in = refs[0]
        refs = refs[2:]
    rows, out_ref, g_ref, pay_ref = refs[:4]
    grads, selfs = refs[4 : 4 + nf], refs[4 + nf : 4 + 2 * nf]
    both, inc, pay = refs[4 + 2 * nf :]
    h = lax.axis_index("feat")
    i = pl.program_id(0)
    feats, step = grads[0].shape
    wide = g_ref.shape[0]
    slots = rep_ref.shape[1]
    part = step * pl.num_programs(0)

    @pl.when(i == 0)
    def _():
        for f in range(nf):
            inc[f] = flip(inc_ref[:, f].reshape(slots, feats))
        pay[...] = pay_in[...].astype(F32) if c else jnp.zeros_like(pay)

    pick = picks(rep_ref[...], (h * nc + c) * part + i * step, step)
    for j in range(nf):
        f = lax.rem(h - j + nf, nf)
        at = pl.multiple_of(f * feats, feats)
        total = parts[j][...].astype(F32) + dot(inc[f], pick, 1, 1)
        rows[pl.ds(at, feats), :] = xs[j][...]
        rows[pl.ds(wide + at, feats), :] = total.astype(BF)
    z = dot(wt_ref[...], rows[...])
    s = jax.nn.sigmoid(z)
    out_ref[...] = (z * s).astype(BF)
    g = (cot_ref[...].astype(F32) * (s * (1.0 + z * (1.0 - s)))).astype(BF)
    g_ref[...] = g
    both[...] = dot(w_ref[...], g).astype(BF)
    for j in range(nf):
        at = pl.multiple_of(lax.rem(h + j, nf) * feats, feats)
        grads[j][...] = both[pl.ds(wide + at, feats), :]
        selfs[j][...] = both[pl.ds(at, feats), :]
    pay[...] += dot(both[wide:, :], pick)

    @pl.when(i == pl.num_programs(0) - 1)
    def _():
        if c + 1 < nc:
            pay_ref[...] = pay[...].astype(BF)
        else:
            for f in range(nf):
                mine = flip(pay[f * feats : (f + 1) * feats].astype(BF))
                pay_ref[:, f] = mine.reshape(pay_ref.shape[0], pay_ref.shape[2], feats)


def weight_kernel(nf, nc, *refs):
    keep_ref, send_ref, acc = refs[2 * nc :]
    h = lax.axis_index("feat")
    bit = lax.rem(lax.axis_index("dom"), 2)
    wide = acc.shape[1]
    feats = wide // nf
    total = dot(refs[0][...], refs[nc][...], 1, 1)
    for c in range(1, nc):
        total = total + dot(refs[c][...], refs[nc + c][...], 1, 1)
    acc[...] = total
    for j in range(nf):
        at = lax.rem(h + j, nf) * feats
        keep_ref[j] = acc[pl.ds(pl.multiple_of(bit * wide + at, feats), feats), :]
        send_ref[j] = acc[pl.ds(pl.multiple_of((1 - bit) * wide + at, feats), feats), :].astype(BF)


def back_kernel(nf, nc, tile, blocks, count, mirrors, values_ref, *rest):
    grads = rest[: nf * nc]
    back_ref, push_ref, acc, x_all, values, tiles, sources, targets, sems = rest[nf * nc :]
    lists = (tiles, sources, targets)
    h = lax.axis_index("feat")
    feats, masters = back_ref.shape
    slots = x_all.shape[1] - masters
    part = masters // nf // nc
    copies = [pltpu.make_async_copy(values_ref, values, sems.at[nf * nc])]
    for j in range(nf):
        for c in range(nc):
            k = j * nc + c
            at = pl.multiple_of((lax.rem(h - j + nf, nf) * nc + c) * part, 128)
            copies.append(
                pltpu.make_async_copy(grads[k], x_all.at[:, pl.ds(at, part)], sems.at[k])
            )
    for copy in copies:
        copy.start()
    acc[...] = jnp.zeros_like(acc)
    total = mirrors[:, 0].astype(F32)
    for f in range(1, nf):
        total = total + mirrors[:, f].astype(F32)
    x_all[:, masters:] = flip(total.astype(BF).reshape(slots, feats))
    list_tiles(blocks, count[0], lists, 1, acc.shape[1] // tile - 1)
    for copy in copies:
        copy.wait()
    run_tiles(count[0], lists, values, 1, x_all, acc, tile)
    partial = acc[:, masters : masters + slots].astype(BF)
    push_ref[...] = flip(partial).reshape(push_ref.shape)
    back_ref[...] = acc[:, :masters].astype(BF)


def final_kernel(nf, nc, rep_ref, inc_ref, back_ref, *rest):
    selfs, out_ref = rest[: nf * nc], rest[nf * nc]
    h = lax.axis_index("feat")
    feats, part = selfs[0].shape
    slots = rep_ref.shape[1]
    inc = flip(inc_ref[...].reshape(slots, feats))
    for j in range(nf):
        for c in range(nc):
            at = pl.multiple_of((lax.rem(h - j + nf, nf) * nc + c) * part, 128)
            back = back_ref[:, pl.ds(at, part)].astype(F32)
            back = back + dot(inc, picks(rep_ref[...], at, part), 1, 1)
            own = selfs[j * nc + c][...].astype(F32)
            out_ref[:, pl.ds(at, part)] = (own + back).astype(BF)


def local(nd, nf, features, weights, tile_values, tile_blocks, tile_counts, replica, cotangent):
    feats, masters = features.shape
    wide = weights.shape[1]
    ntiles, tile, _ = tile_values.shape
    per = replica.shape[2]
    slots = nd * per
    width = masters // nf
    cols = masters + slots + tile
    nc = 2 if width % (2 * tile) == 0 else 1
    part = width // nc
    d = lax.axis_index("dom")
    sd = jax.ShapeDtypeStruct
    lists = [pltpu.SMEM((ntiles + GROUP,), jnp.int32)] * 3
    rep = replica.reshape(1, slots)
    tile_flops = 2 * ntiles * feats * tile * tile

    def call(body, flops, args, specs, outs, scratch=(), grid=(), out_specs=None, alias={}):
        return pl.pallas_call(
            body,
            grid=grid,
            in_specs=[full(a) if p is None else p for a, p in zip(args, specs, strict=True)],
            out_specs=out_specs or [full(o) for o in outs],
            out_shape=outs,
            scratch_shapes=list(scratch),
            input_output_aliases=alias,
            cost_estimate=cost(flops, 2 * sum(a.size for a in args)),
        )(*args)

    def to_peer(x, j):
        return lax.ppermute(x, "feat", [(i, (i + j) % nf) for i in range(nf)])

    def exchange(x, axes):
        flat = x.reshape(-1, per, feats)
        return lax.all_to_all(flat, axes, 0, 0, tiled=True).reshape(x.shape)

    def tile_scratch(nsems):
        return [
            pltpu.VMEM((feats, cols), F32),
            pltpu.VMEM((feats, masters + slots), BF),
            pltpu.VMEM(tile_values.shape, BF),
            *lists,
            pltpu.SemaphoreType.DMA((nsems,)),
        ]

    vec = sd((feats, width), BF)
    pull, *x_halves = call(
        functools.partial(prep_kernel, nf),
        2 * slots * feats * masters,
        [features, rep],
        [None] * 2,
        [sd((nd, per, feats), BF)] + [vec] * nf,
    )
    mirrors = exchange(pull, "dom")
    x_parts = [x_halves[0]] + [to_peer(x_halves[j], j) for j in range(1, nf)]

    blocks = tile_blocks.T
    chunk = sd((feats, part), BF)
    own_part, push, *part_sends = call(
        functools.partial(spread_kernel, nf, nc, tile),
        tile_flops,
        [blocks, tile_counts, mirrors, features, tile_values],
        [SMEM, SMEM, None, ANY, ANY],
        [vec, sd((nd, nf, per, feats), BF)] + [chunk] * ((nf - 1) * nc),
        tile_scratch(nf * nc + 1),
    )
    part_recv = [
        [to_peer(part_sends[(j - 1) * nc + c], j) for j in range(1, nf)]
        for c in range(nc)
    ]
    incoming = exchange(push, ("dom", "feat"))

    flat_w = weights.reshape(2 * wide, wide)
    wt = flat_w.T
    rows, grads, grad_own, grad_recv, self_own, self_recv = [], [], [], [], [], []
    vb = 256 if part % 256 == 0 else 128
    steps = part // vb

    def of_all(height, c):
        return pl.BlockSpec((height, vb), lambda i: (0, c * steps + i))

    def of_chunk(height):
        return pl.BlockSpec((height, vb), lambda i: (0, i))

    for c in range(nc):
        last = c + 1 == nc
        args = [rep, wt, flat_w, incoming, cotangent, *x_parts, own_part, *part_recv[c]]
        specs = [None] * 4 + [of_all(wide, c)] + [of_all(feats, c)] * (nf + 1)
        specs += [of_chunk(feats)] * (nf - 1)
        alias = {}
        if c:
            alias = {len(args) + 1: 1}
            args += [pay, output]
            specs += [None, ANY]
        outs = [
            sd((2 * wide, part), BF),
            sd((wide, width), BF),
            sd((wide, part), BF),
            sd((nd, nf, per, feats) if last else (wide, slots), BF),
        ] + [chunk] * (2 * nf)
        out_specs = [of_chunk(2 * wide), of_all(wide, c), of_chunk(wide), full(outs[3])]
        out_specs += [of_chunk(feats)] * (2 * nf)
        rows_c, output, g_c, pay, *res = call(
            functools.partial(dense_kernel, nf, nc, c),
            8 * wide * wide * part,
            args,
            specs,
            outs,
            [
                pltpu.VMEM((2 * wide, vb), BF),
                pltpu.VMEM((nf, feats, slots), BF),
                pltpu.VMEM((wide, slots), F32),
            ],
            (steps,),
            out_specs,
            alias,
        )
        rows.append(rows_c)
        grads.append(g_c)
        grad_own.append(res[0])
        self_own.append(res[nf])
        grad_recv.append([to_peer(res[j], j) for j in range(1, nf)])
        self_recv.append([to_peer(res[nf + j], j) for j in range(1, nf)])
    grad_mirrors = exchange(pay, ("dom", "feat"))

    keep, send = call(
        functools.partial(weight_kernel, nf, nc),
        4 * wide * wide * width,
        rows + grads,
        [None] * (2 * nc),
        [sd((nf, feats, wide), F32), sd((nf, feats, wide), BF)],
        [pltpu.VMEM((2 * wide, wide), F32)],
    )

    flat_grads = grad_own + [grad_recv[c][j] for j in range(nf - 1) for c in range(nc)]
    back, push = call(
        functools.partial(back_kernel, nf, nc, tile),
        tile_flops,
        [blocks, tile_counts, grad_mirrors, tile_values, *flat_grads],
        [SMEM, SMEM, None, ANY] + [ANY] * (nf * nc),
        [sd((feats, masters), BF), sd((nd, per, feats), BF)],
        tile_scratch(nf * nc + 1),
    )
    back_in = exchange(push, "dom")

    bits = [1 << k for k in range(nd.bit_length() - 1)]

    def swap(x, b):
        return lax.ppermute(x, "dom", [(i, i ^ b) for i in range(nd)])

    for b in bits:
        cur = keep + swap(send, b).astype(F32)
        if b == bits[-1]:
            break
        bit = lax.rem(d // (2 * b), 2)
        size = cur.shape[1] // 2
        wire = F32 if 4 * b >= nd else BF
        keep = lax.dynamic_slice_in_dim(cur, bit * size, size, 1)
        send = lax.dynamic_slice_in_dim(cur, (1 - bit) * size, size, 1).astype(wire)
    total = cur[0]
    for j in range(1, nf):
        total = total + to_peer(cur[j], j)
    total = total.astype(BF)
    for b in reversed(bits):
        bit = lax.rem(d // b, 2)
        other = swap(total, b)
        total = jnp.where(
            bit == 0, jnp.concatenate([total, other], 0), jnp.concatenate([other, total], 0)
        )
    weight_grad = total.reshape(2, feats, wide).astype(F32)

    selfs = [self_own[c] for c in range(nc)]
    selfs += [self_recv[c][j] for j in range(nf - 1) for c in range(nc)]
    (feature_grad,) = call(
        functools.partial(final_kernel, nf, nc),
        2 * slots * feats * masters,
        [rep, back_in, back, *selfs],
        [None] * (3 + nf * nc),
        [sd((feats, masters), BF)],
    )
    return output, feature_grad, weight_grad


def solution(mesh):
    return jax.shard_map(
        functools.partial(local, mesh.shape["dom"], mesh.shape["feat"]),
        mesh=mesh,
        in_specs=(
            P("feat", "dom"),
            P(),
            P("dom", None, None),
            P("dom", None),
            P("dom"),
            P("dom", None, None),
            P(None, ("dom", "feat")),
        ),
        out_specs=(P(None, ("dom", "feat")), P("feat", "dom"), P(None, "feat", None)),
        check_vma=False,
    )
```

profile of v0, /device:TPU:0, one launch (start us, length us, event | category | flops | bytes accessed | tf_op | source)
XLA Modules:
  0.0 151.9 jit_solution(13372196551542083881)
XLA Ops:
  0.6 1.3 reshape.31.rep_ref.refs_0_
  1.9 3.4 %shard_map.94 = (bf16[16,16,256]{2,1,0:T(8,128)(2,1)}, bf16[256,1536]{1,0:T(8,128)(2,1)}, bf16[256,1536]{1,0:T(8,128)(2,1)}) custom-call(bf16[256,3072]{1,0:T(8,128)(2,1)} %x_ref.3, s32[1,256]{1,0:T(1,128)} %reshape.31.rep_ref.refs_0_), custom_call_target="tpu_custom_call" | custom-call | flops 402653184 | bytes 1573376 | tf_op jit(solution)/shard_map/pallas_call | solution.py:268
  5.3 7.4 %all-to-all-start = ((bf16[16,16,256]{2,1,0:T(8,128)(2,1)}), bf16[16,16,256]{2,1,0:T(8,128)(2,1)S(1)}, u32[]{:S(2)}, u32[]{:S(2)}) async-start(bf16[16,16,256]{2,1,0:T(8,128)(2,1)} %get-tuple-element.30), calls=%async_computation | async-start | bytes 262144 | tf_op jit(solution)/shard_map/all_to_all | solution.py:284
  12.7 1.6 %collective-permute-start = (bf16[256,1536]{1,0:T(8,128)(2,1)}, bf16[256,1536]{1,0:T(8,128)(2,1)S(1)}, u32[]{:S(2)}, u32[]{:S(2)}) collective-permute-start(bf16[256,1536]{1,0:T(8,128)(2,1)} %get-tuple-element.33), channel_id=1, source_target_pairs={{0,1},{1,0},{2,3},{3,2},{4,5},{5,4},{6,7},{7,6},{8,9},{9,8},{10,11... | collective-permute-start | bytes 2359304 | tf_op jit(solution)/shard_map/ppermute | solution.py:280
  15.0 5.7 %all-to-all-done.mirrors = bf16[16,16,256]{2,1,0:T(8,128)(2,1)S(1)} async-done(((bf16[16,16,256]{2,1,0:T(8,128)(2,1)}), bf16[16,16,256]{2,1,0:T(8,128)(2,1)S(1)}, u32[]{:S(2)}, u32[]{:S(2)}) %all-to-all-start) | async-done | bytes 131104 | tf_op jit(solution)/shard_map/all_to_all | solution.py:284
  21.3 7.4 %shard_map.95 = (bf16[256,1536]{1,0:T(8,128)(2,1)}, bf16[16,2,16,256]{3,2,1,0:T(8,128)(2,1)}, bf16[256,768]{1,0:T(8,128)(2,1)}, bf16[256,768]{1,0:T(8,128)(2,1)}) custom-call(s32[2,72]{1,0:T(2,128)} %bitcast.26, s32[1]{0:T(128)S(6)} %copy.14.count, bf16[16,16,256]{2,1,0:T(8,128)(2,1)} %copy-done.4, bf16[256,3072]{1,0:T(8,128)(2,1)} %x_ref.3, ...), custom_call_target="tpu_custom_call" | custom-call | flops 603979776 | bytes 4063522 | tf_op jit(solution)/shard_map/pallas_call | solution.py:268
  28.7 2.6 %all-to-all-start.1 = ((bf16[32,16,256]{2,1,0:T(8,128)(2,1)}), bf16[32,16,256]{2,1,0:T(8,128)(2,1)S(1)}, u32[]{:S(2)}, u32[]{:S(2)}) async-start(bf16[32,16,256]{2,1,0:T(8,128)(2,1)} %bitcast.25), calls=%async_computation.1 | async-start | bytes 524288 | tf_op jit(solution)/shard_map/all_to_all | solution.py:284
  31.3 1.7 %collective-permute-start.2 = (bf16[256,768]{1,0:T(8,128)(2,1)}, bf16[256,768]{1,0:T(8,128)(2,1)S(1)}, u32[]{:S(2)}, u32[]{:S(2)}) collective-permute-start(bf16[256,768]{1,0:T(8,128)(2,1)} %get-tuple-element.36), channel_id=1, source_target_pairs={{0,1},{1,0},{2,3},{3,2},{4,5},{5,4},{6,7},{7,6},{8,9},{9,8},{10,11... | collective-permute-start | bytes 1179656 | tf_op jit(solution)/shard_map/ppermute | solution.py:280
  34.7 11.2 %collective-permute-done.2.refs_8_ = bf16[256,768]{1,0:T(8,128)(2,1)S(1)} collective-permute-done((bf16[256,768]{1,0:T(8,128)(2,1)}, bf16[256,768]{1,0:T(8,128)(2,1)S(1)}, u32[]{:S(2)}, u32[]{:S(2)}) %collective-permute-start.2) | collective-permute-done | bytes 393248 | tf_op jit(solution)/shard_map/ppermute | solution.py:280
  47.1 8.9 %shard_map.96 = (bf16[1024,768]{1,0:T(8,128)(2,1)}, bf16[512,1536]{1,0:T(8,128)(2,1)}, bf16[512,768]{1,0:T(8,128)(2,1)}, bf16[512,256]{1,0:T(8,128)(2,1)}, bf16[...) custom-call(s32[1,256]{1,0:T(1,128)} %reshape.31.rep_ref.refs_0_, ...), custom_call_target="tpu_custom_call" | custom-call | flops 1610612736 | bytes 6685184 | tf_op jit(solution)/shard_map/pallas_call | solution.py:268
  56.7 9.2 %shard_map.97 = (bf16[1024,768]{1,0:T(8,128)(2,1)}, bf16[512,1536]{1,0:T(8,128)(2,1)}, bf16[512,768]{1,0:T(8,128)(2,1)}, bf16[16,2,16,256]{3,2,1,0:T(8,128)(2,1)...) custom-call(s32[1,256]{1,0:T(1,128)} %reshape.31.rep_ref.refs_0_, ...), custom_call_target="tpu_custom_call", output_to_operand_aliasing={{1}: (10, {})} | custom-call | flops 1610612736 | bytes 8520192 | tf_op jit(solution)/shard_map/pallas_call | solution.py:268
  66.0 5.5 %shard_map.100 = (f32[2,256,512]{2,1,0:T(8,128)}, bf16[2,256,512]{2,1,0:T(8,128)(2,1)}) custom-call(bf16[1024,768]{1,0:T(8,128)(2,1)} %get-tuple-element.51.refs_0_, bf16[1024,768]{1,0:T(8,128)(2,1)} %get-tuple-element.52.refs_1_, bf16[512,768]{1,0:T(8,128)(2,1)} %get-tuple-element.53.refs_2_, bf16[512,768]{1,0:T(8,128)(2,1)} %get-tuple-element.54.refs_3_), custom_call_target="tpu_custom_call" | custom-call | flops 1610612736 | bytes 4718592 | tf_op jit(solution)/shard_map/pallas_call | solution.py:268
  71.4 2.1 %collective-permute-done.7 = bf16[2,256,512]{2,1,0:T(8,128)(2,1)S(1)} collective-permute-done((bf16[2,256,512]{2,1,0:T(8,128)(2,1)}, bf16[2,256,512]{2,1,0:T(8,128)(2,1)S(1)}, u32[]{:S(2)}, u32[]{:S(2)}) %collective-permute-start.7) | collective-permute-done | bytes 524320 | tf_op jit(solution)/shard_map/ppermute | solution.py:398
  73.6 1.4 convert_add_fusion
  76.3 7.1 %collective-permute-done.8 = bf16[2,128,512]{2,1,0:T(8,128)(2,1)S(1)} collective-permute-done((bf16[2,128,512]{2,1,0:T(8,128)(2,1)S(1)}, bf16[2,128,512]{2,1,0:T(8,128)(2,1)S(1)}, u32[]{:S(2)}, u32[]{:S(2)}) %collective-permute-start.8) | collective-permute-done | bytes 262176 | tf_op jit(solution)/shard_map/ppermute | solution.py:398
  83.5 1.7 %collective-permute-start.9 = (bf16[2,64,512]{2,1,0:T(8,128)(2,1)S(1)}, bf16[2,64,512]{2,1,0:T(8,128)(2,1)S(1)}, u32[]{:S(2)}, u32[]{:S(2)}) collective-permute-start(bf16[2,64,512]{2,1,0:T(8,128)(2,1)S(1)} %dynamic-slice_convert_fusion.1), channel_id=1, source_target_pairs={{0,8},{2,10},{4,12},{6,14},{8,0},{10,2},{12,4},{14,6},{16,24},{18,... | collective-permute-start | bytes 393224 | tf_op jit(solution)/shard_map/ppermute | solution.py:398
  85.2 3.4 %collective-permute-done.9 = bf16[2,64,512]{2,1,0:T(8,128)(2,1)S(1)} collective-permute-done((bf16[2,64,512]{2,1,0:T(8,128)(2,1)S(1)}, bf16[2,64,512]{2,1,0:T(8,128)(2,1)S(1)}, u32[]{:S(2)}, u32[]{:S(2)}) %collective-permute-start.9) | collective-permute-done | bytes 131104 | tf_op jit(solution)/shard_map/ppermute | solution.py:398
  88.6 2.6 %collective-permute-start.10 = (f32[2,32,512]{2,1,0:T(8,128)S(1)}, f32[2,32,512]{2,1,0:T(8,128)S(1)}, u32[]{:S(2)}, u32[]{:S(2)}) collective-permute-start(f32[2,32,512]{2,1,0:T(8,128)S(1)} %constant_dynamic-slice_fusion), channel_id=1, source_target_pairs={{0,16},{2,18},{4,20},{6,22},{8,24},{10,26},{12,28},{14,30},{16,0},... | collective-permute-start | bytes 393224 | tf_op jit(solution)/shard_map/ppermute | solution.py:398
  91.2 4.8 %collective-permute-done.10 = f32[2,32,512]{2,1,0:T(8,128)S(1)} collective-permute-done((f32[2,32,512]{2,1,0:T(8,128)S(1)}, f32[2,32,512]{2,1,0:T(8,128)S(1)}, u32[]{:S(2)}, u32[]{:S(2)}) %collective-permute-start.10) | collective-permute-done | bytes 131104 | tf_op jit(solution)/shard_map/ppermute | solution.py:398
  97.2 4.5 %all-to-all-start.2 = ((bf16[32,16,256]{2,1,0:T(8,128)(2,1)}), bf16[32,16,256]{2,1,0:T(8,128)(2,1)S(1)}, u32[]{:S(2)}, u32[]{:S(2)}) async-start(bf16[32,16,256]{2,1,0:T(8,128)(2,1)} %bitcast.5), calls=%async_computation.2 | async-start | bytes 524288 | tf_op jit(solution)/shard_map/all_to_all | solution.py:284
  101.7 2.7 %collective-permute-start.12 = (bf16[32,512]{1,0:T(8,128)(2,1)S(1)}, bf16[32,512]{1,0:T(8,128)(2,1)S(1)}, u32[]{:S(2)}, u32[]{:S(2)}) collective-permute-start(bf16[32,512]{1,0:T(8,128)(2,1)S(1)} %fusion.1), channel_id=1, source_target_pairs={{0,16},{2,18},{4,20},{6,22},{8,24},{10,26},{12,28},{14,30},{16,0},... | collective-permute-start | bytes 98312 | tf_op jit(solution)/shard_map/ppermute | solution.py:398
  104.4 1.5 collective-permute-start.4
  106.5 6.0 %collective-permute-done.12 = bf16[32,512]{1,0:T(8,128)(2,1)S(1)} collective-permute-done((bf16[32,512]{1,0:T(8,128)(2,1)S(1)}, bf16[32,512]{1,0:T(8,128)(2,1)S(1)}, u32[]{:S(2)}, u32[]{:S(2)}) %collective-permute-start.12) | collective-permute-done | bytes 32800 | tf_op jit(solution)/shard_map/ppermute | solution.py:398
  112.5 4.2 %collective-permute-done.13 = bf16[64,512]{1,0:T(8,128)(2,1)S(1)} collective-permute-done((bf16[64,512]{1,0:T(8,128)(2,1)S(1)}, bf16[64,512]{1,0:T(8,128)(2,1)S(1)}, u32[]{:S(2)}, u32[]{:S(2)}) %collective-permute-start.13) | collective-permute-done | bytes 65568 | tf_op jit(solution)/shard_map/ppermute | solution.py:398
  116.8 1.5 %collective-permute-start.14 = (bf16[128,512]{1,0:T(8,128)(2,1)S(1)}, bf16[128,512]{1,0:T(8,128)(2,1)S(1)}, u32[]{:S(2)}, u32[]{:S(2)}) collective-permute-start(bf16[128,512]{1,0:T(8,128)(2,1)S(1)} %maximum_select_fusion.2), channel_id=1, source_target_pairs={{0,4},{2,6},{4,0},{6,2},{8,12},{10,14},{12,8},{14,10},{16,20},{18,... | collective-permute-start | bytes 393224 | tf_op jit(solution)/shard_map/ppermute | solution.py:398
  118.3 1.5 collective-permute-start.6
  120.4 5.7 %collective-permute-done.3.rest_2_ = bf16[256,768]{1,0:T(8,128)(2,1)S(1)} collective-permute-done((bf16[256,768]{1,0:T(8,128)(2,1)S(1)}, bf16[256,768]{1,0:T(8,128)(2,1)S(1)}, u32[]{:S(2)}, u32[]{:S(2)}) %collective-permute-start.3) | collective-permute-done | bytes 393248 | tf_op jit(solution)/shard_map/ppermute | solution.py:280
  126.9 7.4 %shard_map.98 = (bf16[256,3072]{1,0:T(8,128)(2,1)}, bf16[16,16,256]{2,1,0:T(8,128)(2,1)}) custom-call(s32[2,72]{1,0:T(2,128)} %bitcast.27, s32[1]{0:T(128)S(6)} %copy.14.count, bf16[16,2,16,256]{3,2,1,0:T(8,128)(2,1)} %bitcast.24, bf16[72,128,128]{2,1,0:T(8,128)(2,1)} %values_ref.3, bf16[256,768]{1,0:T(8,128)(2,1)} %get-tuple-element.41.rest_0_, ...), custom_call_target="tpu_custom_call" | custom-call | flops 603979776 | bytes 4194594 | tf_op jit(solution)/shard_map/pallas_call | solution.py:268
  134.4 3.6 %all-to-all-start.3 = ((bf16[16,16,256]{2,1,0:T(8,128)(2,1)}), bf16[16,16,256]{2,1,0:T(8,128)(2,1)S(1)}, u32[]{:S(2)}, u32[]{:S(2)}) async-start(bf16[16,16,256]{2,1,0:T(8,128)(2,1)} %get-tuple-element.45), calls=%async_computation.3 | async-start | bytes 262144 | tf_op jit(solution)/shard_map/all_to_all | solution.py:284
  138.5 3.8 %collective-permute-done.5.rest_2_ = bf16[256,768]{1,0:T(8,128)(2,1)S(1)} collective-permute-done((bf16[256,768]{1,0:T(8,128)(2,1)S(1)}, bf16[256,768]{1,0:T(8,128)(2,1)S(1)}, u32[]{:S(2)}, u32[]{:S(2)}) %collective-permute-start.5) | collective-permute-done | bytes 393248 | tf_op jit(solution)/shard_map/ppermute | solution.py:280
  142.3 3.5 %all-to-all-done.3.inc_ref = bf16[16,16,256]{2,1,0:T(8,128)(2,1)S(1)} async-done(((bf16[16,16,256]{2,1,0:T(8,128)(2,1)}), bf16[16,16,256]{2,1,0:T(8,128)(2,1)S(1)}, u32[]{:S(2)}, u32[]{:S(2)}) %all-to-all-start.3) | async-done | bytes 131104 | tf_op jit(solution)/shard_map/all_to_all | solution.py:284
  146.5 4.0 %shard_map.99 = bf16[256,3072]{1,0:T(8,128)(2,1)} custom-call(s32[1,256]{1,0:T(1,128)} %reshape.31.rep_ref.refs_0_, bf16[16,16,256]{2,1,0:T(8,128)(2,1)} %copy-done.5, bf16[256,3072]{1,0:T(8,128)(2,1)} %get-tuple-element.46.back_ref, bf16[256,768]{1,0:T(8,128)(2,1)} %get-tuple-element.47.rest_0_, bf16[256,768]{1,0:T(8,128)(2,1)} %get-tuple-element.48.rest_1_, ...), custom_call_target="tpu_custom_call" | custom-call | flops 402653184 | bytes 3277312 | tf_op jit(solution)/shard_map/pallas_call | solution.py:268
  (61 shorter events, 11.5 us)
Async XLA Ops:
  5.3 15.3 %all-to-all-start = ((bf16[16,16,256]{2,1,0:T(8,128)(2,1)}), bf16[16,16,256]{2,1,0:T(8,128)(2,1)S(1)}, u32[]{:S(2)}, u32[]{:S(2)}) async-start(bf16[16,16,256]{2,1,0:T(8,128)(2,1)} %get-tuple-element.30), calls=%async_computation | async-start | bytes 262144 | tf_op jit(solution)/shard_map/all_to_all | solution.py:284
  12.7 33.2 %collective-permute-start = (bf16[256,1536]{1,0:T(8,128)(2,1)}, bf16[256,1536]{1,0:T(8,128)(2,1)S(1)}, u32[]{:S(2)}, u32[]{:S(2)}) collective-permute-start(bf16[256,1536]{1,0:T(8,128)(2,1)} %get-tuple-element.33), channel_id=1, source_target_pairs={{0,1},{1,0},{2,3},{3,2},{4,5},{5,4},{6,7},{7,6},{8,9},{9,8},{10,11... | collective-permute-start | bytes 2359304 | tf_op jit(solution)/shard_map/ppermute | solution.py:280
  21.3 12.1 %copy-start = (bf16[2,512,512]{2,1,0:T(8,128)(2,1)S(1)}, bf16[2,512,512]{2,1,0:T(8,128)(2,1)}, u32[]{:S(2)}) copy-start(bf16[2,512,512]{2,1,0:T(8,128)(2,1)} %param.8) | copy-start | bytes 3145732
  28.7 17.2 %all-to-all-start.1 = ((bf16[32,16,256]{2,1,0:T(8,128)(2,1)}), bf16[32,16,256]{2,1,0:T(8,128)(2,1)S(1)}, u32[]{:S(2)}, u32[]{:S(2)}) async-start(bf16[32,16,256]{2,1,0:T(8,128)(2,1)} %bitcast.25), calls=%async_computation.1 | async-start | bytes 524288 | tf_op jit(solution)/shard_map/all_to_all | solution.py:284
  31.3 14.6 %collective-permute-start.2 = (bf16[256,768]{1,0:T(8,128)(2,1)}, bf16[256,768]{1,0:T(8,128)(2,1)S(1)}, u32[]{:S(2)}, u32[]{:S(2)}) collective-permute-start(bf16[256,768]{1,0:T(8,128)(2,1)} %get-tuple-element.36), channel_id=1, source_target_pairs={{0,1},{1,0},{2,3},{3,2},{4,5},{5,4},{6,7},{7,6},{8,9},{9,8},{10,11... | collective-permute-start | bytes 1179656 | tf_op jit(solution)/shard_map/ppermute | solution.py:280
  33.0 23.0 %collective-permute-start.1 = (bf16[256,768]{1,0:T(8,128)(2,1)}, bf16[256,768]{1,0:T(8,128)(2,1)S(1)}, u32[]{:S(2)}, u32[]{:S(2)}) collective-permute-start(bf16[256,768]{1,0:T(8,128)(2,1)} %get-tuple-element.35), channel_id=1, source_target_pairs={{0,1},{1,0},{2,3},{3,2},{4,5},{5,4},{6,7},{7,6},{8,9},{9,8},{10,11... | collective-permute-start | bytes 1179656 | tf_op jit(solution)/shard_map/ppermute | solution.py:280
  45.9 0.8 copy-start.9
  45.9 0.9 copy-start.2
  45.9 1.2 copy-start.1
  56.0 0.8 copy-start.6
  71.4 2.1 %collective-permute-start.7 = (bf16[2,256,512]{2,1,0:T(8,128)(2,1)}, bf16[2,256,512]{2,1,0:T(8,128)(2,1)S(1)}, u32[]{:S(2)}, u32[]{:S(2)}) collective-permute-start(bf16[2,256,512]{2,1,0:T(8,128)(2,1)} %get-tuple-element.56), channel_id=1, source_target_pairs={{0,2},{2,0},{4,6},{6,4},{8,10},{10,8},{12,14},{14,12},{16,18},{18,... | collective-permute-start | bytes 1572872 | tf_op jit(solution)/shard_map/ppermute | solution.py:398
  75.0 8.4 %collective-permute-start.8 = (bf16[2,128,512]{2,1,0:T(8,128)(2,1)S(1)}, bf16[2,128,512]{2,1,0:T(8,128)(2,1)S(1)}, u32[]{:S(2)}, u32[]{:S(2)}) collective-permute-start(bf16[2,128,512]{2,1,0:T(8,128)(2,1)S(1)} %dynamic-slice_convert_fusion), channel_id=1, source_target_pairs={{0,4},{2,6},{4,0},{6,2},{8,12},{10,14},{12,8},{14,10},{16,20},{18,... | collective-permute-start | bytes 786440 | tf_op jit(solution)/shard_map/ppermute | solution.py:398
  76.3 29.6 %copy-start.14 = (bf16[256,768]{1,0:T(8,128)(2,1)S(1)}, bf16[256,768]{1,0:T(8,128)(2,1)}, u32[]{:S(2)}) copy-start(bf16[256,768]{1,0:T(8,128)(2,1)} %get-tuple-element.43) | copy-start | bytes 1179652
  83.5 34.8 %copy-start.13 = (bf16[256,768]{1,0:T(8,128)(2,1)S(1)}, bf16[256,768]{1,0:T(8,128)(2,1)}, u32[]{:S(2)}) copy-start(bf16[256,768]{1,0:T(8,128)(2,1)} %get-tuple-element.50) | copy-start | bytes 1179652
  83.5 36.3 %copy-start.12 = (bf16[256,768]{1,0:T(8,128)(2,1)S(1)}, bf16[256,768]{1,0:T(8,128)(2,1)}, u32[]{:S(2)}) copy-start(bf16[256,768]{1,0:T(8,128)(2,1)} %get-tuple-element.49) | copy-start | bytes 1179652
  83.5 5.0 %collective-permute-start.9 = (bf16[2,64,512]{2,1,0:T(8,128)(2,1)S(1)}, bf16[2,64,512]{2,1,0:T(8,128)(2,1)S(1)}, u32[]{:S(2)}, u32[]{:S(2)}) collective-permute-start(bf16[2,64,512]{2,1,0:T(8,128)(2,1)S(1)} %dynamic-slice_convert_fusion.1), channel_id=1, source_target_pairs={{0,8},{2,10},{4,12},{6,14},{8,0},{10,2},{12,4},{14,6},{16,24},{18,... | collective-permute-start | bytes 393224 | tf_op jit(solution)/shard_map/ppermute | solution.py:398
  88.6 7.3 %collective-permute-start.10 = (f32[2,32,512]{2,1,0:T(8,128)S(1)}, f32[2,32,512]{2,1,0:T(8,128)S(1)}, u32[]{:S(2)}, u32[]{:S(2)}) collective-permute-start(f32[2,32,512]{2,1,0:T(8,128)S(1)} %constant_dynamic-slice_fusion), channel_id=1, source_target_pairs={{0,16},{2,18},{4,20},{6,22},{8,24},{10,26},{12,28},{14,30},{16,0},... | collective-permute-start | bytes 393224 | tf_op jit(solution)/shard_map/ppermute | solution.py:398
  96.0 5.6 %collective-permute-start.11 = (f32[32,512]{1,0:T(8,128)S(1)}, f32[32,512]{1,0:T(8,128)S(1)}, u32[]{:S(2)}, u32[]{:S(2)}) collective-permute-start(f32[32,512]{1,0:T(8,128)S(1)} %slice_bitcast_fusion), channel_id=1, source_target_pairs={{0,1},{1,0},{2,3},{3,2},{4,5},{5,4},{6,7},{7,6},{8,9},{9,8},{10,11... | collective-permute-start | bytes 196616 | tf_op jit(solution)/shard_map/ppermute | solution.py:280
  97.2 28.9 %all-to-all-start.2 = ((bf16[32,16,256]{2,1,0:T(8,128)(2,1)}), bf16[32,16,256]{2,1,0:T(8,128)(2,1)S(1)}, u32[]{:S(2)}, u32[]{:S(2)}) async-start(bf16[32,16,256]{2,1,0:T(8,128)(2,1)} %bitcast.5), calls=%async_computation.2 | async-start | bytes 524288 | tf_op jit(solution)/shard_map/all_to_all | solution.py:284
  101.7 10.7 %collective-permute-start.12 = (bf16[32,512]{1,0:T(8,128)(2,1)S(1)}, bf16[32,512]{1,0:T(8,128)(2,1)S(1)}, u32[]{:S(2)}, u32[]{:S(2)}) collective-permute-start(bf16[32,512]{1,0:T(8,128)(2,1)S(1)} %fusion.1), channel_id=1, source_target_pairs={{0,16},{2,18},{4,20},{6,22},{8,24},{10,26},{12,28},{14,30},{16,0},... | collective-permute-start | bytes 98312 | tf_op jit(solution)/shard_map/ppermute | solution.py:398
  104.4 15.9 %collective-permute-start.4 = (bf16[256,768]{1,0:T(8,128)(2,1)}, bf16[256,768]{1,0:T(8,128)(2,1)S(1)}, u32[]{:S(2)}, u32[]{:S(2)}) collective-permute-start(bf16[256,768]{1,0:T(8,128)(2,1)} %get-tuple-element.44), channel_id=1, source_target_pairs={{0,1},{1,0},{2,3},{3,2},{4,5},{5,4},{6,7},{7,6},{8,9},{9,8},{10,11... | collective-permute-start | bytes 1179656 | tf_op jit(solution)/shard_map/ppermute | solution.py:280
  105.9 20.2 %collective-permute-start.3 = (bf16[256,768]{1,0:T(8,128)(2,1)S(1)}, bf16[256,768]{1,0:T(8,128)(2,1)S(1)}, u32[]{:S(2)}, u32[]{:S(2)}) collective-permute-start(bf16[256,768]{1,0:T(8,128)(2,1)S(1)} %copy-done.14), channel_id=1, source_target_pairs={{0,1},{1,0},{2,3},{3,2},{4,5},{5,4},{6,7},{7,6},{8,9},{9,8},{10,11... | collective-permute-start | bytes 1179656 | tf_op jit(solution)/shard_map/ppermute | solution.py:280
  112.4 4.3 %collective-permute-start.13 = (bf16[64,512]{1,0:T(8,128)(2,1)S(1)}, bf16[64,512]{1,0:T(8,128)(2,1)S(1)}, u32[]{:S(2)}, u32[]{:S(2)}) collective-permute-start(bf16[64,512]{1,0:T(8,128)(2,1)S(1)} %maximum_select_fusion.3), channel_id=1, source_target_pairs={{0,8},{2,10},{4,12},{6,14},{8,0},{10,2},{12,4},{14,6},{16,24},{18,... | collective-permute-start | bytes 196616 | tf_op jit(solution)/shard_map/ppermute | solution.py:398
  116.8 21.2 %collective-permute-start.14 = (bf16[128,512]{1,0:T(8,128)(2,1)S(1)}, bf16[128,512]{1,0:T(8,128)(2,1)S(1)}, u32[]{:S(2)}, u32[]{:S(2)}) collective-permute-start(bf16[128,512]{1,0:T(8,128)(2,1)S(1)} %maximum_select_fusion.2), channel_id=1, source_target_pairs={{0,4},{2,6},{4,0},{6,2},{8,12},{10,14},{12,8},{14,10},{16,20},{18,... | collective-permute-start | bytes 393224 | tf_op jit(solution)/shard_map/ppermute | solution.py:398
  118.3 20.2 %collective-permute-start.6 = (bf16[256,768]{1,0:T(8,128)(2,1)S(1)}, bf16[256,768]{1,0:T(8,128)(2,1)S(1)}, u32[]{:S(2)}, u32[]{:S(2)}) collective-permute-start(bf16[256,768]{1,0:T(8,128)(2,1)S(1)} %copy-done.13), channel_id=1, source_target_pairs={{0,1},{1,0},{2,3},{3,2},{4,5},{5,4},{6,7},{7,6},{8,9},{9,8},{10,11... | collective-permute-start | bytes 1179656 | tf_op jit(solution)/shard_map/ppermute | solution.py:280
  119.8 22.5 %collective-permute-start.5 = (bf16[256,768]{1,0:T(8,128)(2,1)S(1)}, bf16[256,768]{1,0:T(8,128)(2,1)S(1)}, u32[]{:S(2)}, u32[]{:S(2)}) collective-permute-start(bf16[256,768]{1,0:T(8,128)(2,1)S(1)} %copy-done.12), channel_id=1, source_target_pairs={{0,1},{1,0},{2,3},{3,2},{4,5},{5,4},{6,7},{7,6},{8,9},{9,8},{10,11... | collective-permute-start | bytes 1179656 | tf_op jit(solution)/shard_map/ppermute | solution.py:280
  120.4 5.8 %copy-start.7 = (bf16[256,768]{1,0:T(8,128)(2,1)}, bf16[256,768]{1,0:T(8,128)(2,1)S(1)}, u32[]{:S(2)}) copy-start(bf16[256,768]{1,0:T(8,128)(2,1)S(1)} %collective-permute-done.4.rest_3_) | copy-start | bytes 1179652
  126.1 0.8 copy-start.3
  134.4 11.5 %all-to-all-start.3 = ((bf16[16,16,256]{2,1,0:T(8,128)(2,1)}), bf16[16,16,256]{2,1,0:T(8,128)(2,1)S(1)}, u32[]{:S(2)}, u32[]{:S(2)}) async-start(bf16[16,16,256]{2,1,0:T(8,128)(2,1)} %get-tuple-element.45), calls=%async_computation.3 | async-start | bytes 262144 | tf_op jit(solution)/shard_map/all_to_all | solution.py:284
  138.0 12.5 %collective-permute-start.15 = (bf16[256,512]{1,0:T(8,128)(2,1)S(1)}, bf16[256,512]{1,0:T(8,128)(2,1)S(1)}, u32[]{:S(2)}, u32[]{:S(2)}) collective-permute-start(bf16[256,512]{1,0:T(8,128)(2,1)S(1)} %maximum_select_fusion.1), channel_id=1, source_target_pairs={{0,2},{2,0},{4,6},{6,4},{8,10},{10,8},{12,14},{14,12},{16,18},{18,... | collective-permute-start | bytes 786440 | tf_op jit(solution)/shard_map/ppermute | solution.py:398
  138.5 7.4 %copy-start.10 = (bf16[256,768]{1,0:T(8,128)(2,1)}, bf16[256,768]{1,0:T(8,128)(2,1)S(1)}, u32[]{:S(2)}) copy-start(bf16[256,768]{1,0:T(8,128)(2,1)S(1)} %collective-permute-done.6.rest_3_) | copy-start | bytes 1179652
  142.3 3.5 %copy-start.11 = (bf16[256,768]{1,0:T(8,128)(2,1)}, bf16[256,768]{1,0:T(8,128)(2,1)S(1)}, u32[]{:S(2)}) copy-start(bf16[256,768]{1,0:T(8,128)(2,1)S(1)} %collective-permute-done.5.rest_2_) | copy-start | bytes 1179652
  (3 other events, 2.0 us)
where the time goes:
time: 152 us
  waiting for transfers between devices  57.6 us (38%)
  Pallas kernels  45.8 us (30%)
  starting transfers between devices  37.2 us (24%)
  local copies, waits for them, and re-layouts  6.75 us (4%)
  other arithmetic  2.92 us (2%)
  between operations  1.52 us (1%)
    pallas_call x7, Pallas kernels, call(): pl.pallas_call(body, grid=grid, in_specs=[full(a) if p is None else p for...  45.8 us
    ppermute x8, waiting for transfers between devices, swap(): return lax.ppermute(x, 'dom', [(i, i ^ b) for i in range(nd)])  27.6 us
    ppermute x8, waiting for transfers between devices, to_peer(): return lax.ppermute(x, 'feat', [(i, (i + j) % nf) for i in range(nf)])  20.8 us
    all_to_all x4, starting transfers between devices, exchange(): return lax.all_to_all(flat, axes, 0, 0, tiled=True).reshape(x.shape)  18 us
    ppermute x8, starting transfers between devices, swap(): return lax.ppermute(x, 'dom', [(i, i ^ b) for i in range(nd)])  10.3 us
    all_to_all x4, waiting for transfers between devices, exchange(): return lax.all_to_all(flat, axes, 0, 0, tiled=True).reshape(x.shape)  9.17 us
    ppermute x8, starting transfers between devices, to_peer(): return lax.ppermute(x, 'feat', [(i, (i + j) % nf) for i in range(nf)])  8.89 us
    unnamed x30, local copies, waits for them, and re-layouts  4.04 us
  transfers between devices with their start and end apart: 20, of which 11 were waited for; matrix products, arithmetic and copies ran while one was open for 1% of the time, Pallas kernels for 18%

commit v1 on v0

--- a/solution.py
+++ b/solution.py
@@ -140,9 +140,9 @@
     if c:
         pay_in = refs[0]
         refs = refs[2:]
-    rows, out_ref, g_ref, pay_ref = refs[:4]
+    agg_ref, out_ref, g_ref, pay_ref = refs[:4]
     grads, selfs = refs[4 : 4 + nf], refs[4 + nf : 4 + 2 * nf]
-    both, inc, pay = refs[4 + 2 * nf :]
+    rows, both, inc, pay = refs[4 + 2 * nf :]
     h = lax.axis_index("feat")
     i = pl.program_id(0)
     feats, step = grads[0].shape
@@ -163,8 +163,9 @@
         total = parts[j][...].astype(F32) + dot(inc[f], pick, 1, 1)
         rows[pl.ds(at, feats), :] = xs[j][...]
         rows[pl.ds(wide + at, feats), :] = total.astype(BF)
+    agg_ref[...] = rows[wide:, :]
     z = dot(wt_ref[...], rows[...])
-    s = jax.nn.sigmoid(z)
+    s = 0.5 + 0.5 * jnp.tanh(0.5 * z)
     out_ref[...] = (z * s).astype(BF)
     g = (cot_ref[...].astype(F32) * (s * (1.0 + z * (1.0 - s)))).astype(BF)
     g_ref[...] = g
@@ -186,19 +187,74 @@
 
 
 def weight_kernel(nf, nc, *refs):
-    keep_ref, send_ref, acc = refs[2 * nc :]
+    xs, aggs, grads = refs[:nf], refs[nf : nf + nc], refs[nf + nc : nf + 2 * nc]
+    keep_ref, send_ref, acc = refs[nf + 2 * nc :]
     h = lax.axis_index("feat")
     bit = lax.rem(lax.axis_index("dom"), 2)
     wide = acc.shape[1]
     feats = wide // nf
-    total = dot(refs[0][...], refs[nc][...], 1, 1)
-    for c in range(1, nc):
-        total = total + dot(refs[c][...], refs[nc + c][...], 1, 1)
-    acc[...] = total
+    part = grads[0].shape[1]
+
+    def summed(terms):
+        total = None
+        for left, right in terms:
+            term = dot(left, right, 1, 1)
+            total = term if total is None else total + term
+        return total
+
+    acc[wide:, :] = summed((aggs[c][...], grads[c][...]) for c in range(nc))
+    for j in range(nf):
+        at = pl.multiple_of(lax.rem(h - j + nf, nf) * feats, feats)
+        acc[pl.ds(at, feats), :] = summed(
+            (xs[j][:, c * part : (c + 1) * part], grads[c][...]) for c in range(nc)
+        )
     for j in range(nf):
         at = lax.rem(h + j, nf) * feats
         keep_ref[j] = acc[pl.ds(pl.multiple_of(bit * wide + at, feats), feats), :]
         send_ref[j] = acc[pl.ds(pl.multiple_of((1 - bit) * wide + at, feats), feats), :].astype(BF)
+
+
+def radices_of(n):
+    radices = [2] * min(2, n.bit_length() - 1)
+    n //= 1 << len(radices)
+    while n > 1:
+        radices.append(4 if n % 4 == 0 else 2)
+        n //= radices[-1]
+    return tuple(radices)
+
+
+def unit_of(radices, k):
+    unit = 1
+    for r in radices[:k]:
+        unit *= r
+    return unit
+
+
+def relative(radices, m):
+    number = 0
+    size = unit_of(radices, len(radices))
+    for k, r in enumerate(radices):
+        size //= r
+        number += (m // size) % r * unit_of(radices, k)
+    return number
+
+
+def assemble_kernel(radices, own_ref, other_ref, out_ref):
+    d = lax.axis_index("dom")
+    nd = 1
+    for r in radices:
+        nd *= r
+    rows = out_ref.shape[0] // nd
+    half = nd // 2
+    for m in range(nd):
+        at, owner, height = 0, d ^ relative(radices, m), out_ref.shape[0]
+        for r in radices:
+            height //= r
+            at = at + lax.rem(owner, r) * height
+            owner = owner // r
+        ref, k = (own_ref, m) if m < half else (other_ref, m - half)
+        piece = ref[k * rows : (k + 1) * rows, :]
+        out_ref[pl.ds(pl.multiple_of(at, rows), rows), :] = piece.astype(F32)
 
 
 def back_kernel(nf, nc, tile, blocks, count, mirrors, values_ref, *rest):
@@ -342,12 +398,12 @@
             args += [pay, output]
             specs += [None, ANY]
         outs = [
-            sd((2 * wide, part), BF),
+            sd((wide, part), BF),
             sd((wide, width), BF),
             sd((wide, part), BF),
             sd((nd, nf, per, feats) if last else (wide, slots), BF),
         ] + [chunk] * (2 * nf)
-        out_specs = [of_chunk(2 * wide), of_all(wide, c), of_chunk(wide), full(outs[3])]
+        out_specs = [of_chunk(wide), of_all(wide, c), of_chunk(wide), full(outs[3])]
         out_specs += [of_chunk(feats)] * (2 * nf)
         rows_c, output, g_c, pay, *res = call(
             functools.partial(dense_kernel, nf, nc, c),
@@ -356,6 +412,7 @@
             specs,
             outs,
             [
+                pltpu.VMEM((2 * wide, vb), BF),
                 pltpu.VMEM((2 * wide, vb), BF),
                 pltpu.VMEM((nf, feats, slots), BF),
                 pltpu.VMEM((wide, slots), F32),
@@ -375,8 +432,8 @@
     keep, send = call(
         functools.partial(weight_kernel, nf, nc),
         4 * wide * wide * width,
-        rows + grads,
-        [None] * (2 * nc),
+        x_parts + rows + grads,
+        [None] * (nf + 2 * nc),
         [sd((nf, feats, wide), F32), sd((nf, feats, wide), BF)],
         [pltpu.VMEM((2 * wide, wide), F32)],
     )
@@ -392,31 +449,54 @@
     )
     back_in = exchange(push, "dom")
 
-    bits = [1 << k for k in range(nd.bit_length() - 1)]
+    radices = radices_of(nd)
 
     def swap(x, b):
         return lax.ppermute(x, "dom", [(i, i ^ b) for i in range(nd)])
 
-    for b in bits:
-        cur = keep + swap(send, b).astype(F32)
-        if b == bits[-1]:
+    sends = [send]
+    for k, r in enumerate(radices):
+        unit = unit_of(radices, k)
+        cur = keep
+        for m in range(1, r):
+            cur = cur + swap(sends[m - 1], m * unit).astype(F32)
+        if k + 1 == len(radices):
             break
-        bit = lax.rem(d // (2 * b), 2)
-        size = cur.shape[1] // 2
-        wire = F32 if 4 * b >= nd else BF
-        keep = lax.dynamic_slice_in_dim(cur, bit * size, size, 1)
-        send = lax.dynamic_slice_in_dim(cur, (1 - bit) * size, size, 1).astype(wire)
+        size = cur.shape[1] // radices[k + 1]
+        digit = lax.rem(d // unit_of(radices, k + 1), radices[k + 1])
+        pieces = [
+            lax.dynamic_slice_in_dim(cur, (digit ^ m) * size, size, 1)
+            for m in range(radices[k + 1])
+        ]
+        keep, sends = pieces[0], [piece.astype(BF) for piece in pieces[1:]]
     total = cur[0]
     for j in range(1, nf):
         total = total + to_peer(cur[j], j)
     total = total.astype(BF)
-    for b in reversed(bits):
-        bit = lax.rem(d // b, 2)
-        other = swap(total, b)
-        total = jnp.where(
-            bit == 0, jnp.concatenate([total, other], 0), jnp.concatenate([other, total], 0)
+    for k in reversed(range(1, len(radices))):
+        unit = unit_of(radices, k)
+        others = [swap(total, m * unit) for m in range(1, radices[k])]
+        total = jnp.concatenate([total, *others], 0)
+    other = swap(total, 1)
+    if total.shape[0] * 2 // nd % 8 == 0:
+        (weight_grad,) = call(
+            functools.partial(assemble_kernel, radices),
+            0,
+            [total, other],
+            [None] * 2,
+            [sd((2 * feats, wide), F32)],
         )
-    weight_grad = total.reshape(2, feats, wide).astype(F32)
+    else:
+        total = jnp.concatenate([total, other], 0).reshape(nd, -1, wide)
+        owners = jnp.arange(nd)
+        place, rest = jnp.zeros_like(owners), owners
+        for r in radices:
+            place, rest = place * r + rest % r, rest // r
+        held = jnp.zeros_like(owners).at[place].set(owners) ^ d
+        numbers = jnp.array([relative(radices, m) for m in range(nd)])
+        index = jnp.zeros_like(owners).at[numbers].set(jnp.arange(nd))[held]
+        weight_grad = total[index].reshape(2 * feats, wide).astype(F32)
+    weight_grad = weight_grad.reshape(2, feats, wide)
 
     selfs = [self_own[c] for c in range(nc)]
     selfs += [self_recv[c][j] for j in range(nf - 1) for c in range(nc)]

time: 152 us -> 145 us (0.954)
  waiting for transfers between devices: 57.6 us -> 46.9 us
  Pallas kernels: 45.8 us -> 48.3 us
    ppermute x8 -> x10, waiting for transfers between devices: 27.6 us -> 14.2 us  [swap(): return lax.ppermute(x, 'dom', [(i, i ^ b) for i in range(nd)])]
    ppermute x8, waiting for transfers between devices: 20.8 us -> 26.3 us  [to_peer(): return lax.ppermute(x, 'feat', [(i, (i + j) % nf) for i in range(nf)])]
    all_to_all x4, waiting for transfers between devices: 9.17 us -> 6.38 us  [exchange(): return lax.all_to_all(flat, axes, 0, 0, tiled=True).reshape(x.shape)]
    pallas_call x7 -> x8, Pallas kernels: 45.8 us -> 48.3 us  [call(): pl.pallas_call(body, grid=grid, in_specs=[full(a) if p is None else p for...]
    ppermute x8 -> x10, starting transfers between devices: 10.3 us -> 11.8 us  [swap(): return lax.ppermute(x, 'dom', [(i, i ^ b) for i in range(nd)])]
    unnamed x30 -> x35, local copies, waits for them, and re-layouts: 4.04 us -> 4.62 us
  transfers between devices with their start and end apart: 20 -> 22, of which waited for: 11 -> 7; matrix products, arithmetic and copies ran while one was open for 1% -> 1% of each run, Pallas kernels for 18% -> 19%
where the time goes in v1:
time: 145 us; the launch traced here: 144 us
  Pallas kernels  48.3 us (33%)
  waiting for transfers between devices  46.9 us (32%)
  starting transfers between devices  38.4 us (26%)
  local copies, waits for them, and re-layouts  7.39 us (5%)
  between operations  1.56 us (1%)
  other arithmetic  1.51 us (1%)
    pallas_call x8, Pallas kernels, call(): pl.pallas_call(body, grid=grid, in_specs=[full(a) if p is None else p for...  48.3 us
    ppermute x8, waiting for transfers between devices, to_peer(): return lax.ppermute(x, 'feat', [(i, (i + j) % nf) for i in range(nf)])  26.3 us
    all_to_all x4, starting transfers between devices, exchange(): return lax.all_to_all(flat, axes, 0, 0, tiled=True).reshape(x.shape)  17.8 us
    ppermute x10, waiting for transfers between devices, swap(): return lax.ppermute(x, 'dom', [(i, i ^ b) for i in range(nd)])  14.2 us
    ppermute x10, starting transfers between devices, swap(): return lax.ppermute(x, 'dom', [(i, i ^ b) for i in range(nd)])  11.8 us
    ppermute x8, starting transfers between devices, to_peer(): return lax.ppermute(x, 'feat', [(i, (i + j) % nf) for i in range(nf)])  8.77 us
    all_to_all x4, waiting for transfers between devices, exchange(): return lax.all_to_all(flat, axes, 0, 0, tiled=True).reshape(x.shape)  6.38 us
    unnamed x35, local copies, waits for them, and re-layouts  4.62 us
  transfers between devices with their start and end apart: 22, of which 7 were waited for; matrix products, arithmetic and copies ran while one was open for 1% of the time, Pallas kernels for 19%

profile of v1, /device:TPU:0, one launch (start us, length us, event | category | flops | bytes accessed | tf_op | source)
XLA Modules:
  0.0 144.0 jit_solution(7847812515398495596)
XLA Ops:
  0.6 1.4 reshape.27.rep_ref.refs_0_
  2.0 3.4 %shard_map.94 = (bf16[16,16,256]{2,1,0:T(8,128)(2,1)}, bf16[256,1536]{1,0:T(8,128)(2,1)}, bf16[256,1536]{1,0:T(8,128)(2,1)}) custom-call(bf16[256,3072]{1,0:T(8,128)(2,1)} %x_ref.3, s32[1,256]{1,0:T(1,128)} %reshape.27.rep_ref.refs_0_), custom_call_target="tpu_custom_call" | custom-call | flops 402653184 | bytes 1573376 | tf_op jit(solution)/shard_map/pallas_call | solution.py:324
  5.4 7.4 %all-to-all-start = ((bf16[16,16,256]{2,1,0:T(8,128)(2,1)}), bf16[16,16,256]{2,1,0:T(8,128)(2,1)S(1)}, u32[]{:S(2)}, u32[]{:S(2)}) async-start(bf16[16,16,256]{2,1,0:T(8,128)(2,1)} %get-tuple-element.30), calls=%async_computation | async-start | bytes 262144 | tf_op jit(solution)/shard_map/all_to_all | solution.py:340
  12.8 1.6 %collective-permute-start = (bf16[256,1536]{1,0:T(8,128)(2,1)}, bf16[256,1536]{1,0:T(8,128)(2,1)S(1)}, u32[]{:S(2)}, u32[]{:S(2)}) collective-permute-start(bf16[256,1536]{1,0:T(8,128)(2,1)} %get-tuple-element.33), channel_id=1, source_target_pairs={{0,1},{1,0},{2,3},{3,2},{4,5},{5,4},{6,7},{7,6},{8,9},{9,8},{10,11... | collective-permute-start | bytes 2359304 | tf_op jit(solution)/shard_map/ppermute | solution.py:336
  15.0 5.7 %all-to-all-done.mirrors = bf16[16,16,256]{2,1,0:T(8,128)(2,1)S(1)} async-done(((bf16[16,16,256]{2,1,0:T(8,128)(2,1)}), bf16[16,16,256]{2,1,0:T(8,128)(2,1)S(1)}, u32[]{:S(2)}, u32[]{:S(2)}) %all-to-all-start) | async-done | bytes 131104 | tf_op jit(solution)/shard_map/all_to_all | solution.py:340
  21.3 7.4 %shard_map.95 = (bf16[256,1536]{1,0:T(8,128)(2,1)}, bf16[16,2,16,256]{3,2,1,0:T(8,128)(2,1)}, bf16[256,768]{1,0:T(8,128)(2,1)}, bf16[256,768]{1,0:T(8,128)(2,1)}) custom-call(s32[2,72]{1,0:T(2,128)} %bitcast.26, s32[1]{0:T(128)S(6)} %copy.18.count, bf16[16,16,256]{2,1,0:T(8,128)(2,1)} %copy-done.4, bf16[256,3072]{1,0:T(8,128)(2,1)} %x_ref.3, ...), custom_call_target="tpu_custom_call" | custom-call | flops 603979776 | bytes 4063522 | tf_op jit(solution)/shard_map/pallas_call | solution.py:324
  28.8 2.6 %all-to-all-start.1 = ((bf16[32,16,256]{2,1,0:T(8,128)(2,1)}), bf16[32,16,256]{2,1,0:T(8,128)(2,1)S(1)}, u32[]{:S(2)}, u32[]{:S(2)}) async-start(bf16[32,16,256]{2,1,0:T(8,128)(2,1)} %bitcast.25), calls=%async_computation.1 | async-start | bytes 524288 | tf_op jit(solution)/shard_map/all_to_all | solution.py:340
  31.4 1.7 %collective-permute-start.2 = (bf16[256,768]{1,0:T(8,128)(2,1)}, bf16[256,768]{1,0:T(8,128)(2,1)S(1)}, u32[]{:S(2)}, u32[]{:S(2)}) collective-permute-start(bf16[256,768]{1,0:T(8,128)(2,1)} %get-tuple-element.36), channel_id=1, source_target_pairs={{0,1},{1,0},{2,3},{3,2},{4,5},{5,4},{6,7},{7,6},{8,9},{9,8},{10,11... | collective-permute-start | bytes 1179656 | tf_op jit(solution)/shard_map/ppermute | solution.py:336
  33.5 1.3 copy.12.refs_1_
  34.8 11.2 %collective-permute-done.2.refs_8_ = bf16[256,768]{1,0:T(8,128)(2,1)S(1)} collective-permute-done((bf16[256,768]{1,0:T(8,128)(2,1)}, bf16[256,768]{1,0:T(8,128)(2,1)S(1)}, u32[]{:S(2)}, u32[]{:S(2)}) %collective-permute-start.2) | collective-permute-done | bytes 393248 | tf_op jit(solution)/shard_map/ppermute | solution.py:336
  47.1 9.0 %shard_map.96 = (bf16[512,768]{1,0:T(8,128)(2,1)}, bf16[512,1536]{1,0:T(8,128)(2,1)}, bf16[512,768]{1,0:T(8,128)(2,1)}, bf16[512,256]{1,0:T(8,128)(2,1)}, bf16[2...) custom-call(s32[1,256]{1,0:T(1,128)} %reshape.27.rep_ref.refs_0_, ...), custom_call_target="tpu_custom_call" | custom-call | flops 1610612736 | bytes 6685184 | tf_op jit(solution)/shard_map/pallas_call | solution.py:324
  56.9 9.3 %shard_map.97 = (bf16[512,768]{1,0:T(8,128)(2,1)}, bf16[512,1536]{1,0:T(8,128)(2,1)}, bf16[512,768]{1,0:T(8,128)(2,1)}, bf16[16,2,16,256]{3,2,1,0:T(8,128)(2,1)}...) custom-call(s32[1,256]{1,0:T(1,128)} %reshape.27.rep_ref.refs_0_, ...), custom_call_target="tpu_custom_call", output_to_operand_aliasing={{1}: (10, {})} | custom-call | flops 1610612736 | bytes 8520192 | tf_op jit(solution)/shard_map/pallas_call | solution.py:324
  66.2 5.5 %shard_map.100 = (f32[2,256,512]{2,1,0:T(8,128)}, bf16[2,256,512]{2,1,0:T(8,128)(2,1)}) custom-call(bf16[256,1536]{1,0:T(8,128)(2,1)} %get-tuple-element.32.refs_5_.refs_0_, bf16[256,1536]{1,0:T(8,128)(2,1)} %copy-done.1, bf16[512,768]{1,0:T(8,128)(2,1)} %get-tuple-element.51.refs_2_, bf16[512,768]{1,0:T(8,128)(2,1)} %get-tuple-element.52.refs_3_, ...), custom_call_target="tpu_custom_call" | custom-call | flops 1610612736 | bytes 4718592 | tf_op jit(solution)/shard_map/pallas_call | solution.py:324
  71.7 2.1 %collective-permute-done.7 = bf16[2,256,512]{2,1,0:T(8,128)(2,1)S(1)} collective-permute-done((bf16[2,256,512]{2,1,0:T(8,128)(2,1)}, bf16[2,256,512]{2,1,0:T(8,128)(2,1)S(1)}, u32[]{:S(2)}, u32[]{:S(2)}) %collective-permute-start.7) | collective-permute-done | bytes 524320 | tf_op jit(solution)/shard_map/ppermute | solution.py:455
  73.8 1.4 convert_add_fusion
  75.3 1.3 collective-permute-start.8
  76.6 7.1 %collective-permute-done.8 = bf16[2,128,512]{2,1,0:T(8,128)(2,1)S(1)} collective-permute-done((bf16[2,128,512]{2,1,0:T(8,128)(2,1)S(1)}, bf16[2,128,512]{2,1,0:T(8,128)(2,1)S(1)}, u32[]{:S(2)}, u32[]{:S(2)}) %collective-permute-start.8) | collective-permute-done | bytes 262176 | tf_op jit(solution)/shard_map/ppermute | solution.py:455
  83.8 2.6 %collective-permute-start.10 = (bf16[2,32,512]{2,1,0:T(8,128)(2,1)S(1)}, bf16[2,32,512]{2,1,0:T(8,128)(2,1)S(1)}, u32[]{:S(2)}, u32[]{:S(2)}) collective-permute-start(bf16[2,32,512]{2,1,0:T(8,128)(2,1)S(1)} %get-tuple-element.61), channel_id=1, source_target_pairs={{0,16},{2,18},{4,20},{6,22},{8,24},{10,26},{12,28},{14,30},{16,0},... | collective-permute-start | bytes 196616 | tf_op jit(solution)/shard_map/ppermute | solution.py:455
  86.3 1.5 %collective-permute-start.11 = (bf16[2,32,512]{2,1,0:T(8,128)(2,1)S(1)}, bf16[2,32,512]{2,1,0:T(8,128)(2,1)S(1)}, u32[]{:S(2)}, u32[]{:S(2)}) collective-permute-start(bf16[2,32,512]{2,1,0:T(8,128)(2,1)S(1)} %get-tuple-element.60), channel_id=1, source_target_pairs={{0,24},{2,26},{4,28},{6,30},{8,16},{10,18},{12,20},{14,22},{16,8},... | collective-permute-start | bytes 196616 | tf_op jit(solution)/shard_map/ppermute | solution.py:455
  88.7 4.3 %all-to-all-start.2 = ((bf16[32,16,256]{2,1,0:T(8,128)(2,1)}), bf16[32,16,256]{2,1,0:T(8,128)(2,1)S(1)}, u32[]{:S(2)}, u32[]{:S(2)}) async-start(bf16[32,16,256]{2,1,0:T(8,128)(2,1)} %bitcast.5), calls=%async_computation.2 | async-start | bytes 524288 | tf_op jit(solution)/shard_map/all_to_all | solution.py:340
  93.0 1.8 %collective-permute-start.3 = (bf16[256,768]{1,0:T(8,128)(2,1)}, bf16[256,768]{1,0:T(8,128)(2,1)S(1)}, u32[]{:S(2)}, u32[]{:S(2)}) collective-permute-start(bf16[256,768]{1,0:T(8,128)(2,1)} %get-tuple-element.43), channel_id=1, source_target_pairs={{0,1},{1,0},{2,3},{3,2},{4,5},{5,4},{6,7},{7,6},{8,9},{9,8},{10,11... | collective-permute-start | bytes 1179656 | tf_op jit(solution)/shard_map/ppermute | solution.py:336
  95.3 1.8 %collective-permute-start.6 = (bf16[256,768]{1,0:T(8,128)(2,1)S(1)}, bf16[256,768]{1,0:T(8,128)(2,1)S(1)}, u32[]{:S(2)}, u32[]{:S(2)}) collective-permute-start(bf16[256,768]{1,0:T(8,128)(2,1)S(1)} %copy-done.15), channel_id=1, source_target_pairs={{0,1},{1,0},{2,3},{3,2},{4,5},{5,4},{6,7},{7,6},{8,9},{9,8},{10,11... | collective-permute-start | bytes 1179656 | tf_op jit(solution)/shard_map/ppermute | solution.py:336
  97.3 15.1 %collective-permute-done.12 = f32[32,512]{1,0:T(8,128)S(1)} collective-permute-done((f32[32,512]{1,0:T(8,128)S(1)}, f32[32,512]{1,0:T(8,128)S(1)}, u32[]{:S(2)}, u32[]{:S(2)}) %collective-permute-start.12) | collective-permute-done | bytes 65568 | tf_op jit(solution)/shard_map/ppermute | solution.py:336
  112.4 2.0 %collective-permute-start.13 = (bf16[32,512]{1,0:T(8,128)(2,1)S(1)}, bf16[32,512]{1,0:T(8,128)(2,1)S(1)}, u32[]{:S(2)}, u32[]{:S(2)}) collective-permute-start(bf16[32,512]{1,0:T(8,128)(2,1)S(1)} %get-tuple-element.58), channel_id=1, source_target_pairs={{0,8},{2,10},{4,12},{6,14},{8,0},{10,2},{12,4},{14,6},{16,24},{18,... | collective-permute-start | bytes 98312 | tf_op jit(solution)/shard_map/ppermute | solution.py:455
  114.3 0.9 collective-permute-start.14
  115.3 1.5 %collective-permute-start.15 = (bf16[32,512]{1,0:T(8,128)(2,1)S(1)}, bf16[32,512]{1,0:T(8,128)(2,1)S(1)}, u32[]{:S(2)}, u32[]{:S(2)}) collective-permute-start(bf16[32,512]{1,0:T(8,128)(2,1)S(1)} %get-tuple-element.58), channel_id=1, source_target_pairs={{0,24},{2,26},{4,28},{6,30},{8,16},{10,18},{12,20},{14,22},{16,8},... | collective-permute-start | bytes 98312 | tf_op jit(solution)/shard_map/ppermute | solution.py:455
  117.5 7.4 %shard_map.98 = (bf16[256,3072]{1,0:T(8,128)(2,1)}, bf16[16,16,256]{2,1,0:T(8,128)(2,1)}) custom-call(s32[2,72]{1,0:T(2,128)} %bitcast.27, s32[1]{0:T(128)S(6)} %copy.18.count, bf16[16,2,16,256]{3,2,1,0:T(8,128)(2,1)} %bitcast.23, bf16[72,128,128]{2,1,0:T(8,128)(2,1)} %values_ref.3, bf16[256,768]{1,0:T(8,128)(2,1)} %get-tuple-element.41.rest_0_, ...), custom_call_target="tpu_custom_call" | custom-call | flops 603979776 | bytes 4194594 | tf_op jit(solution)/shard_map/pallas_call | solution.py:324
  125.0 3.5 %all-to-all-start.3 = ((bf16[16,16,256]{2,1,0:T(8,128)(2,1)}), bf16[16,16,256]{2,1,0:T(8,128)(2,1)S(1)}, u32[]{:S(2)}, u32[]{:S(2)}) async-start(bf16[16,16,256]{2,1,0:T(8,128)(2,1)} %get-tuple-element.45), calls=%async_computation.3 | async-start | bytes 262144 | tf_op jit(solution)/shard_map/all_to_all | solution.py:340
  128.6 2.0 %collective-permute-start.16 = (bf16[128,512]{1,0:T(8,128)(2,1)S(1)}, bf16[128,512]{1,0:T(8,128)(2,1)S(1)}, u32[]{:S(2)}, u32[]{:S(2)}) collective-permute-start(bf16[128,512]{1,0:T(8,128)(2,1)S(1)} %pad_maximum_fusion), channel_id=1, source_target_pairs={{0,4},{2,6},{4,0},{6,2},{8,12},{10,14},{12,8},{14,10},{16,20},{18,... | collective-permute-start | bytes 393224 | tf_op jit(solution)/shard_map/ppermute | solution.py:455
  130.5 5.0 %collective-permute-done.16 = bf16[128,512]{1,0:T(8,128)(2,1)S(1)} collective-permute-done((bf16[128,512]{1,0:T(8,128)(2,1)S(1)}, bf16[128,512]{1,0:T(8,128)(2,1)S(1)}, u32[]{:S(2)}, u32[]{:S(2)}) %collective-permute-start.16) | collective-permute-done | bytes 131104 | tf_op jit(solution)/shard_map/ppermute | solution.py:455
  137.0 4.0 %shard_map.99 = bf16[256,3072]{1,0:T(8,128)(2,1)} custom-call(s32[1,256]{1,0:T(1,128)} %reshape.27.rep_ref.refs_0_, bf16[16,16,256]{2,1,0:T(8,128)(2,1)} %copy-done.5, bf16[256,3072]{1,0:T(8,128)(2,1)} %get-tuple-element.46.back_ref, bf16[256,768]{1,0:T(8,128)(2,1)} %get-tuple-element.47.rest_0_, bf16[256,768]{1,0:T(8,128)(2,1)} %get-tuple-element.48.rest_1_, ...), custom_call_target="tpu_custom_call" | custom-call | flops 402653184 | bytes 3277312 | tf_op jit(solution)/shard_map/pallas_call | solution.py:324
  141.8 2.3 %shard_map.101 = f32[512,512]{1,0:T(8,128)} custom-call(bf16[256,512]{1,0:T(8,128)(2,1)} %copy-done.12, bf16[256,512]{1,0:T(8,128)(2,1)} %copy-done.13), custom_call_target="tpu_custom_call" | custom-call | bytes 524288 | tf_op jit(solution)/shard_map/pallas_call | solution.py:324
  (66 shorter events, 7.5 us)
Async XLA Ops:
  5.4 15.3 %all-to-all-start = ((bf16[16,16,256]{2,1,0:T(8,128)(2,1)}), bf16[16,16,256]{2,1,0:T(8,128)(2,1)S(1)}, u32[]{:S(2)}, u32[]{:S(2)}) async-start(bf16[16,16,256]{2,1,0:T(8,128)(2,1)} %get-tuple-element.30), calls=%async_computation | async-start | bytes 262144 | tf_op jit(solution)/shard_map/all_to_all | solution.py:340
  12.8 33.2 %collective-permute-start = (bf16[256,1536]{1,0:T(8,128)(2,1)}, bf16[256,1536]{1,0:T(8,128)(2,1)S(1)}, u32[]{:S(2)}, u32[]{:S(2)}) collective-permute-start(bf16[256,1536]{1,0:T(8,128)(2,1)} %get-tuple-element.33), channel_id=1, source_target_pairs={{0,1},{1,0},{2,3},{3,2},{4,5},{5,4},{6,7},{7,6},{8,9},{9,8},{10,11... | collective-permute-start | bytes 2359304 | tf_op jit(solution)/shard_map/ppermute | solution.py:336
  21.3 12.1 %copy-start = (bf16[2,512,512]{2,1,0:T(8,128)(2,1)S(1)}, bf16[2,512,512]{2,1,0:T(8,128)(2,1)}, u32[]{:S(2)}) copy-start(bf16[2,512,512]{2,1,0:T(8,128)(2,1)} %param.8) | copy-start | bytes 3145732
  28.8 17.2 %all-to-all-start.1 = ((bf16[32,16,256]{2,1,0:T(8,128)(2,1)}), bf16[32,16,256]{2,1,0:T(8,128)(2,1)S(1)}, u32[]{:S(2)}, u32[]{:S(2)}) async-start(bf16[32,16,256]{2,1,0:T(8,128)(2,1)} %bitcast.25), calls=%async_computation.1 | async-start | bytes 524288 | tf_op jit(solution)/shard_map/all_to_all | solution.py:340
  31.4 14.6 %collective-permute-start.2 = (bf16[256,768]{1,0:T(8,128)(2,1)}, bf16[256,768]{1,0:T(8,128)(2,1)S(1)}, u32[]{:S(2)}, u32[]{:S(2)}) collective-permute-start(bf16[256,768]{1,0:T(8,128)(2,1)} %get-tuple-element.36), channel_id=1, source_target_pairs={{0,1},{1,0},{2,3},{3,2},{4,5},{5,4},{6,7},{7,6},{8,9},{9,8},{10,11... | collective-permute-start | bytes 1179656 | tf_op jit(solution)/shard_map/ppermute | solution.py:336
  33.1 23.0 %collective-permute-start.1 = (bf16[256,768]{1,0:T(8,128)(2,1)}, bf16[256,768]{1,0:T(8,128)(2,1)S(1)}, u32[]{:S(2)}, u32[]{:S(2)}) collective-permute-start(bf16[256,768]{1,0:T(8,128)(2,1)} %get-tuple-element.35), channel_id=1, source_target_pairs={{0,1},{1,0},{2,3},{3,2},{4,5},{5,4},{6,7},{7,6},{8,9},{9,8},{10,11... | collective-permute-start | bytes 1179656 | tf_op jit(solution)/shard_map/ppermute | solution.py:336
  46.0 0.9 copy-start.2
  46.0 1.1 copy-start.1
  71.7 2.1 %collective-permute-start.7 = (bf16[2,256,512]{2,1,0:T(8,128)(2,1)}, bf16[2,256,512]{2,1,0:T(8,128)(2,1)S(1)}, u32[]{:S(2)}, u32[]{:S(2)}) collective-permute-start(bf16[2,256,512]{2,1,0:T(8,128)(2,1)} %get-tuple-element.56), channel_id=1, source_target_pairs={{0,2},{2,0},{4,6},{6,4},{8,10},{10,8},{12,14},{14,12},{16,18},{18,... | collective-permute-start | bytes 1572872 | tf_op jit(solution)/shard_map/ppermute | solution.py:455
  75.2 20.0 %copy-start.15 = (bf16[256,768]{1,0:T(8,128)(2,1)S(1)}, bf16[256,768]{1,0:T(8,128)(2,1)}, u32[]{:S(2)}) copy-start(bf16[256,768]{1,0:T(8,128)(2,1)} %get-tuple-element.50) | copy-start | bytes 1179652
  75.2 21.8 %copy-start.14 = (bf16[256,768]{1,0:T(8,128)(2,1)S(1)}, bf16[256,768]{1,0:T(8,128)(2,1)}, u32[]{:S(2)}) copy-start(bf16[256,768]{1,0:T(8,128)(2,1)} %get-tuple-element.49) | copy-start | bytes 1179652
  75.3 8.4 %collective-permute-start.8 = (bf16[2,128,512]{2,1,0:T(8,128)(2,1)S(1)}, bf16[2,128,512]{2,1,0:T(8,128)(2,1)S(1)}, u32[]{:S(2)}, u32[]{:S(2)}) collective-permute-start(bf16[2,128,512]{2,1,0:T(8,128)(2,1)S(1)} %dynamic-slice_convert_fusion), channel_id=1, source_target_pairs={{0,4},{2,6},{4,0},{6,2},{8,12},{10,14},{12,8},{14,10},{16,20},{18,... | collective-permute-start | bytes 786440 | tf_op jit(solution)/shard_map/ppermute | solution.py:455
  83.8 11.1 %collective-permute-start.10 = (bf16[2,32,512]{2,1,0:T(8,128)(2,1)S(1)}, bf16[2,32,512]{2,1,0:T(8,128)(2,1)S(1)}, u32[]{:S(2)}, u32[]{:S(2)}) collective-permute-start(bf16[2,32,512]{2,1,0:T(8,128)(2,1)S(1)} %get-tuple-element.61), channel_id=1, source_target_pairs={{0,16},{2,18},{4,20},{6,22},{8,24},{10,26},{12,28},{14,30},{16,0},... | collective-permute-start | bytes 196616 | tf_op jit(solution)/shard_map/ppermute | solution.py:455
  86.3 8.5 %collective-permute-start.11 = (bf16[2,32,512]{2,1,0:T(8,128)(2,1)S(1)}, bf16[2,32,512]{2,1,0:T(8,128)(2,1)S(1)}, u32[]{:S(2)}, u32[]{:S(2)}) collective-permute-start(bf16[2,32,512]{2,1,0:T(8,128)(2,1)S(1)} %get-tuple-element.60), channel_id=1, source_target_pairs={{0,24},{2,26},{4,28},{6,30},{8,16},{10,18},{12,20},{14,22},{16,8},... | collective-permute-start | bytes 196616 | tf_op jit(solution)/shard_map/ppermute | solution.py:455
  87.8 7.0 %collective-permute-start.9 = (bf16[2,32,512]{2,1,0:T(8,128)(2,1)S(1)}, bf16[2,32,512]{2,1,0:T(8,128)(2,1)S(1)}, u32[]{:S(2)}, u32[]{:S(2)}) collective-permute-start(bf16[2,32,512]{2,1,0:T(8,128)(2,1)S(1)} %get-tuple-element.59), channel_id=1, source_target_pairs={{0,8},{2,10},{4,12},{6,14},{8,0},{10,2},{12,4},{14,6},{16,24},{18,... | collective-permute-start | bytes 196616 | tf_op jit(solution)/shard_map/ppermute | solution.py:455
  87.8 26.5 %collective-permute-start.4 = (bf16[256,768]{1,0:T(8,128)(2,1)}, bf16[256,768]{1,0:T(8,128)(2,1)S(1)}, u32[]{:S(2)}, u32[]{:S(2)}) collective-permute-start(bf16[256,768]{1,0:T(8,128)(2,1)} %get-tuple-element.44), channel_id=1, source_target_pairs={{0,1},{1,0},{2,3},{3,2},{4,5},{5,4},{6,7},{7,6},{8,9},{9,8},{10,11... | collective-permute-start | bytes 1179656 | tf_op jit(solution)/shard_map/ppermute | solution.py:336
  88.7 28.1 %all-to-all-start.2 = ((bf16[32,16,256]{2,1,0:T(8,128)(2,1)}), bf16[32,16,256]{2,1,0:T(8,128)(2,1)S(1)}, u32[]{:S(2)}, u32[]{:S(2)}) async-start(bf16[32,16,256]{2,1,0:T(8,128)(2,1)} %bitcast.5), calls=%async_computation.2 | async-start | bytes 524288 | tf_op jit(solution)/shard_map/all_to_all | solution.py:340
  93.0 22.3 %collective-permute-start.3 = (bf16[256,768]{1,0:T(8,128)(2,1)}, bf16[256,768]{1,0:T(8,128)(2,1)S(1)}, u32[]{:S(2)}, u32[]{:S(2)}) collective-permute-start(bf16[256,768]{1,0:T(8,128)(2,1)} %get-tuple-element.43), channel_id=1, source_target_pairs={{0,1},{1,0},{2,3},{3,2},{4,5},{5,4},{6,7},{7,6},{8,9},{9,8},{10,11... | collective-permute-start | bytes 1179656 | tf_op jit(solution)/shard_map/ppermute | solution.py:336
  94.9 17.4 %collective-permute-start.12 = (f32[32,512]{1,0:T(8,128)S(1)}, f32[32,512]{1,0:T(8,128)S(1)}, u32[]{:S(2)}, u32[]{:S(2)}) collective-permute-start(f32[32,512]{1,0:T(8,128)S(1)} %slice_bitcast_fusion), channel_id=1, source_target_pairs={{0,1},{1,0},{2,3},{3,2},{4,5},{5,4},{6,7},{7,6},{8,9},{9,8},{10,11... | collective-permute-start | bytes 196616 | tf_op jit(solution)/shard_map/ppermute | solution.py:336
  95.3 40.4 %collective-permute-start.6 = (bf16[256,768]{1,0:T(8,128)(2,1)S(1)}, bf16[256,768]{1,0:T(8,128)(2,1)S(1)}, u32[]{:S(2)}, u32[]{:S(2)}) collective-permute-start(bf16[256,768]{1,0:T(8,128)(2,1)S(1)} %copy-done.15), channel_id=1, source_target_pairs={{0,1},{1,0},{2,3},{3,2},{4,5},{5,4},{6,7},{7,6},{8,9},{9,8},{10,11... | collective-permute-start | bytes 1179656 | tf_op jit(solution)/shard_map/ppermute | solution.py:336
  97.0 38.6 %collective-permute-start.5 = (bf16[256,768]{1,0:T(8,128)(2,1)S(1)}, bf16[256,768]{1,0:T(8,128)(2,1)S(1)}, u32[]{:S(2)}, u32[]{:S(2)}) collective-permute-start(bf16[256,768]{1,0:T(8,128)(2,1)S(1)} %copy-done.14), channel_id=1, source_target_pairs={{0,1},{1,0},{2,3},{3,2},{4,5},{5,4},{6,7},{7,6},{8,9},{9,8},{10,11... | collective-permute-start | bytes 1179656 | tf_op jit(solution)/shard_map/ppermute | solution.py:336
  112.4 16.2 %collective-permute-start.13 = (bf16[32,512]{1,0:T(8,128)(2,1)S(1)}, bf16[32,512]{1,0:T(8,128)(2,1)S(1)}, u32[]{:S(2)}, u32[]{:S(2)}) collective-permute-start(bf16[32,512]{1,0:T(8,128)(2,1)S(1)} %get-tuple-element.58), channel_id=1, source_target_pairs={{0,8},{2,10},{4,12},{6,14},{8,0},{10,2},{12,4},{14,6},{16,24},{18,... | collective-permute-start | bytes 98312 | tf_op jit(solution)/shard_map/ppermute | solution.py:455
  114.3 2.5 %copy-start.7 = (bf16[256,768]{1,0:T(8,128)(2,1)}, bf16[256,768]{1,0:T(8,128)(2,1)S(1)}, u32[]{:S(2)}) copy-start(bf16[256,768]{1,0:T(8,128)(2,1)S(1)} %collective-permute-done.4.rest_3_) | copy-start | bytes 1179652
  114.3 14.2 %collective-permute-start.14 = (bf16[32,512]{1,0:T(8,128)(2,1)S(1)}, bf16[32,512]{1,0:T(8,128)(2,1)S(1)}, u32[]{:S(2)}, u32[]{:S(2)}) collective-permute-start(bf16[32,512]{1,0:T(8,128)(2,1)S(1)} %get-tuple-element.58), channel_id=1, source_target_pairs={{0,16},{2,18},{4,20},{6,22},{8,24},{10,26},{12,28},{14,30},{16,0},... | collective-permute-start | bytes 98312 | tf_op jit(solution)/shard_map/ppermute | solution.py:455
  115.3 1.5 %copy-start.8 = (bf16[256,768]{1,0:T(8,128)(2,1)}, bf16[256,768]{1,0:T(8,128)(2,1)S(1)}, u32[]{:S(2)}) copy-start(bf16[256,768]{1,0:T(8,128)(2,1)S(1)} %collective-permute-done.3.rest_2_) | copy-start | bytes 1179652
  115.3 13.2 %collective-permute-start.15 = (bf16[32,512]{1,0:T(8,128)(2,1)S(1)}, bf16[32,512]{1,0:T(8,128)(2,1)S(1)}, u32[]{:S(2)}, u32[]{:S(2)}) collective-permute-start(bf16[32,512]{1,0:T(8,128)(2,1)S(1)} %get-tuple-element.58), channel_id=1, source_target_pairs={{0,24},{2,26},{4,28},{6,30},{8,16},{10,18},{12,20},{14,22},{16,8},... | collective-permute-start | bytes 98312 | tf_op jit(solution)/shard_map/ppermute | solution.py:455
  125.0 11.4 %all-to-all-start.3 = ((bf16[16,16,256]{2,1,0:T(8,128)(2,1)}), bf16[16,16,256]{2,1,0:T(8,128)(2,1)S(1)}, u32[]{:S(2)}, u32[]{:S(2)}) async-start(bf16[16,16,256]{2,1,0:T(8,128)(2,1)} %get-tuple-element.45), calls=%async_computation.3 | async-start | bytes 262144 | tf_op jit(solution)/shard_map/all_to_all | solution.py:340
  128.6 7.0 %collective-permute-start.16 = (bf16[128,512]{1,0:T(8,128)(2,1)S(1)}, bf16[128,512]{1,0:T(8,128)(2,1)S(1)}, u32[]{:S(2)}, u32[]{:S(2)}) collective-permute-start(bf16[128,512]{1,0:T(8,128)(2,1)S(1)} %pad_maximum_fusion), channel_id=1, source_target_pairs={{0,4},{2,6},{4,0},{6,2},{8,12},{10,14},{12,8},{14,10},{16,20},{18,... | collective-permute-start | bytes 393224 | tf_op jit(solution)/shard_map/ppermute | solution.py:455
  135.5 5.5 %copy-start.12 = (bf16[256,512]{1,0:T(8,128)(2,1)}, bf16[256,512]{1,0:T(8,128)(2,1)S(1)}, u32[]{:S(2)}) copy-start(bf16[256,512]{1,0:T(8,128)(2,1)S(1)} %constant_dynamic-update-slice_fusion.own_ref) | copy-start | bytes 786436
  135.5 5.5 %collective-permute-start.17 = (bf16[256,512]{1,0:T(8,128)(2,1)S(1)}, bf16[256,512]{1,0:T(8,128)(2,1)S(1)}, u32[]{:S(2)}, u32[]{:S(2)}) collective-permute-start(bf16[256,512]{1,0:T(8,128)(2,1)S(1)} %constant_dynamic-update-slice_fusion.own_ref), channel_id=1, source_target_pairs={{0,2},{2,0},{4,6},{6,4},{8,10},{10,8},{12,14},{14,12},{16,18},{18,... | collective-permute-start | bytes 786440 | tf_op jit(solution)/shard_map/ppermute | solution.py:455
  135.6 0.8 copy-start.10
  135.7 0.9 copy-start.11
  (6 other events, 4.2 us)

commit v2 on v1

--- a/solution.py
+++ b/solution.py
@@ -48,20 +48,22 @@
     return next(b for b in (512, 256, 128) if n % b == 0)
 
 
-def list_tiles(blocks, count, lists, source_col, trash):
+def list_tiles(blocks, count, lists, source_col, trash, low, high):
     tiles, sources, targets = lists
 
-    def step(t, _):
-        tiles[t] = t
-        sources[t] = blocks[source_col, t]
-        targets[t] = blocks[1 - source_col, t]
-        return 0
-
-    lax.fori_loop(0, count, step, 0)
+    def step(t, n):
+        source = blocks[source_col, t]
+        tiles[n] = t
+        sources[n] = source - low
+        targets[n] = blocks[1 - source_col, t]
+        return n + jnp.logical_and(source >= low, source < high).astype(jnp.int32)
+
+    n = lax.fori_loop(0, count, step, jnp.int32(0))
     for u in range(GROUP):
-        tiles[count + u] = 0
-        sources[count + u] = 0
-        targets[count + u] = trash
+        tiles[n + u] = 0
+        sources[n + u] = 0
+        targets[n + u] = trash
+    return n
 
 
 def run_tiles(n, lists, values, tile_dim, x_all, acc, tile):
@@ -84,7 +86,10 @@
     return ref[:, pl.ds(at, tile)]
 
 
-def prep_kernel(nf, x_ref, rep_ref, pull_ref, *halves):
+def prep_kernel(nf, x_ref, replica, pull_ref, rep_ref, *halves):
+    rep_ref[...] = jnp.concatenate(
+        [replica[0, p : p + 1, :] for p in range(replica.shape[1])], axis=1
+    )
     h = lax.axis_index("feat")
     _, masters = x_ref.shape
     width = halves[0].shape[1]
@@ -99,91 +104,140 @@
         halves[j][...] = x_ref[:, pl.ds(at, width)]
 
 
-def spread_kernel(nf, nc, tile, blocks, count, mirrors, x_ref, values_ref, *rest):
-    own_ref, push_ref = rest[:2]
-    rest = rest[2:]
-    sends = rest[: (nf - 1) * nc]
-    acc, x_all, values, tiles, sources, targets, sems = rest[(nf - 1) * nc :]
-    lists = (tiles, sources, targets)
-    h = lax.axis_index("feat")
-    feats, masters = x_ref.shape
-    width = own_ref.shape[1]
-    slots = x_all.shape[1] - masters
+def spread_own(tile, blocks, count, x_ref, values_ref, out_ref, acc, x, values, *rest):
+    lists, sems = rest[:3], rest[3]
+    masters = x.shape[1]
     copies = [
-        pltpu.make_async_copy(x_ref, x_all.at[:, :masters], sems.at[0]),
+        pltpu.make_async_copy(x_ref, x, sems.at[0]),
         pltpu.make_async_copy(values_ref, values, sems.at[1]),
     ]
     for copy in copies:
         copy.start()
     acc[...] = jnp.zeros_like(acc)
-    x_all[:, masters:] = flip(mirrors[...].reshape(slots, feats))
-    list_tiles(blocks, count[0], lists, 0, acc.shape[1] // tile - 1)
+    n = list_tiles(blocks, count[0], lists, 0, acc.shape[1] // tile - 1, 0, masters // tile)
     for copy in copies:
         copy.wait()
-    run_tiles(count[0], lists, values, 0, x_all, acc, tile)
+    run_tiles(n, lists, values, 0, x, acc, tile)
+    out_ref[...] = acc[:, : out_ref.shape[1]].astype(BF)
+
+
+def spread_mirrors(nf, nc, tile, blocks, count, mirrors, values_ref, own_ref, *rest):
+    part_ref, push_ref = rest[:2]
+    sends = rest[2 : 2 + (nf - 1) * nc]
+    acc, own, x, values, *lists, sems = rest[2 + (nf - 1) * nc :]
+    h = lax.axis_index("feat")
+    feats, width = part_ref.shape
+    slots = x.shape[1]
+    masters = own.shape[1] - slots
+    copies = [
+        pltpu.make_async_copy(values_ref, values, sems.at[0]),
+        pltpu.make_async_copy(own_ref, own, sems.at[1]),
+    ]
+    for copy in copies:
+        copy.start()
+    acc[...] = jnp.zeros_like(acc)
+    x[...] = flip(mirrors[...].reshape(slots, feats))
+    low = masters // tile
+    n = list_tiles(
+        blocks, count[0], lists, 0, acc.shape[1] // tile - 1, low, own.shape[1] // tile
+    )
+    for copy in copies:
+        copy.wait()
+    run_tiles(n, lists, values, 0, x, acc, tile)
+
+    def total(at, size):
+        return (own[:, pl.ds(at, size)].astype(F32) + acc[:, pl.ds(at, size)]).astype(BF)
+
     part = width // nc
     for j in range(1, nf):
         for c in range(nc):
             at = pl.multiple_of(lax.rem(h + j, nf) * width + c * part, 128)
-            sends[(j - 1) * nc + c][...] = acc[:, pl.ds(at, part)].astype(BF)
-    push = flip(acc[:, masters : masters + slots].astype(BF))
+            sends[(j - 1) * nc + c][...] = total(at, part)
+    push = flip(total(masters, slots))
     push = push.reshape(push_ref.shape[0], push_ref.shape[2], feats)
     for f in range(nf):
         push_ref[:, f] = push
-    own_ref[...] = acc[:, pl.ds(pl.multiple_of(h * width, 128), width)].astype(BF)
+    part_ref[...] = total(pl.multiple_of(h * width, 128), width)
 
 
 def dense_kernel(nf, nc, c, *refs):
-    rep_ref, wt_ref, w_ref, inc_ref, cot_ref = refs[:5]
+    rep_ref, inc_ref, wt_hbm, w_hbm, cot_hbm = refs[:5]
     xs, parts = refs[5 : 5 + nf], refs[5 + nf : 5 + 2 * nf]
     refs = refs[5 + 2 * nf :]
     if c:
         pay_in = refs[0]
         refs = refs[2:]
-    agg_ref, out_ref, g_ref, pay_ref = refs[:4]
+    agg_hbm, out_hbm, g_hbm, pay_ref = refs[:4]
     grads, selfs = refs[4 : 4 + nf], refs[4 + nf : 4 + 2 * nf]
-    rows, both, inc, pay = refs[4 + 2 * nf :]
+    wt, w, cot, rows, terms, out, g_all, both, in_sems, out_sems = refs[4 + 2 * nf :]
     h = lax.axis_index("feat")
-    i = pl.program_id(0)
-    feats, step = grads[0].shape
-    wide = g_ref.shape[0]
+    feats, part = grads[0].shape
+    wide = w.shape[1]
     slots = rep_ref.shape[1]
-    part = step * pl.num_programs(0)
-
-    @pl.when(i == 0)
-    def _():
+    chunk = pl.ds(c * part, part)
+
+    def place(f):
+        return pl.ds(pl.multiple_of(f * feats, feats), feats)
+
+    early, late = [], []
+    for j in range(nf):
+        f = lax.rem(h - j + nf, nf)
+        term = parts[j].at[:, chunk] if j == 0 else parts[j]
+        early.append(pltpu.make_async_copy(term, terms.at[j], in_sems.at[j]))
+        x = xs[j].at[:, chunk]
+        early.append(pltpu.make_async_copy(x, rows.at[place(f)], in_sems.at[nf + j]))
+    late.append(pltpu.make_async_copy(wt_hbm, wt, in_sems.at[2 * nf]))
+    late.append(pltpu.make_async_copy(cot_hbm.at[:, chunk], cot, in_sems.at[2 * nf + 1]))
+    late.append(pltpu.make_async_copy(w_hbm, w, in_sems.at[2 * nf + 2]))
+    for copy in early + late:
+        copy.start()
+    pick = picks(rep_ref[...], (h * nc + c) * part, part)
+    incs = [flip(inc_ref[:, lax.rem(h - j + nf, nf)].reshape(slots, feats)) for j in range(nf)]
+    adds = [dot(inc, pick, 1, 1) for inc in incs]
+    for copy in early:
+        copy.wait()
+    for j in range(nf):
+        f = lax.rem(h - j + nf, nf)
+        total = terms[j].astype(F32) + adds[j]
+        rows[pl.ds(pl.multiple_of(wide + f * feats, feats), feats), :] = total.astype(BF)
+    out_copies = []
+
+    def put(src, dst):
+        copy = pltpu.make_async_copy(src, dst, out_sems.at[len(out_copies)])
+        copy.start()
+        out_copies.append(copy)
+
+    put(rows.at[wide:], agg_hbm)
+    for copy in late:
+        copy.wait()
+    step = 256 if part % 256 == 0 else 128
+    for b in range(0, part, step):
+        cols = slice(b, b + step)
+        z = dot(wt[...], rows[:, cols])
+        s = 0.5 + 0.5 * jnp.tanh(0.5 * z)
+        out[:, cols] = (z * s).astype(BF)
+        g = (cot[:, cols].astype(F32) * (s * (1.0 + z * (1.0 - s)))).astype(BF)
+        g_all[:, cols] = g
+        both[:, cols] = dot(w[...], g).astype(BF)
+        for j in range(nf):
+            at = lax.rem(h + j, nf)
+            peer = pl.ds(pl.multiple_of(wide + at * feats, feats), feats)
+            put(both.at[peer, cols], grads[j].at[:, cols])
+            put(both.at[place(at), cols], selfs[j].at[:, cols])
+        put(g_all.at[:, cols], g_hbm.at[:, cols])
+        put(out.at[:, cols], out_hbm.at[:, pl.ds(c * part + b, step)])
+    pay = dot(both[wide:, :], pick)
+    if c:
+        pay = pay + pay_in[...].astype(F32)
+    pay = pay.astype(BF)
+    if c + 1 < nc:
+        pay_ref[...] = pay
+    else:
         for f in range(nf):
-            inc[f] = flip(inc_ref[:, f].reshape(slots, feats))
-        pay[...] = pay_in[...].astype(F32) if c else jnp.zeros_like(pay)
-
-    pick = picks(rep_ref[...], (h * nc + c) * part + i * step, step)
-    for j in range(nf):
-        f = lax.rem(h - j + nf, nf)
-        at = pl.multiple_of(f * feats, feats)
-        total = parts[j][...].astype(F32) + dot(inc[f], pick, 1, 1)
-        rows[pl.ds(at, feats), :] = xs[j][...]
-        rows[pl.ds(wide + at, feats), :] = total.astype(BF)
-    agg_ref[...] = rows[wide:, :]
-    z = dot(wt_ref[...], rows[...])
-    s = 0.5 + 0.5 * jnp.tanh(0.5 * z)
-    out_ref[...] = (z * s).astype(BF)
-    g = (cot_ref[...].astype(F32) * (s * (1.0 + z * (1.0 - s)))).astype(BF)
-    g_ref[...] = g
-    both[...] = dot(w_ref[...], g).astype(BF)
-    for j in range(nf):
-        at = pl.multiple_of(lax.rem(h + j, nf) * feats, feats)
-        grads[j][...] = both[pl.ds(wide + at, feats), :]
-        selfs[j][...] = both[pl.ds(at, feats), :]
-    pay[...] += dot(both[wide:, :], pick)
-
-    @pl.when(i == pl.num_programs(0) - 1)
-    def _():
-        if c + 1 < nc:
-            pay_ref[...] = pay[...].astype(BF)
-        else:
-            for f in range(nf):
-                mine = flip(pay[f * feats : (f + 1) * feats].astype(BF))
-                pay_ref[:, f] = mine.reshape(pay_ref.shape[0], pay_ref.shape[2], feats)
+            mine = flip(pay[f * feats : (f + 1) * feats])
+            pay_ref[:, f] = mine.reshape(pay_ref.shape[0], pay_ref.shape[2], feats)
+    for copy in out_copies:
+        copy.wait()
 
 
 def weight_kernel(nf, nc, *refs):
@@ -280,7 +334,7 @@
     for f in range(1, nf):
         total = total + mirrors[:, f].astype(F32)
     x_all[:, masters:] = flip(total.astype(BF).reshape(slots, feats))
-    list_tiles(blocks, count[0], lists, 1, acc.shape[1] // tile - 1)
+    list_tiles(blocks, count[0], lists, 1, acc.shape[1] // tile - 1, 0, x_all.shape[1] // tile)
     for copy in copies:
         copy.wait()
     run_tiles(count[0], lists, values, 1, x_all, acc, tile)
@@ -317,7 +371,6 @@
     d = lax.axis_index("dom")
     sd = jax.ShapeDtypeStruct
     lists = [pltpu.SMEM((ntiles + GROUP,), jnp.int32)] * 3
-    rep = replica.reshape(1, slots)
     tile_flops = 2 * ntiles * feats * tile * tile
 
     def call(body, flops, args, specs, outs, scratch=(), grid=(), out_specs=None, alias={}):
@@ -349,25 +402,43 @@
         ]
 
     vec = sd((feats, width), BF)
-    pull, *x_halves = call(
+    pull, rep, *x_halves = call(
         functools.partial(prep_kernel, nf),
         2 * slots * feats * masters,
-        [features, rep],
+        [features, replica],
         [None] * 2,
-        [sd((nd, per, feats), BF)] + [vec] * nf,
+        [sd((nd, per, feats), BF), sd((1, slots), jnp.int32)] + [vec] * nf,
     )
     mirrors = exchange(pull, "dom")
     x_parts = [x_halves[0]] + [to_peer(x_halves[j], j) for j in range(1, nf)]
 
     blocks = tile_blocks.T
     chunk = sd((feats, part), BF)
+    sums = pltpu.VMEM((feats, cols), F32)
+    all_values = pltpu.VMEM(tile_values.shape, BF)
+    pair = pltpu.SemaphoreType.DMA((2,))
+    (own_sums,) = call(
+        functools.partial(spread_own, tile),
+        tile_flops,
+        [blocks, tile_counts, features, tile_values],
+        [SMEM, SMEM, ANY, ANY],
+        [sd((feats, masters + slots), BF)],
+        [sums, pltpu.VMEM((feats, masters), BF), all_values, *lists, pair],
+    )
     own_part, push, *part_sends = call(
-        functools.partial(spread_kernel, nf, nc, tile),
-        tile_flops,
-        [blocks, tile_counts, mirrors, features, tile_values],
+        functools.partial(spread_mirrors, nf, nc, tile),
+        tile_flops // 4,
+        [blocks, tile_counts, mirrors, tile_values, own_sums],
         [SMEM, SMEM, None, ANY, ANY],
         [vec, sd((nd, nf, per, feats), BF)] + [chunk] * ((nf - 1) * nc),
-        tile_scratch(nf * nc + 1),
+        [
+            sums,
+            pltpu.VMEM((feats, masters + slots), BF),
+            pltpu.VMEM((feats, slots), BF),
+            all_values,
+            *lists,
+            pair,
+        ],
     )
     part_recv = [
         [to_peer(part_sends[(j - 1) * nc + c], j) for j in range(1, nf)]
@@ -378,20 +449,11 @@
     flat_w = weights.reshape(2 * wide, wide)
     wt = flat_w.T
     rows, grads, grad_own, grad_recv, self_own, self_recv = [], [], [], [], [], []
-    vb = 256 if part % 256 == 0 else 128
-    steps = part // vb
-
-    def of_all(height, c):
-        return pl.BlockSpec((height, vb), lambda i: (0, c * steps + i))
-
-    def of_chunk(height):
-        return pl.BlockSpec((height, vb), lambda i: (0, i))
-
+    step = 256 if part % 256 == 0 else 128
     for c in range(nc):
         last = c + 1 == nc
-        args = [rep, wt, flat_w, incoming, cotangent, *x_parts, own_part, *part_recv[c]]
-        specs = [None] * 4 + [of_all(wide, c)] + [of_all(feats, c)] * (nf + 1)
-        specs += [of_chunk(feats)] * (nf - 1)
+        args = [rep, incoming, wt, flat_w, cotangent, *x_parts, own_part, *part_recv[c]]
+        specs = [None] * 2 + [ANY] * (len(args) - 2)
         alias = {}
         if c:
             alias = {len(args) + 1: 1}
@@ -403,8 +465,6 @@
             sd((wide, part), BF),
             sd((nd, nf, per, feats) if last else (wide, slots), BF),
         ] + [chunk] * (2 * nf)
-        out_specs = [of_chunk(wide), of_all(wide, c), of_chunk(wide), full(outs[3])]
-        out_specs += [of_chunk(feats)] * (2 * nf)
         rows_c, output, g_c, pay, *res = call(
             functools.partial(dense_kernel, nf, nc, c),
             8 * wide * wide * part,
@@ -412,13 +472,19 @@
             specs,
             outs,
             [
-                pltpu.VMEM((2 * wide, vb), BF),
-                pltpu.VMEM((2 * wide, vb), BF),
-                pltpu.VMEM((nf, feats, slots), BF),
-                pltpu.VMEM((wide, slots), F32),
+                pltpu.VMEM((wide, 2 * wide), BF),
+                pltpu.VMEM((2 * wide, wide), BF),
+                pltpu.VMEM((wide, part), BF),
+                pltpu.VMEM((2 * wide, part), BF),
+                pltpu.VMEM((nf, feats, part), BF),
+                pltpu.VMEM((wide, part), BF),
+                pltpu.VMEM((wide, part), BF),
+                pltpu.VMEM((2 * wide, part), BF),
+                pltpu.SemaphoreType.DMA((2 * nf + 3,)),
+                pltpu.SemaphoreType.DMA((1 + (part // step) * (2 * nf + 2),)),
             ],
-            (steps,),
-            out_specs,
+            (),
+            [ANY] * 3 + [full(outs[3])] + [ANY] * (2 * nf),
             alias,
         )
         rows.append(rows_c)

time: 145 us -> 142 us (0.979)
  waiting for transfers between devices: 46.9 us -> 41.4 us
  Pallas kernels: 48.3 us -> 50.2 us
  starting transfers between devices: 38.4 us -> 40.3 us
    all_to_all x4, waiting for transfers between devices: 6.38 us -> 0.97 us  [exchange(): return lax.all_to_all(flat, axes, 0, 0, tiled=True).reshape(x.shape)]
    pallas_call x8 -> x9, Pallas kernels: 48.3 us -> 50.2 us  [call(): pl.pallas_call(body, grid=grid, in_specs=[full(a) if p is None else p for...]
  transfers between devices with their start and end apart: 22 -> 22, of which waited for: 7 -> 7; matrix products, arithmetic and copies ran while one was open for 1% -> 1% of each run, Pallas kernels for 19% -> 22%
where the time goes in v2:
time: 142 us; the launch traced here: 141 us
  Pallas kernels  50.2 us (35%)
  waiting for transfers between devices  41.4 us (29%)
  starting transfers between devices  40.3 us (28%)
  local copies, waits for them, and re-layouts  5.98 us (4%)
  between operations  1.58 us (1%)
  other arithmetic  1.51 us (1%)
    pallas_call x9, Pallas kernels, call(): pl.pallas_call(body, grid=grid, in_specs=[full(a) if p is None else p for...  50.2 us
    ppermute x8, waiting for transfers between devices, to_peer(): return lax.ppermute(x, 'feat', [(i, (i + j) % nf) for i in range(nf)])  26.2 us
    all_to_all x4, starting transfers between devices, exchange(): return lax.all_to_all(flat, axes, 0, 0, tiled=True).reshape(x.shape)  18.5 us
    ppermute x10, waiting for transfers between devices, swap(): return lax.ppermute(x, 'dom', [(i, i ^ b) for i in range(nd)])  14.2 us
    ppermute x10, starting transfers between devices, swap(): return lax.ppermute(x, 'dom', [(i, i ^ b) for i in range(nd)])  11.7 us
    ppermute x8, starting transfers between devices, to_peer(): return lax.ppermute(x, 'feat', [(i, (i + j) % nf) for i in range(nf)])  10.1 us
    unnamed x35, local copies, waits for them, and re-layouts  4.58 us
  transfers between devices with their start and end apart: 22, of which 7 were waited for; matrix products, arithmetic and copies ran while one was open for 1% of the time, Pallas kernels for 22%

profile of v2, /device:TPU:0, one launch (start us, length us, event | category | flops | bytes accessed | tf_op | source)
XLA Modules:
  0.0 141.0 jit_solution(14193414241794210584)
XLA Ops:
  0.6 3.5 %shard_map.94 = (bf16[16,16,256]{2,1,0:T(8,128)(2,1)}, s32[1,256]{1,0:T(1,128)}, bf16[256,1536]{1,0:T(8,128)(2,1)}, bf16[256,1536]{1,0:T(8,128)(2,1)}) custom-call(bf16[256,3072]{1,0:T(8,128)(2,1)} %x_ref.3, s32[1,16,16]{2,1,0:T(8,128)} %replica.1), custom_call_target="tpu_custom_call" | custom-call | flops 402653184 | bytes 1573376 | tf_op jit(solution)/shard_map/pallas_call | solution.py:377
  4.1 3.0 %collective-permute-start = (bf16[256,1536]{1,0:T(8,128)(2,1)}, bf16[256,1536]{1,0:T(8,128)(2,1)S(1)}, u32[]{:S(2)}, u32[]{:S(2)}) collective-permute-start(bf16[256,1536]{1,0:T(8,128)(2,1)} %get-tuple-element.35), channel_id=1, source_target_pairs={{0,1},{1,0},{2,3},{3,2},{4,5},{5,4},{6,7},{7,6},{8,9},{9,8},{10,11... | collective-permute-start | bytes 2359304 | tf_op jit(solution)/shard_map/ppermute | solution.py:389
  7.1 5.9 %all-to-all-start = ((bf16[16,16,256]{2,1,0:T(8,128)(2,1)}), bf16[16,16,256]{2,1,0:T(8,128)(2,1)S(1)}, u32[]{:S(2)}, u32[]{:S(2)}) async-start(bf16[16,16,256]{2,1,0:T(8,128)(2,1)} %get-tuple-element.32), calls=%async_computation | async-start | bytes 262144 | tf_op jit(solution)/shard_map/all_to_all | solution.py:393
  13.7 7.0 %shard_map.95.own_ref = bf16[256,3328]{1,0:T(8,128)(2,1)} custom-call(s32[2,72]{1,0:T(2,128)} %bitcast.26, s32[1]{0:T(128)S(6)} %copy.18.count, bf16[256,3072]{1,0:T(8,128)(2,1)} %x_ref.3, bf16[72,128,128]{2,1,0:T(8,128)(2,1)} %values_ref.5), custom_call_target="tpu_custom_call" | custom-call | flops 603979776 | bytes 3932450 | tf_op jit(solution)/shard_map/pallas_call | solution.py:377
  21.6 5.0 %shard_map.96 = (bf16[256,1536]{1,0:T(8,128)(2,1)}, bf16[16,2,16,256]{3,2,1,0:T(8,128)(2,1)}, bf16[256,768]{1,0:T(8,128)(2,1)}, bf16[256,768]{1,0:T(8,128)(2,1)}) custom-call(s32[2,72]{1,0:T(2,128)} %bitcast.27, s32[1]{0:T(128)S(6)} %copy.18.count, bf16[16,16,256]{2,1,0:T(8,128)(2,1)} %copy-done.4, bf16[72,128,128]{2,1,0:T(8,128)(2,1)} %values_ref.5, ...), custom_call_target="tpu_custom_call" | custom-call | flops 150994944 | bytes 4194594 | tf_op jit(solution)/shard_map/pallas_call | solution.py:377
  26.6 4.5 %all-to-all-start.1 = ((bf16[32,16,256]{2,1,0:T(8,128)(2,1)}), bf16[32,16,256]{2,1,0:T(8,128)(2,1)S(1)}, u32[]{:S(2)}, u32[]{:S(2)}) async-start(bf16[32,16,256]{2,1,0:T(8,128)(2,1)} %bitcast.25), calls=%async_computation.1 | async-start | bytes 524288 | tf_op jit(solution)/shard_map/all_to_all | solution.py:393
  31.1 1.8 %collective-permute-start.2 = (bf16[256,768]{1,0:T(8,128)(2,1)}, bf16[256,768]{1,0:T(8,128)(2,1)S(1)}, u32[]{:S(2)}, u32[]{:S(2)}) collective-permute-start(bf16[256,768]{1,0:T(8,128)(2,1)} %get-tuple-element.38), channel_id=1, source_target_pairs={{0,1},{1,0},{2,3},{3,2},{4,5},{5,4},{6,7},{7,6},{8,9},{9,8},{10,11... | collective-permute-start | bytes 1179656 | tf_op jit(solution)/shard_map/ppermute | solution.py:389
  33.2 1.3 copy.12.refs_2_
  34.5 11.3 %collective-permute-done.2.refs_8_ = bf16[256,768]{1,0:T(8,128)(2,1)S(1)} collective-permute-done((bf16[256,768]{1,0:T(8,128)(2,1)}, bf16[256,768]{1,0:T(8,128)(2,1)S(1)}, u32[]{:S(2)}, u32[]{:S(2)}) %collective-permute-start.2) | collective-permute-done | bytes 393248 | tf_op jit(solution)/shard_map/ppermute | solution.py:389
  47.0 7.7 %shard_map.97 = (bf16[512,768]{1,0:T(8,128)(2,1)}, bf16[512,1536]{1,0:T(8,128)(2,1)}, bf16[512,768]{1,0:T(8,128)(2,1)}, bf16[512,256]{1,0:T(8,128)(2,1)}, bf16[2...) custom-call(s32[1,256]{1,0:T(1,128)} %get-tuple-element.31.refs_0_.rep_ref, ...), custom_call_target="tpu_custom_call" | custom-call | flops 1610612736 | bytes 6685184 | tf_op jit(solution)/shard_map/pallas_call | solution.py:377
  55.4 7.8 %shard_map.98 = (bf16[512,768]{1,0:T(8,128)(2,1)}, bf16[512,1536]{1,0:T(8,128)(2,1)}, bf16[512,768]{1,0:T(8,128)(2,1)}, bf16[16,2,16,256]{3,2,1,0:T(8,128)(2,1)}...) custom-call(s32[1,256]{1,0:T(1,128)} %get-tuple-element.31.refs_0_.r, ...), custom_call_target="tpu_custom_call", output_to_operand_aliasing={{1}: (10, {})} | custom-call | flops 1610612736 | bytes 8520192 | tf_op jit(solution)/shard_map/pallas_call | solution.py:377
  63.3 5.5 %shard_map.101 = (f32[2,256,512]{2,1,0:T(8,128)}, bf16[2,256,512]{2,1,0:T(8,128)(2,1)}) custom-call(bf16[256,1536]{1,0:T(8,128)(2,1)} %get-tuple-element.34.refs_5_.refs_0_, bf16[256,1536]{1,0:T(8,128)(2,1)} %copy-done.1, bf16[512,768]{1,0:T(8,128)(2,1)} %get-tuple-element.53.refs_2_, bf16[512,768]{1,0:T(8,128)(2,1)} %get-tuple-element.54.refs_3_, ...), custom_call_target="tpu_custom_call" | custom-call | flops 1610612736 | bytes 4718592 | tf_op jit(solution)/shard_map/pallas_call | solution.py:377
  68.7 2.1 %collective-permute-done.7 = bf16[2,256,512]{2,1,0:T(8,128)(2,1)S(1)} collective-permute-done((bf16[2,256,512]{2,1,0:T(8,128)(2,1)}, bf16[2,256,512]{2,1,0:T(8,128)(2,1)S(1)}, u32[]{:S(2)}, u32[]{:S(2)}) %collective-permute-start.7) | collective-permute-done | bytes 524320 | tf_op jit(solution)/shard_map/ppermute | solution.py:521
  70.8 1.4 convert_add_fusion
  72.3 1.3 collective-permute-start.8
  73.6 7.1 %collective-permute-done.8 = bf16[2,128,512]{2,1,0:T(8,128)(2,1)S(1)} collective-permute-done((bf16[2,128,512]{2,1,0:T(8,128)(2,1)S(1)}, bf16[2,128,512]{2,1,0:T(8,128)(2,1)S(1)}, u32[]{:S(2)}, u32[]{:S(2)}) %collective-permute-start.8) | collective-permute-done | bytes 262176 | tf_op jit(solution)/shard_map/ppermute | solution.py:521
  80.8 2.5 %collective-permute-start.10 = (bf16[2,32,512]{2,1,0:T(8,128)(2,1)S(1)}, bf16[2,32,512]{2,1,0:T(8,128)(2,1)S(1)}, u32[]{:S(2)}, u32[]{:S(2)}) collective-permute-start(bf16[2,32,512]{2,1,0:T(8,128)(2,1)S(1)} %get-tuple-element.63), channel_id=1, source_target_pairs={{0,16},{2,18},{4,20},{6,22},{8,24},{10,26},{12,28},{14,30},{16,0},... | collective-permute-start | bytes 196616 | tf_op jit(solution)/shard_map/ppermute | solution.py:521
  83.3 1.5 %collective-permute-start.11 = (bf16[2,32,512]{2,1,0:T(8,128)(2,1)S(1)}, bf16[2,32,512]{2,1,0:T(8,128)(2,1)S(1)}, u32[]{:S(2)}, u32[]{:S(2)}) collective-permute-start(bf16[2,32,512]{2,1,0:T(8,128)(2,1)S(1)} %get-tuple-element.62), channel_id=1, source_target_pairs={{0,24},{2,26},{4,28},{6,30},{8,16},{10,18},{12,20},{14,22},{16,8},... | collective-permute-start | bytes 196616 | tf_op jit(solution)/shard_map/ppermute | solution.py:521
  84.8 0.8 collective-permute-start.4
  85.6 4.6 %all-to-all-start.2 = ((bf16[32,16,256]{2,1,0:T(8,128)(2,1)}), bf16[32,16,256]{2,1,0:T(8,128)(2,1)S(1)}, u32[]{:S(2)}, u32[]{:S(2)}) async-start(bf16[32,16,256]{2,1,0:T(8,128)(2,1)} %bitcast.5), calls=%async_computation.2 | async-start | bytes 524288 | tf_op jit(solution)/shard_map/all_to_all | solution.py:393
  90.2 1.7 %collective-permute-start.3 = (bf16[256,768]{1,0:T(8,128)(2,1)}, bf16[256,768]{1,0:T(8,128)(2,1)S(1)}, u32[]{:S(2)}, u32[]{:S(2)}) collective-permute-start(bf16[256,768]{1,0:T(8,128)(2,1)} %get-tuple-element.45), channel_id=1, source_target_pairs={{0,1},{1,0},{2,3},{3,2},{4,5},{5,4},{6,7},{7,6},{8,9},{9,8},{10,11... | collective-permute-start | bytes 1179656 | tf_op jit(solution)/shard_map/ppermute | solution.py:389
  92.4 1.6 %collective-permute-start.6 = (bf16[256,768]{1,0:T(8,128)(2,1)S(1)}, bf16[256,768]{1,0:T(8,128)(2,1)S(1)}, u32[]{:S(2)}, u32[]{:S(2)}) collective-permute-start(bf16[256,768]{1,0:T(8,128)(2,1)S(1)} %copy-done.15), channel_id=1, source_target_pairs={{0,1},{1,0},{2,3},{3,2},{4,5},{5,4},{6,7},{7,6},{8,9},{9,8},{10,11... | collective-permute-start | bytes 1179656 | tf_op jit(solution)/shard_map/ppermute | solution.py:389
  94.4 14.9 %collective-permute-done.12 = f32[32,512]{1,0:T(8,128)S(1)} collective-permute-done((f32[32,512]{1,0:T(8,128)S(1)}, f32[32,512]{1,0:T(8,128)S(1)}, u32[]{:S(2)}, u32[]{:S(2)}) %collective-permute-start.12) | collective-permute-done | bytes 65568 | tf_op jit(solution)/shard_map/ppermute | solution.py:389
  109.3 2.0 %collective-permute-start.13 = (bf16[32,512]{1,0:T(8,128)(2,1)S(1)}, bf16[32,512]{1,0:T(8,128)(2,1)S(1)}, u32[]{:S(2)}, u32[]{:S(2)}) collective-permute-start(bf16[32,512]{1,0:T(8,128)(2,1)S(1)} %get-tuple-element.60), channel_id=1, source_target_pairs={{0,8},{2,10},{4,12},{6,14},{8,0},{10,2},{12,4},{14,6},{16,24},{18,... | collective-permute-start | bytes 98312 | tf_op jit(solution)/shard_map/ppermute | solution.py:521
  111.3 1.0 collective-permute-start.14
  112.3 1.5 %collective-permute-start.15 = (bf16[32,512]{1,0:T(8,128)(2,1)S(1)}, bf16[32,512]{1,0:T(8,128)(2,1)S(1)}, u32[]{:S(2)}, u32[]{:S(2)}) collective-permute-start(bf16[32,512]{1,0:T(8,128)(2,1)S(1)} %get-tuple-element.60), channel_id=1, source_target_pairs={{0,24},{2,26},{4,28},{6,30},{8,16},{10,18},{12,20},{14,22},{16,8},... | collective-permute-start | bytes 98312 | tf_op jit(solution)/shard_map/ppermute | solution.py:521
  114.5 7.4 %shard_map.99 = (bf16[256,3072]{1,0:T(8,128)(2,1)}, bf16[16,16,256]{2,1,0:T(8,128)(2,1)}) custom-call(s32[2,72]{1,0:T(2,128)} %bitcast.28, s32[1]{0:T(128)S(6)} %copy.18.count, bf16[16,2,16,256]{3,2,1,0:T(8,128)(2,1)} %bitcast.23, bf16[72,128,128]{2,1,0:T(8,128)(2,1)} %values_ref.5, bf16[256,768]{1,0:T(8,128)(2,1)} %get-tuple-element.43.rest_0_, ...), custom_call_target="tpu_custom_call" | custom-call | flops 603979776 | bytes 4194594 | tf_op jit(solution)/shard_map/pallas_call | solution.py:377
  121.9 3.5 %all-to-all-start.3 = ((bf16[16,16,256]{2,1,0:T(8,128)(2,1)}), bf16[16,16,256]{2,1,0:T(8,128)(2,1)S(1)}, u32[]{:S(2)}, u32[]{:S(2)}) async-start(bf16[16,16,256]{2,1,0:T(8,128)(2,1)} %get-tuple-element.47), calls=%async_computation.3 | async-start | bytes 262144 | tf_op jit(solution)/shard_map/all_to_all | solution.py:393
  125.5 1.9 %collective-permute-start.16 = (bf16[128,512]{1,0:T(8,128)(2,1)S(1)}, bf16[128,512]{1,0:T(8,128)(2,1)S(1)}, u32[]{:S(2)}, u32[]{:S(2)}) collective-permute-start(bf16[128,512]{1,0:T(8,128)(2,1)S(1)} %pad_maximum_fusion), channel_id=1, source_target_pairs={{0,4},{2,6},{4,0},{6,2},{8,12},{10,14},{12,8},{14,10},{16,20},{18,... | collective-permute-start | bytes 393224 | tf_op jit(solution)/shard_map/ppermute | solution.py:521
  127.4 5.0 %collective-permute-done.16 = bf16[128,512]{1,0:T(8,128)(2,1)S(1)} collective-permute-done((bf16[128,512]{1,0:T(8,128)(2,1)S(1)}, bf16[128,512]{1,0:T(8,128)(2,1)S(1)}, u32[]{:S(2)}, u32[]{:S(2)}) %collective-permute-start.16) | collective-permute-done | bytes 131104 | tf_op jit(solution)/shard_map/ppermute | solution.py:521
  133.9 4.0 %shard_map.100 = bf16[256,3072]{1,0:T(8,128)(2,1)} custom-call(s32[1,256]{1,0:T(1,128)} %get-tuple-element.31.refs_0_.rep_ref, bf16[16,16,256]{2,1,0:T(8,128)(2,1)} %copy-done.5, bf16[256,3072]{1,0:T(8,128)(2,1)} %get-tuple-element.48.back_ref, bf16[256,768]{1,0:T(8,128)(2,1)} %get-tuple-element.49.rest_0_, bf16[256,768]{1,0:T(8,128)(2,1)} %get-tuple-element.50.rest_1_, ...), custom_call_target="tpu_custom_call" | custom-call | flops 402653184 | bytes 3277312 | tf_op jit(solution)/shard_map/pallas_call | solution.py:377
  138.7 2.3 %shard_map.102 = f32[512,512]{1,0:T(8,128)} custom-call(bf16[256,512]{1,0:T(8,128)(2,1)} %copy-done.12, bf16[256,512]{1,0:T(8,128)(2,1)} %copy-done.13), custom_call_target="tpu_custom_call" | custom-call | bytes 524288 | tf_op jit(solution)/shard_map/pallas_call | solution.py:377
  (66 shorter events, 7.1 us)
Async XLA Ops:
  4.1 41.7 %collective-permute-start = (bf16[256,1536]{1,0:T(8,128)(2,1)}, bf16[256,1536]{1,0:T(8,128)(2,1)S(1)}, u32[]{:S(2)}, u32[]{:S(2)}) collective-permute-start(bf16[256,1536]{1,0:T(8,128)(2,1)} %get-tuple-element.35), channel_id=1, source_target_pairs={{0,1},{1,0},{2,3},{3,2},{4,5},{5,4},{6,7},{7,6},{8,9},{9,8},{10,11... | collective-permute-start | bytes 2359304 | tf_op jit(solution)/shard_map/ppermute | solution.py:389
  7.1 13.8 %all-to-all-start = ((bf16[16,16,256]{2,1,0:T(8,128)(2,1)}), bf16[16,16,256]{2,1,0:T(8,128)(2,1)S(1)}, u32[]{:S(2)}, u32[]{:S(2)}) async-start(bf16[16,16,256]{2,1,0:T(8,128)(2,1)} %get-tuple-element.32), calls=%async_computation | async-start | bytes 262144 | tf_op jit(solution)/shard_map/all_to_all | solution.py:393
  20.7 12.5 %copy-start = (bf16[2,512,512]{2,1,0:T(8,128)(2,1)S(1)}, bf16[2,512,512]{2,1,0:T(8,128)(2,1)}, u32[]{:S(2)}) copy-start(bf16[2,512,512]{2,1,0:T(8,128)(2,1)} %param.8) | copy-start | bytes 3145732
  26.6 19.2 %all-to-all-start.1 = ((bf16[32,16,256]{2,1,0:T(8,128)(2,1)}), bf16[32,16,256]{2,1,0:T(8,128)(2,1)S(1)}, u32[]{:S(2)}, u32[]{:S(2)}) async-start(bf16[32,16,256]{2,1,0:T(8,128)(2,1)} %bitcast.25), calls=%async_computation.1 | async-start | bytes 524288 | tf_op jit(solution)/shard_map/all_to_all | solution.py:393
  31.1 14.7 %collective-permute-start.2 = (bf16[256,768]{1,0:T(8,128)(2,1)}, bf16[256,768]{1,0:T(8,128)(2,1)S(1)}, u32[]{:S(2)}, u32[]{:S(2)}) collective-permute-start(bf16[256,768]{1,0:T(8,128)(2,1)} %get-tuple-element.38), channel_id=1, source_target_pairs={{0,1},{1,0},{2,3},{3,2},{4,5},{5,4},{6,7},{7,6},{8,9},{9,8},{10,11... | collective-permute-start | bytes 1179656 | tf_op jit(solution)/shard_map/ppermute | solution.py:389
  33.0 21.7 %collective-permute-start.1 = (bf16[256,768]{1,0:T(8,128)(2,1)}, bf16[256,768]{1,0:T(8,128)(2,1)S(1)}, u32[]{:S(2)}, u32[]{:S(2)}) collective-permute-start(bf16[256,768]{1,0:T(8,128)(2,1)} %get-tuple-element.37), channel_id=1, source_target_pairs={{0,1},{1,0},{2,3},{3,2},{4,5},{5,4},{6,7},{7,6},{8,9},{9,8},{10,11... | collective-permute-start | bytes 1179656 | tf_op jit(solution)/shard_map/ppermute | solution.py:389
  45.8 0.9 copy-start.2
  45.8 1.1 copy-start.1
  68.7 2.1 %collective-permute-start.7 = (bf16[2,256,512]{2,1,0:T(8,128)(2,1)}, bf16[2,256,512]{2,1,0:T(8,128)(2,1)S(1)}, u32[]{:S(2)}, u32[]{:S(2)}) collective-permute-start(bf16[2,256,512]{2,1,0:T(8,128)(2,1)} %get-tuple-element.58), channel_id=1, source_target_pairs={{0,2},{2,0},{4,6},{6,4},{8,10},{10,8},{12,14},{14,12},{16,18},{18,... | collective-permute-start | bytes 1572872 | tf_op jit(solution)/shard_map/ppermute | solution.py:521
  72.3 20.1 %copy-start.15 = (bf16[256,768]{1,0:T(8,128)(2,1)S(1)}, bf16[256,768]{1,0:T(8,128)(2,1)}, u32[]{:S(2)}) copy-start(bf16[256,768]{1,0:T(8,128)(2,1)} %get-tuple-element.52) | copy-start | bytes 1179652
  72.3 21.7 %copy-start.14 = (bf16[256,768]{1,0:T(8,128)(2,1)S(1)}, bf16[256,768]{1,0:T(8,128)(2,1)}, u32[]{:S(2)}) copy-start(bf16[256,768]{1,0:T(8,128)(2,1)} %get-tuple-element.51) | copy-start | bytes 1179652
  72.3 8.4 %collective-permute-start.8 = (bf16[2,128,512]{2,1,0:T(8,128)(2,1)S(1)}, bf16[2,128,512]{2,1,0:T(8,128)(2,1)S(1)}, u32[]{:S(2)}, u32[]{:S(2)}) collective-permute-start(bf16[2,128,512]{2,1,0:T(8,128)(2,1)S(1)} %dynamic-slice_convert_fusion), channel_id=1, source_target_pairs={{0,4},{2,6},{4,0},{6,2},{8,12},{10,14},{12,8},{14,10},{16,20},{18,... | collective-permute-start | bytes 786440 | tf_op jit(solution)/shard_map/ppermute | solution.py:521
  80.8 11.0 %collective-permute-start.10 = (bf16[2,32,512]{2,1,0:T(8,128)(2,1)S(1)}, bf16[2,32,512]{2,1,0:T(8,128)(2,1)S(1)}, u32[]{:S(2)}, u32[]{:S(2)}) collective-permute-start(bf16[2,32,512]{2,1,0:T(8,128)(2,1)S(1)} %get-tuple-element.63), channel_id=1, source_target_pairs={{0,16},{2,18},{4,20},{6,22},{8,24},{10,26},{12,28},{14,30},{16,0},... | collective-permute-start | bytes 196616 | tf_op jit(solution)/shard_map/ppermute | solution.py:521
  83.3 8.5 %collective-permute-start.11 = (bf16[2,32,512]{2,1,0:T(8,128)(2,1)S(1)}, bf16[2,32,512]{2,1,0:T(8,128)(2,1)S(1)}, u32[]{:S(2)}, u32[]{:S(2)}) collective-permute-start(bf16[2,32,512]{2,1,0:T(8,128)(2,1)S(1)} %get-tuple-element.62), channel_id=1, source_target_pairs={{0,24},{2,26},{4,28},{6,30},{8,16},{10,18},{12,20},{14,22},{16,8},... | collective-permute-start | bytes 196616 | tf_op jit(solution)/shard_map/ppermute | solution.py:521
  84.8 7.0 %collective-permute-start.9 = (bf16[2,32,512]{2,1,0:T(8,128)(2,1)S(1)}, bf16[2,32,512]{2,1,0:T(8,128)(2,1)S(1)}, u32[]{:S(2)}, u32[]{:S(2)}) collective-permute-start(bf16[2,32,512]{2,1,0:T(8,128)(2,1)S(1)} %get-tuple-element.61), channel_id=1, source_target_pairs={{0,8},{2,10},{4,12},{6,14},{8,0},{10,2},{12,4},{14,6},{16,24},{18,... | collective-permute-start | bytes 196616 | tf_op jit(solution)/shard_map/ppermute | solution.py:521
  84.8 26.5 %collective-permute-start.4 = (bf16[256,768]{1,0:T(8,128)(2,1)}, bf16[256,768]{1,0:T(8,128)(2,1)S(1)}, u32[]{:S(2)}, u32[]{:S(2)}) collective-permute-start(bf16[256,768]{1,0:T(8,128)(2,1)} %get-tuple-element.46), channel_id=1, source_target_pairs={{0,1},{1,0},{2,3},{3,2},{4,5},{5,4},{6,7},{7,6},{8,9},{9,8},{10,11... | collective-permute-start | bytes 1179656 | tf_op jit(solution)/shard_map/ppermute | solution.py:389
  85.6 28.2 %all-to-all-start.2 = ((bf16[32,16,256]{2,1,0:T(8,128)(2,1)}), bf16[32,16,256]{2,1,0:T(8,128)(2,1)S(1)}, u32[]{:S(2)}, u32[]{:S(2)}) async-start(bf16[32,16,256]{2,1,0:T(8,128)(2,1)} %bitcast.5), calls=%async_computation.2 | async-start | bytes 524288 | tf_op jit(solution)/shard_map/all_to_all | solution.py:393
  90.2 22.1 %collective-permute-start.3 = (bf16[256,768]{1,0:T(8,128)(2,1)}, bf16[256,768]{1,0:T(8,128)(2,1)S(1)}, u32[]{:S(2)}, u32[]{:S(2)}) collective-permute-start(bf16[256,768]{1,0:T(8,128)(2,1)} %get-tuple-element.45), channel_id=1, source_target_pairs={{0,1},{1,0},{2,3},{3,2},{4,5},{5,4},{6,7},{7,6},{8,9},{9,8},{10,11... | collective-permute-start | bytes 1179656 | tf_op jit(solution)/shard_map/ppermute | solution.py:389
  91.9 17.4 %collective-permute-start.12 = (f32[32,512]{1,0:T(8,128)S(1)}, f32[32,512]{1,0:T(8,128)S(1)}, u32[]{:S(2)}, u32[]{:S(2)}) collective-permute-start(f32[32,512]{1,0:T(8,128)S(1)} %slice_bitcast_fusion), channel_id=1, source_target_pairs={{0,1},{1,0},{2,3},{3,2},{4,5},{5,4},{6,7},{7,6},{8,9},{9,8},{10,11... | collective-permute-start | bytes 196616 | tf_op jit(solution)/shard_map/ppermute | solution.py:389
  92.4 40.1 %collective-permute-start.6 = (bf16[256,768]{1,0:T(8,128)(2,1)S(1)}, bf16[256,768]{1,0:T(8,128)(2,1)S(1)}, u32[]{:S(2)}, u32[]{:S(2)}) collective-permute-start(bf16[256,768]{1,0:T(8,128)(2,1)S(1)} %copy-done.15), channel_id=1, source_target_pairs={{0,1},{1,0},{2,3},{3,2},{4,5},{5,4},{6,7},{7,6},{8,9},{9,8},{10,11... | collective-permute-start | bytes 1179656 | tf_op jit(solution)/shard_map/ppermute | solution.py:389
  94.0 38.6 %collective-permute-start.5 = (bf16[256,768]{1,0:T(8,128)(2,1)S(1)}, bf16[256,768]{1,0:T(8,128)(2,1)S(1)}, u32[]{:S(2)}, u32[]{:S(2)}) collective-permute-start(bf16[256,768]{1,0:T(8,128)(2,1)S(1)} %copy-done.14), channel_id=1, source_target_pairs={{0,1},{1,0},{2,3},{3,2},{4,5},{5,4},{6,7},{7,6},{8,9},{9,8},{10,11... | collective-permute-start | bytes 1179656 | tf_op jit(solution)/shard_map/ppermute | solution.py:389
  109.3 16.1 %collective-permute-start.13 = (bf16[32,512]{1,0:T(8,128)(2,1)S(1)}, bf16[32,512]{1,0:T(8,128)(2,1)S(1)}, u32[]{:S(2)}, u32[]{:S(2)}) collective-permute-start(bf16[32,512]{1,0:T(8,128)(2,1)S(1)} %get-tuple-element.60), channel_id=1, source_target_pairs={{0,8},{2,10},{4,12},{6,14},{8,0},{10,2},{12,4},{14,6},{16,24},{18,... | collective-permute-start | bytes 98312 | tf_op jit(solution)/shard_map/ppermute | solution.py:521
  111.3 2.5 %copy-start.7 = (bf16[256,768]{1,0:T(8,128)(2,1)}, bf16[256,768]{1,0:T(8,128)(2,1)S(1)}, u32[]{:S(2)}) copy-start(bf16[256,768]{1,0:T(8,128)(2,1)S(1)} %collective-permute-done.4.rest_3_) | copy-start | bytes 1179652
  111.3 14.1 %collective-permute-start.14 = (bf16[32,512]{1,0:T(8,128)(2,1)S(1)}, bf16[32,512]{1,0:T(8,128)(2,1)S(1)}, u32[]{:S(2)}, u32[]{:S(2)}) collective-permute-start(bf16[32,512]{1,0:T(8,128)(2,1)S(1)} %get-tuple-element.60), channel_id=1, source_target_pairs={{0,16},{2,18},{4,20},{6,22},{8,24},{10,26},{12,28},{14,30},{16,0},... | collective-permute-start | bytes 98312 | tf_op jit(solution)/shard_map/ppermute | solution.py:521
  112.3 1.5 %copy-start.8 = (bf16[256,768]{1,0:T(8,128)(2,1)}, bf16[256,768]{1,0:T(8,128)(2,1)S(1)}, u32[]{:S(2)}) copy-start(bf16[256,768]{1,0:T(8,128)(2,1)S(1)} %collective-permute-done.3.rest_2_) | copy-start | bytes 1179652
  112.3 13.2 %collective-permute-start.15 = (bf16[32,512]{1,0:T(8,128)(2,1)S(1)}, bf16[32,512]{1,0:T(8,128)(2,1)S(1)}, u32[]{:S(2)}, u32[]{:S(2)}) collective-permute-start(bf16[32,512]{1,0:T(8,128)(2,1)S(1)} %get-tuple-element.60), channel_id=1, source_target_pairs={{0,24},{2,26},{4,28},{6,30},{8,16},{10,18},{12,20},{14,22},{16,8},... | collective-permute-start | bytes 98312 | tf_op jit(solution)/shard_map/ppermute | solution.py:521
  121.9 11.4 %all-to-all-start.3 = ((bf16[16,16,256]{2,1,0:T(8,128)(2,1)}), bf16[16,16,256]{2,1,0:T(8,128)(2,1)S(1)}, u32[]{:S(2)}, u32[]{:S(2)}) async-start(bf16[16,16,256]{2,1,0:T(8,128)(2,1)} %get-tuple-element.47), calls=%async_computation.3 | async-start | bytes 262144 | tf_op jit(solution)/shard_map/all_to_all | solution.py:393
  125.5 6.9 %collective-permute-start.16 = (bf16[128,512]{1,0:T(8,128)(2,1)S(1)}, bf16[128,512]{1,0:T(8,128)(2,1)S(1)}, u32[]{:S(2)}, u32[]{:S(2)}) collective-permute-start(bf16[128,512]{1,0:T(8,128)(2,1)S(1)} %pad_maximum_fusion), channel_id=1, source_target_pairs={{0,4},{2,6},{4,0},{6,2},{8,12},{10,14},{12,8},{14,10},{16,20},{18,... | collective-permute-start | bytes 393224 | tf_op jit(solution)/shard_map/ppermute | solution.py:521
  132.4 5.6 %copy-start.12 = (bf16[256,512]{1,0:T(8,128)(2,1)}, bf16[256,512]{1,0:T(8,128)(2,1)S(1)}, u32[]{:S(2)}) copy-start(bf16[256,512]{1,0:T(8,128)(2,1)S(1)} %constant_dynamic-update-slice_fusion.own_ref) | copy-start | bytes 786436
  132.4 5.6 %collective-permute-start.17 = (bf16[256,512]{1,0:T(8,128)(2,1)S(1)}, bf16[256,512]{1,0:T(8,128)(2,1)S(1)}, u32[]{:S(2)}, u32[]{:S(2)}) collective-permute-start(bf16[256,512]{1,0:T(8,128)(2,1)S(1)} %constant_dynamic-update-slice_fusion.own_ref), channel_id=1, source_target_pairs={{0,2},{2,0},{4,6},{6,4},{8,10},{10,8},{12,14},{14,12},{16,18},{18,... | collective-permute-start | bytes 786440 | tf_op jit(solution)/shard_map/ppermute | solution.py:521
  132.5 0.8 copy-start.10
  132.6 0.9 copy-start.11
  (6 other events, 4.2 us)

commit v3 on v2

--- a/solution.py
+++ b/solution.py
@@ -10,6 +10,7 @@
 BF = jnp.bfloat16
 F32 = jnp.float32
 GROUP = 8
+SMALL = 24 * 1024 * 1024
 
 
 def dot(a, b, ca=1, cb=0):
@@ -166,7 +167,7 @@
     refs = refs[5 + 2 * nf :]
     if c:
         pay_in = refs[0]
-        refs = refs[2:]
+        refs = refs[2 + nf :]
     agg_hbm, out_hbm, g_hbm, pay_ref = refs[:4]
     grads, selfs = refs[4 : 4 + nf], refs[4 + nf : 4 + 2 * nf]
     wt, w, cot, rows, terms, out, g_all, both, in_sems, out_sems = refs[4 + 2 * nf :]
@@ -223,7 +224,7 @@
             at = lax.rem(h + j, nf)
             peer = pl.ds(pl.multiple_of(wide + at * feats, feats), feats)
             put(both.at[peer, cols], grads[j].at[:, cols])
-            put(both.at[place(at), cols], selfs[j].at[:, cols])
+            put(both.at[place(at), cols], selfs[j].at[:, pl.ds(c * part + b, step)])
         put(g_all.at[:, cols], g_hbm.at[:, cols])
         put(out.at[:, cols], out_hbm.at[:, pl.ds(c * part + b, step)])
     pay = dot(both[wide:, :], pick)
@@ -241,27 +242,31 @@
 
 
 def weight_kernel(nf, nc, *refs):
-    xs, aggs, grads = refs[:nf], refs[nf : nf + nc], refs[nf + nc : nf + 2 * nc]
-    keep_ref, send_ref, acc = refs[nf + 2 * nc :]
+    ins = refs[: nf + 2 * nc]
+    keep_ref, send_ref, acc = refs[nf + 2 * nc : nf + 2 * nc + 3]
+    held, sems = refs[nf + 2 * nc + 3 : -1], refs[-1]
     h = lax.axis_index("feat")
     bit = lax.rem(lax.axis_index("dom"), 2)
     wide = acc.shape[1]
     feats = wide // nf
+    copies = [pltpu.make_async_copy(a, b, sems.at[k]) for k, (a, b) in enumerate(zip(ins, held))]
+    order = [[nf + nc + c, nf + c] for c in range(nc)]
+    order[0] += list(range(nf))
+    for group in order:
+        for k in group:
+            copies[k].start()
+    xs, aggs, grads = held[:nf], held[nf : nf + nc], held[nf + nc :]
     part = grads[0].shape[1]
-
-    def summed(terms):
-        total = None
-        for left, right in terms:
-            term = dot(left, right, 1, 1)
-            total = term if total is None else total + term
-        return total
-
-    acc[wide:, :] = summed((aggs[c][...], grads[c][...]) for c in range(nc))
-    for j in range(nf):
-        at = pl.multiple_of(lax.rem(h - j + nf, nf) * feats, feats)
-        acc[pl.ds(at, feats), :] = summed(
-            (xs[j][:, c * part : (c + 1) * part], grads[c][...]) for c in range(nc)
-        )
+    for c in range(nc):
+        for k in order[c]:
+            copies[k].wait()
+        terms = [(pl.ds(wide, wide), aggs[c][...])]
+        for j in range(nf):
+            at = pl.multiple_of(lax.rem(h - j + nf, nf) * feats, feats)
+            terms.append((pl.ds(at, feats), xs[j][:, c * part : (c + 1) * part]))
+        for at, left in terms:
+            term = dot(left, grads[c][...], 1, 1)
+            acc[at, :] = term if c == 0 else acc[at, :] + term
     for j in range(nf):
         at = lax.rem(h + j, nf) * feats
         keep_ref[j] = acc[pl.ds(pl.multiple_of(bit * wide + at, feats), feats), :]
@@ -344,9 +349,10 @@
 
 
 def final_kernel(nf, nc, rep_ref, inc_ref, back_ref, *rest):
-    selfs, out_ref = rest[: nf * nc], rest[nf * nc]
+    selfs, out_ref = rest[:nf], rest[nf]
     h = lax.axis_index("feat")
-    feats, part = selfs[0].shape
+    feats, width = selfs[0].shape
+    part = width // nc
     slots = rep_ref.shape[1]
     inc = flip(inc_ref[...].reshape(slots, feats))
     for j in range(nf):
@@ -354,7 +360,7 @@
             at = pl.multiple_of((lax.rem(h - j + nf, nf) * nc + c) * part, 128)
             back = back_ref[:, pl.ds(at, part)].astype(F32)
             back = back + dot(inc, picks(rep_ref[...], at, part), 1, 1)
-            own = selfs[j * nc + c][...].astype(F32)
+            own = selfs[j][:, c * part : (c + 1) * part].astype(F32)
             out_ref[:, pl.ds(at, part)] = (own + back).astype(BF)
 
 
@@ -373,7 +379,7 @@
     lists = [pltpu.SMEM((ntiles + GROUP,), jnp.int32)] * 3
     tile_flops = 2 * ntiles * feats * tile * tile
 
-    def call(body, flops, args, specs, outs, scratch=(), grid=(), out_specs=None, alias={}):
+    def call(body, flops, args, specs, outs, scratch=(), grid=(), out_specs=None, alias={}, limit=None):
         return pl.pallas_call(
             body,
             grid=grid,
@@ -382,6 +388,7 @@
             out_shape=outs,
             scratch_shapes=list(scratch),
             input_output_aliases=alias,
+            compiler_params=pltpu.CompilerParams(vmem_limit_bytes=limit),
             cost_estimate=cost(flops, 2 * sum(a.size for a in args)),
         )(*args)
 
@@ -448,7 +455,7 @@
 
     flat_w = weights.reshape(2 * wide, wide)
     wt = flat_w.T
-    rows, grads, grad_own, grad_recv, self_own, self_recv = [], [], [], [], [], []
+    rows, grads, grad_own, grad_recv = [], [], [], []
     step = 256 if part % 256 == 0 else 128
     for c in range(nc):
         last = c + 1 == nc
@@ -457,14 +464,15 @@
         alias = {}
         if c:
             alias = {len(args) + 1: 1}
-            args += [pay, output]
-            specs += [None, ANY]
+            alias |= {len(args) + 2 + j: 4 + nf + j for j in range(nf)}
+            args += [pay, output, *selfs]
+            specs += [None] + [ANY] * (1 + nf)
         outs = [
             sd((wide, part), BF),
             sd((wide, width), BF),
             sd((wide, part), BF),
             sd((nd, nf, per, feats) if last else (wide, slots), BF),
-        ] + [chunk] * (2 * nf)
+        ] + [chunk] * nf + [vec] * nf
         rows_c, output, g_c, pay, *res = call(
             functools.partial(dense_kernel, nf, nc, c),
             8 * wide * wide * part,
@@ -490,18 +498,21 @@
         rows.append(rows_c)
         grads.append(g_c)
         grad_own.append(res[0])
-        self_own.append(res[nf])
+        selfs = res[nf:]
         grad_recv.append([to_peer(res[j], j) for j in range(1, nf)])
-        self_recv.append([to_peer(res[nf + j], j) for j in range(1, nf)])
+    selfs = [selfs[0]] + [to_peer(selfs[j], j) for j in range(1, nf)]
     grad_mirrors = exchange(pay, ("dom", "feat"))
 
     keep, send = call(
         functools.partial(weight_kernel, nf, nc),
         4 * wide * wide * width,
         x_parts + rows + grads,
-        [None] * (nf + 2 * nc),
+        [ANY] * (nf + 2 * nc),
         [sd((nf, feats, wide), F32), sd((nf, feats, wide), BF)],
-        [pltpu.VMEM((2 * wide, wide), F32)],
+        [pltpu.VMEM((2 * wide, wide), F32)]
+        + [pltpu.VMEM((feats, width), BF)] * nf
+        + [pltpu.VMEM((wide, part), BF)] * (2 * nc)
+        + [pltpu.SemaphoreType.DMA((nf + 2 * nc,))],
     )
 
     flat_grads = grad_own + [grad_recv[c][j] for j in range(nf - 1) for c in range(nc)]
@@ -551,6 +562,7 @@
             [total, other],
             [None] * 2,
             [sd((2 * feats, wide), F32)],
+            limit=SMALL,
         )
     else:
         total = jnp.concatenate([total, other], 0).reshape(nd, -1, wide)
@@ -564,14 +576,13 @@
         weight_grad = total[index].reshape(2 * feats, wide).astype(F32)
     weight_grad = weight_grad.reshape(2, feats, wide)
 
-    selfs = [self_own[c] for c in range(nc)]
-    selfs += [self_recv[c][j] for j in range(nf - 1) for c in range(nc)]
     (feature_grad,) = call(
         functools.partial(final_kernel, nf, nc),
         2 * slots * feats * masters,
         [rep, back_in, back, *selfs],
-        [None] * (3 + nf * nc),
+        [None] * (3 + nf),
         [sd((feats, masters), BF)],
+        limit=SMALL,
     )
     return output, feature_grad, weight_grad
 

time: 142 us -> 139 us (0.979)
  Pallas kernels: 50.2 us -> 47.1 us
    pallas_call x9, Pallas kernels: 50.2 us -> 47.1 us  [call(): pl.pallas_call(body, grid=grid, in_specs=[full(a) if p is None else p for...]
    ppermute x8 -> x7, waiting for transfers between devices: 26.2 us -> 25.4 us  [to_peer(): return lax.ppermute(x, 'feat', [(i, (i + j) % nf) for i in range(nf)])]
    ppermute x8 -> x7, starting transfers between devices: 10.1 us -> 10 us  [to_peer(): return lax.ppermute(x, 'feat', [(i, (i + j) % nf) for i in range(nf)])]
    unnamed x35 -> x27, local copies, waits for them, and re-layouts: 4.58 us -> 4.62 us
  transfers between devices with their start and end apart: 22 -> 21, of which waited for: 7 -> 7; matrix products, arithmetic and copies ran while one was open for 1% -> 1% of each run, Pallas kernels for 22% -> 21%
where the time goes in v3:
time: 139 us; the launch traced here: 138 us
  Pallas kernels  47.1 us (34%)
  starting transfers between devices  41.5 us (30%)
  waiting for transfers between devices  40.6 us (29%)
  local copies, waits for them, and re-layouts  6.02 us (4%)
  between operations  1.58 us (1%)
  other arithmetic  1.51 us (1%)
    pallas_call x9, Pallas kernels, call(): pl.pallas_call(body, grid=grid, in_specs=[full(a) if p is None else p for...  47.1 us
    ppermute x7, waiting for transfers between devices, to_peer(): return lax.ppermute(x, 'feat', [(i, (i + j) % nf) for i in range(nf)])  25.4 us
    all_to_all x4, starting transfers between devices, exchange(): return lax.all_to_all(flat, axes, 0, 0, tiled=True).reshape(x.shape)  19.1 us
    ppermute x10, waiting for transfers between devices, swap(): return lax.ppermute(x, 'dom', [(i, i ^ b) for i in range(nd)])  14.2 us
    ppermute x10, starting transfers between devices, swap(): return lax.ppermute(x, 'dom', [(i, i ^ b) for i in range(nd)])  12.3 us
    ppermute x7, starting transfers between devices, to_peer(): return lax.ppermute(x, 'feat', [(i, (i + j) % nf) for i in range(nf)])  10 us
    unnamed x27, local copies, waits for them, and re-layouts  4.62 us
  transfers between devices with their start and end apart: 21, of which 7 were waited for; matrix products, arithmetic and copies ran while one was open for 1% of the time, Pallas kernels for 21%

profile of v3, /device:TPU:0, one launch (start us, length us, event | category | flops | bytes accessed | tf_op | source)
XLA Modules:
  0.0 138.3 jit_solution(9947878421849208621)
XLA Ops:
  0.6 3.5 %shard_map.94 = (bf16[16,16,256]{2,1,0:T(8,128)(2,1)}, s32[1,256]{1,0:T(1,128)}, bf16[256,1536]{1,0:T(8,128)(2,1)}, bf16[256,1536]{1,0:T(8,128)(2,1)}) custom-call(bf16[256,3072]{1,0:T(8,128)(2,1)} %x_ref.3, s32[1,16,16]{2,1,0:T(8,128)} %replica.1), custom_call_target="tpu_custom_call" | custom-call | flops 402653184 | bytes 1573376 | tf_op jit(solution)/shard_map/pallas_call | solution.py:383
  4.1 3.0 %collective-permute-start = (bf16[256,1536]{1,0:T(8,128)(2,1)}, bf16[256,1536]{1,0:T(8,128)(2,1)S(1)}, u32[]{:S(2)}, u32[]{:S(2)}) collective-permute-start(bf16[256,1536]{1,0:T(8,128)(2,1)} %get-tuple-element.35), channel_id=1, source_target_pairs={{0,1},{1,0},{2,3},{3,2},{4,5},{5,4},{6,7},{7,6},{8,9},{9,8},{10,11... | collective-permute-start | bytes 2359304 | tf_op jit(solution)/shard_map/ppermute | solution.py:396
  7.1 5.9 %all-to-all-start = ((bf16[16,16,256]{2,1,0:T(8,128)(2,1)}), bf16[16,16,256]{2,1,0:T(8,128)(2,1)S(1)}, u32[]{:S(2)}, u32[]{:S(2)}) async-start(bf16[16,16,256]{2,1,0:T(8,128)(2,1)} %get-tuple-element.32), calls=%async_computation | async-start | bytes 262144 | tf_op jit(solution)/shard_map/all_to_all | solution.py:400
  13.7 7.0 %shard_map.95.own_ref = bf16[256,3328]{1,0:T(8,128)(2,1)} custom-call(s32[2,72]{1,0:T(2,128)} %bitcast.27, s32[1]{0:T(128)S(6)} %copy.22.count, bf16[256,3072]{1,0:T(8,128)(2,1)} %x_ref.3, bf16[72,128,128]{2,1,0:T(8,128)(2,1)} %values_ref.5), custom_call_target="tpu_custom_call" | custom-call | flops 603979776 | bytes 3932450 | tf_op jit(solution)/shard_map/pallas_call | solution.py:383
  21.6 5.0 %shard_map.96 = (bf16[256,1536]{1,0:T(8,128)(2,1)}, bf16[16,2,16,256]{3,2,1,0:T(8,128)(2,1)}, bf16[256,768]{1,0:T(8,128)(2,1)}, bf16[256,768]{1,0:T(8,128)(2,1)}) custom-call(s32[2,72]{1,0:T(2,128)} %bitcast.28, s32[1]{0:T(128)S(6)} %copy.22.count, bf16[16,16,256]{2,1,0:T(8,128)(2,1)} %copy-done.8, bf16[72,128,128]{2,1,0:T(8,128)(2,1)} %values_ref.5, ...), custom_call_target="tpu_custom_call" | custom-call | flops 150994944 | bytes 4194594 | tf_op jit(solution)/shard_map/pallas_call | solution.py:383
  26.6 4.5 %all-to-all-start.1 = ((bf16[32,16,256]{2,1,0:T(8,128)(2,1)}), bf16[32,16,256]{2,1,0:T(8,128)(2,1)S(1)}, u32[]{:S(2)}, u32[]{:S(2)}) async-start(bf16[32,16,256]{2,1,0:T(8,128)(2,1)} %bitcast.26), calls=%async_computation.1 | async-start | bytes 524288 | tf_op jit(solution)/shard_map/all_to_all | solution.py:400
  31.1 1.8 %collective-permute-start.2 = (bf16[256,768]{1,0:T(8,128)(2,1)}, bf16[256,768]{1,0:T(8,128)(2,1)S(1)}, u32[]{:S(2)}, u32[]{:S(2)}) collective-permute-start(bf16[256,768]{1,0:T(8,128)(2,1)} %get-tuple-element.38), channel_id=1, source_target_pairs={{0,1},{1,0},{2,3},{3,2},{4,5},{5,4},{6,7},{7,6},{8,9},{9,8},{10,11... | collective-permute-start | bytes 1179656 | tf_op jit(solution)/shard_map/ppermute | solution.py:396
  33.2 1.3 copy.14.refs_2_
  34.5 11.3 %collective-permute-done.2.refs_8_ = bf16[256,768]{1,0:T(8,128)(2,1)S(1)} collective-permute-done((bf16[256,768]{1,0:T(8,128)(2,1)}, bf16[256,768]{1,0:T(8,128)(2,1)S(1)}, u32[]{:S(2)}, u32[]{:S(2)}) %collective-permute-start.2) | collective-permute-done | bytes 393248 | tf_op jit(solution)/shard_map/ppermute | solution.py:396
  46.9 7.7 %shard_map.97 = (bf16[512,768]{1,0:T(8,128)(2,1)}, bf16[512,1536]{1,0:T(8,128)(2,1)}, bf16[512,768]{1,0:T(8,128)(2,1)}, bf16[512,256]{1,0:T(8,128)(2,1)}, bf16[2...) custom-call(s32[1,256]{1,0:T(1,128)} %get-tuple-element.31.refs_0_.rep_ref, ...), custom_call_target="tpu_custom_call" | custom-call | flops 1610612736 | bytes 6685184 | tf_op jit(solution)/shard_map/pallas_call | solution.py:383
  55.4 7.8 %shard_map.98 = (bf16[512,768]{1,0:T(8,128)(2,1)}, bf16[512,1536]{1,0:T(8,128)(2,1)}, bf16[512,768]{1,0:T(8,128)(2,1)}, bf16[16,2,16,256]{3,2,1,0:T(8,128)(2,1)}...) custom-call(s32[1,256]{1,0:T(1,128)} %get-tuple-element.31.refs_0_.r, ...), custom_call_target="tpu_custom_call", output_to_operand_aliasing={{1}: (10, {}), {6}: (11, {}), {7}: (12, {})} | custom-call | flops 1610612736 | bytes 10093056 | tf_op jit(solution)/shard_map/pallas_call | solution.py:383
  63.2 5.2 %shard_map.101 = (f32[2,256,512]{2,1,0:T(8,128)}, bf16[2,256,512]{2,1,0:T(8,128)(2,1)}) custom-call(bf16[256,1536]{1,0:T(8,128)(2,1)} %get-tuple-element.34.refs_5_.refs_0_, bf16[256,1536]{1,0:T(8,128)(2,1)} %copy-done.4, bf16[512,768]{1,0:T(8,128)(2,1)} %get-tuple-element.53.refs_2_, bf16[512,768]{1,0:T(8,128)(2,1)} %get-tuple-element.54.refs_3_, ...), custom_call_target="tpu_custom_call" | custom-call | flops 1610612736 | bytes 4718592 | tf_op jit(solution)/shard_map/pallas_call | solution.py:383
  68.6 2.1 %collective-permute-done.6 = bf16[2,256,512]{2,1,0:T(8,128)(2,1)S(1)} collective-permute-done((bf16[2,256,512]{2,1,0:T(8,128)(2,1)}, bf16[2,256,512]{2,1,0:T(8,128)(2,1)S(1)}, u32[]{:S(2)}, u32[]{:S(2)}) %collective-permute-start.6) | collective-permute-done | bytes 524320 | tf_op jit(solution)/shard_map/ppermute | solution.py:532
  70.6 1.4 %convert_add_fusion = f32[2,256,512]{2,1,0:T(8,128)S(1)} fusion(f32[2,256,512]{2,1,0:T(8,128)} %get-tuple-element.57, bf16[2,256,512]{2,1,0:T(8,128)(2,1)S(1)} %collective-permute-done.6), kind=kLoop, calls=%fused_computation | loop fusion | flops 524288 | bytes 2621440 | tf_op jit(solution)/shard_map/add | solution.py:539
  72.1 1.3 collective-permute-start.7
  73.4 7.1 %collective-permute-done.7 = bf16[2,128,512]{2,1,0:T(8,128)(2,1)S(1)} collective-permute-done((bf16[2,128,512]{2,1,0:T(8,128)(2,1)S(1)}, bf16[2,128,512]{2,1,0:T(8,128)(2,1)S(1)}, u32[]{:S(2)}, u32[]{:S(2)}) %collective-permute-start.7) | collective-permute-done | bytes 262176 | tf_op jit(solution)/shard_map/ppermute | solution.py:532
  80.6 3.4 %collective-permute-start.10 = (bf16[2,32,512]{2,1,0:T(8,128)(2,1)S(1)}, bf16[2,32,512]{2,1,0:T(8,128)(2,1)S(1)}, u32[]{:S(2)}, u32[]{:S(2)}) collective-permute-start(bf16[2,32,512]{2,1,0:T(8,128)(2,1)S(1)} %get-tuple-element.62), channel_id=1, source_target_pairs={{0,24},{2,26},{4,28},{6,30},{8,16},{10,18},{12,20},{14,22},{16,8},... | collective-permute-start | bytes 196616 | tf_op jit(solution)/shard_map/ppermute | solution.py:532
  84.0 1.1 collective-permute-start.9
  85.1 1.0 collective-permute-start.4
  86.1 4.5 %all-to-all-start.2 = ((bf16[32,16,256]{2,1,0:T(8,128)(2,1)}), bf16[32,16,256]{2,1,0:T(8,128)(2,1)S(1)}, u32[]{:S(2)}, u32[]{:S(2)}) async-start(bf16[32,16,256]{2,1,0:T(8,128)(2,1)} %bitcast.25), calls=%async_computation.2 | async-start | bytes 524288 | tf_op jit(solution)/shard_map/all_to_all | solution.py:400
  90.6 1.8 %collective-permute-start.3 = (bf16[256,768]{1,0:T(8,128)(2,1)}, bf16[256,768]{1,0:T(8,128)(2,1)}, u32[]{:S(2)}, u32[]{:S(2)}) collective-permute-start(bf16[256,768]{1,0:T(8,128)(2,1)} %get-tuple-element.47), channel_id=1, source_target_pairs={{0,1},{1,0},{2,3},{3,2},{4,5},{5,4},{6,7},{7,6},{8,9},{9,8},{10,11... | collective-permute-start | bytes 1179656 | tf_op jit(solution)/shard_map/ppermute | solution.py:396
  92.8 1.8 %collective-permute-start.5 = (bf16[256,1536]{1,0:T(8,128)(2,1)S(1)}, bf16[256,1536]{1,0:T(8,128)(2,1)S(1)}, u32[]{:S(2)}, u32[]{:S(2)}) collective-permute-start(bf16[256,1536]{1,0:T(8,128)(2,1)S(1)} %copy-done.7), channel_id=1, source_target_pairs={{0,1},{1,0},{2,3},{3,2},{4,5},{5,4},{6,7},{7,6},{8,9},{9,8},{10,11... | collective-permute-start | bytes 2359304 | tf_op jit(solution)/shard_map/ppermute | solution.py:396
  94.6 14.1 %collective-permute-done.11 = f32[32,512]{1,0:T(8,128)S(1)} collective-permute-done((f32[32,512]{1,0:T(8,128)S(1)}, f32[32,512]{1,0:T(8,128)S(1)}, u32[]{:S(2)}, u32[]{:S(2)}) %collective-permute-start.11) | collective-permute-done | bytes 65568 | tf_op jit(solution)/shard_map/ppermute | solution.py:396
  108.7 1.0 collective-permute-start.12
  109.7 2.9 %collective-permute-start.13 = (bf16[32,512]{1,0:T(8,128)(2,1)S(1)}, bf16[32,512]{1,0:T(8,128)(2,1)S(1)}, u32[]{:S(2)}, u32[]{:S(2)}) collective-permute-start(bf16[32,512]{1,0:T(8,128)(2,1)S(1)} %get-tuple-element.60), channel_id=1, source_target_pairs={{0,16},{2,18},{4,20},{6,22},{8,24},{10,26},{12,28},{14,30},{16,0},... | collective-permute-start | bytes 98312 | tf_op jit(solution)/shard_map/ppermute | solution.py:532
  113.9 7.5 %shard_map.99 = (bf16[256,3072]{1,0:T(8,128)(2,1)}, bf16[16,16,256]{2,1,0:T(8,128)(2,1)}) custom-call(s32[2,72]{1,0:T(2,128)} %bitcast.29, s32[1]{0:T(128)S(6)} %copy.22.count, bf16[16,2,16,256]{3,2,1,0:T(8,128)(2,1)} %bitcast.23, bf16[72,128,128]{2,1,0:T(8,128)(2,1)} %values_ref.5, bf16[256,768]{1,0:T(8,128)(2,1)} %get-tuple-element.45.rest_0_, ...), custom_call_target="tpu_custom_call" | custom-call | flops 603979776 | bytes 4194594 | tf_op jit(solution)/shard_map/pallas_call | solution.py:383
  121.4 4.2 %all-to-all-start.3 = ((bf16[16,16,256]{2,1,0:T(8,128)(2,1)}), bf16[16,16,256]{2,1,0:T(8,128)(2,1)S(1)}, u32[]{:S(2)}, u32[]{:S(2)}) async-start(bf16[16,16,256]{2,1,0:T(8,128)(2,1)} %get-tuple-element.49), calls=%async_computation.3 | async-start | bytes 262144 | tf_op jit(solution)/shard_map/all_to_all | solution.py:400
  125.6 2.0 %collective-permute-start.15 = (bf16[128,512]{1,0:T(8,128)(2,1)S(1)}, bf16[128,512]{1,0:T(8,128)(2,1)S(1)}, u32[]{:S(2)}, u32[]{:S(2)}) collective-permute-start(bf16[128,512]{1,0:T(8,128)(2,1)S(1)} %pad_maximum_fusion), channel_id=1, source_target_pairs={{0,4},{2,6},{4,0},{6,2},{8,12},{10,14},{12,8},{14,10},{16,20},{18,... | collective-permute-start | bytes 393224 | tf_op jit(solution)/shard_map/ppermute | solution.py:532
  127.6 5.0 %collective-permute-done.15 = bf16[128,512]{1,0:T(8,128)(2,1)S(1)} collective-permute-done((bf16[128,512]{1,0:T(8,128)(2,1)S(1)}, bf16[128,512]{1,0:T(8,128)(2,1)S(1)}, u32[]{:S(2)}, u32[]{:S(2)}) %collective-permute-start.15) | collective-permute-done | bytes 131104 | tf_op jit(solution)/shard_map/ppermute | solution.py:532
  133.5 1.4 %copy-done.1 = bf16[256,3072]{1,0:T(8,128)(2,1)S(1)} copy-done((bf16[256,3072]{1,0:T(8,128)(2,1)S(1)}, bf16[256,3072]{1,0:T(8,128)(2,1)}, u32[]{:S(2)}) %copy-start.1) | copy-done | bytes 1572888
  134.9 2.1 %shard_map.100 = bf16[256,3072]{1,0:T(8,128)(2,1)} custom-call(s32[1,256]{1,0:T(1,128)S(1)} %copy-done.2, bf16[16,16,256]{2,1,0:T(8,128)(2,1)S(1)} %all-to-all-done.3.inc_ref, bf16[256,3072]{1,0:T(8,128)(2,1)S(1)} %copy-done.1, bf16[256,1536]{1,0:T(8,128)(2,1)S(1)} %copy-done, bf16[256,1536]{1,0:T(8,128)(2,1)S(1)} %collective-permute-done.5.rest_1_), custom_call_target="tpu_custom_call" | custom-call | flops 402653184 | bytes 3277312 | tf_op jit(solution)/shard_map/pallas_call | solution.py:383
  137.0 1.2 shard_map.102
  (56 shorter events, 5.8 us)
Async XLA Ops:
  4.1 41.7 %collective-permute-start = (bf16[256,1536]{1,0:T(8,128)(2,1)}, bf16[256,1536]{1,0:T(8,128)(2,1)S(1)}, u32[]{:S(2)}, u32[]{:S(2)}) collective-permute-start(bf16[256,1536]{1,0:T(8,128)(2,1)} %get-tuple-element.35), channel_id=1, source_target_pairs={{0,1},{1,0},{2,3},{3,2},{4,5},{5,4},{6,7},{7,6},{8,9},{9,8},{10,11... | collective-permute-start | bytes 2359304 | tf_op jit(solution)/shard_map/ppermute | solution.py:396
  7.1 13.8 %all-to-all-start = ((bf16[16,16,256]{2,1,0:T(8,128)(2,1)}), bf16[16,16,256]{2,1,0:T(8,128)(2,1)S(1)}, u32[]{:S(2)}, u32[]{:S(2)}) async-start(bf16[16,16,256]{2,1,0:T(8,128)(2,1)} %get-tuple-element.32), calls=%async_computation | async-start | bytes 262144 | tf_op jit(solution)/shard_map/all_to_all | solution.py:400
  20.7 12.5 %copy-start.3 = (bf16[2,512,512]{2,1,0:T(8,128)(2,1)S(1)}, bf16[2,512,512]{2,1,0:T(8,128)(2,1)}, u32[]{:S(2)}) copy-start(bf16[2,512,512]{2,1,0:T(8,128)(2,1)} %param.8) | copy-start | bytes 3145732
  26.6 19.2 %all-to-all-start.1 = ((bf16[32,16,256]{2,1,0:T(8,128)(2,1)}), bf16[32,16,256]{2,1,0:T(8,128)(2,1)S(1)}, u32[]{:S(2)}, u32[]{:S(2)}) async-start(bf16[32,16,256]{2,1,0:T(8,128)(2,1)} %bitcast.26), calls=%async_computation.1 | async-start | bytes 524288 | tf_op jit(solution)/shard_map/all_to_all | solution.py:400
  31.1 14.7 %collective-permute-start.2 = (bf16[256,768]{1,0:T(8,128)(2,1)}, bf16[256,768]{1,0:T(8,128)(2,1)S(1)}, u32[]{:S(2)}, u32[]{:S(2)}) collective-permute-start(bf16[256,768]{1,0:T(8,128)(2,1)} %get-tuple-element.38), channel_id=1, source_target_pairs={{0,1},{1,0},{2,3},{3,2},{4,5},{5,4},{6,7},{7,6},{8,9},{9,8},{10,11... | collective-permute-start | bytes 1179656 | tf_op jit(solution)/shard_map/ppermute | solution.py:396
  33.0 21.7 %collective-permute-start.1 = (bf16[256,768]{1,0:T(8,128)(2,1)}, bf16[256,768]{1,0:T(8,128)(2,1)S(1)}, u32[]{:S(2)}, u32[]{:S(2)}) collective-permute-start(bf16[256,768]{1,0:T(8,128)(2,1)} %get-tuple-element.37), channel_id=1, source_target_pairs={{0,1},{1,0},{2,3},{3,2},{4,5},{5,4},{6,7},{7,6},{8,9},{9,8},{10,11... | collective-permute-start | bytes 1179656 | tf_op jit(solution)/shard_map/ppermute | solution.py:396
  45.8 0.8 copy-start.10
  45.8 0.9 copy-start.5
  45.8 1.1 copy-start.4
  54.6 0.8 copy-start.11
  68.5 2.2 %collective-permute-start.6 = (bf16[2,256,512]{2,1,0:T(8,128)(2,1)}, bf16[2,256,512]{2,1,0:T(8,128)(2,1)S(1)}, u32[]{:S(2)}, u32[]{:S(2)}) collective-permute-start(bf16[2,256,512]{2,1,0:T(8,128)(2,1)} %get-tuple-element.58), channel_id=1, source_target_pairs={{0,2},{2,0},{4,6},{6,4},{8,10},{10,8},{12,14},{14,12},{16,18},{18,... | collective-permute-start | bytes 1572872 | tf_op jit(solution)/shard_map/ppermute | solution.py:532
  72.1 20.8 %copy-start.7 = (bf16[256,1536]{1,0:T(8,128)(2,1)S(1)}, bf16[256,1536]{1,0:T(8,128)(2,1)}, u32[]{:S(2)}) copy-start(bf16[256,1536]{1,0:T(8,128)(2,1)} %get-tuple-element.52) | copy-start | bytes 2359300
  72.1 8.4 %collective-permute-start.7 = (bf16[2,128,512]{2,1,0:T(8,128)(2,1)S(1)}, bf16[2,128,512]{2,1,0:T(8,128)(2,1)S(1)}, u32[]{:S(2)}, u32[]{:S(2)}) collective-permute-start(bf16[2,128,512]{2,1,0:T(8,128)(2,1)S(1)} %dynamic-slice_convert_fusion), channel_id=1, source_target_pairs={{0,4},{2,6},{4,0},{6,2},{8,12},{10,14},{12,8},{14,10},{16,20},{18,... | collective-permute-start | bytes 786440 | tf_op jit(solution)/shard_map/ppermute | solution.py:532
  80.6 11.8 %collective-permute-start.10 = (bf16[2,32,512]{2,1,0:T(8,128)(2,1)S(1)}, bf16[2,32,512]{2,1,0:T(8,128)(2,1)S(1)}, u32[]{:S(2)}, u32[]{:S(2)}) collective-permute-start(bf16[2,32,512]{2,1,0:T(8,128)(2,1)S(1)} %get-tuple-element.62), channel_id=1, source_target_pairs={{0,24},{2,26},{4,28},{6,30},{8,16},{10,18},{12,20},{14,22},{16,8},... | collective-permute-start | bytes 196616 | tf_op jit(solution)/shard_map/ppermute | solution.py:532
  84.0 8.4 %collective-permute-start.8 = (bf16[2,32,512]{2,1,0:T(8,128)(2,1)S(1)}, bf16[2,32,512]{2,1,0:T(8,128)(2,1)S(1)}, u32[]{:S(2)}, u32[]{:S(2)}) collective-permute-start(bf16[2,32,512]{2,1,0:T(8,128)(2,1)S(1)} %get-tuple-element.61), channel_id=1, source_target_pairs={{0,8},{2,10},{4,12},{6,14},{8,0},{10,2},{12,4},{14,6},{16,24},{18,... | collective-permute-start | bytes 196616 | tf_op jit(solution)/shard_map/ppermute | solution.py:532
  84.0 8.4 %collective-permute-start.9 = (bf16[2,32,512]{2,1,0:T(8,128)(2,1)S(1)}, bf16[2,32,512]{2,1,0:T(8,128)(2,1)S(1)}, u32[]{:S(2)}, u32[]{:S(2)}) collective-permute-start(bf16[2,32,512]{2,1,0:T(8,128)(2,1)S(1)} %get-tuple-element.63), channel_id=1, source_target_pairs={{0,16},{2,18},{4,20},{6,22},{8,24},{10,26},{12,28},{14,30},{16,0},... | collective-permute-start | bytes 196616 | tf_op jit(solution)/shard_map/ppermute | solution.py:532
  85.1 27.5 %collective-permute-start.4 = (bf16[256,768]{1,0:T(8,128)(2,1)}, bf16[256,768]{1,0:T(8,128)(2,1)S(1)}, u32[]{:S(2)}, u32[]{:S(2)}) collective-permute-start(bf16[256,768]{1,0:T(8,128)(2,1)} %get-tuple-element.48), channel_id=1, source_target_pairs={{0,1},{1,0},{2,3},{3,2},{4,5},{5,4},{6,7},{7,6},{8,9},{9,8},{10,11... | collective-permute-start | bytes 1179656 | tf_op jit(solution)/shard_map/ppermute | solution.py:396
  86.1 27.1 %all-to-all-start.2 = ((bf16[32,16,256]{2,1,0:T(8,128)(2,1)}), bf16[32,16,256]{2,1,0:T(8,128)(2,1)S(1)}, u32[]{:S(2)}, u32[]{:S(2)}) async-start(bf16[32,16,256]{2,1,0:T(8,128)(2,1)} %bitcast.25), calls=%async_computation.2 | async-start | bytes 524288 | tf_op jit(solution)/shard_map/all_to_all | solution.py:400
  90.6 22.6 %collective-permute-start.3 = (bf16[256,768]{1,0:T(8,128)(2,1)}, bf16[256,768]{1,0:T(8,128)(2,1)}, u32[]{:S(2)}, u32[]{:S(2)}) collective-permute-start(bf16[256,768]{1,0:T(8,128)(2,1)} %get-tuple-element.47), channel_id=1, source_target_pairs={{0,1},{1,0},{2,3},{3,2},{4,5},{5,4},{6,7},{7,6},{8,9},{9,8},{10,11... | collective-permute-start | bytes 1179656 | tf_op jit(solution)/shard_map/ppermute | solution.py:396
  92.5 16.2 %collective-permute-start.11 = (f32[32,512]{1,0:T(8,128)S(1)}, f32[32,512]{1,0:T(8,128)S(1)}, u32[]{:S(2)}, u32[]{:S(2)}) collective-permute-start(f32[32,512]{1,0:T(8,128)S(1)} %slice_bitcast_fusion), channel_id=1, source_target_pairs={{0,1},{1,0},{2,3},{3,2},{4,5},{5,4},{6,7},{7,6},{8,9},{9,8},{10,11... | collective-permute-start | bytes 196616 | tf_op jit(solution)/shard_map/ppermute | solution.py:396
  92.8 40.6 %collective-permute-start.5 = (bf16[256,1536]{1,0:T(8,128)(2,1)S(1)}, bf16[256,1536]{1,0:T(8,128)(2,1)S(1)}, u32[]{:S(2)}, u32[]{:S(2)}) collective-permute-start(bf16[256,1536]{1,0:T(8,128)(2,1)S(1)} %copy-done.7), channel_id=1, source_target_pairs={{0,1},{1,0},{2,3},{3,2},{4,5},{5,4},{6,7},{7,6},{8,9},{9,8},{10,11... | collective-permute-start | bytes 2359304 | tf_op jit(solution)/shard_map/ppermute | solution.py:396
  108.7 16.9 %collective-permute-start.12 = (bf16[32,512]{1,0:T(8,128)(2,1)S(1)}, bf16[32,512]{1,0:T(8,128)(2,1)S(1)}, u32[]{:S(2)}, u32[]{:S(2)}) collective-permute-start(bf16[32,512]{1,0:T(8,128)(2,1)S(1)} %get-tuple-element.60), channel_id=1, source_target_pairs={{0,8},{2,10},{4,12},{6,14},{8,0},{10,2},{12,4},{14,6},{16,24},{18,... | collective-permute-start | bytes 98312 | tf_op jit(solution)/shard_map/ppermute | solution.py:532
  109.7 15.9 %collective-permute-start.13 = (bf16[32,512]{1,0:T(8,128)(2,1)S(1)}, bf16[32,512]{1,0:T(8,128)(2,1)S(1)}, u32[]{:S(2)}, u32[]{:S(2)}) collective-permute-start(bf16[32,512]{1,0:T(8,128)(2,1)S(1)} %get-tuple-element.60), channel_id=1, source_target_pairs={{0,16},{2,18},{4,20},{6,22},{8,24},{10,26},{12,28},{14,30},{16,0},... | collective-permute-start | bytes 98312 | tf_op jit(solution)/shard_map/ppermute | solution.py:532
  112.6 0.7 copy-start.9
  112.6 13.0 %collective-permute-start.14 = (bf16[32,512]{1,0:T(8,128)(2,1)S(1)}, bf16[32,512]{1,0:T(8,128)(2,1)S(1)}, u32[]{:S(2)}, u32[]{:S(2)}) collective-permute-start(bf16[32,512]{1,0:T(8,128)(2,1)S(1)} %get-tuple-element.60), channel_id=1, source_target_pairs={{0,24},{2,26},{4,28},{6,30},{8,16},{10,18},{12,20},{14,22},{16,8},... | collective-permute-start | bytes 98312 | tf_op jit(solution)/shard_map/ppermute | solution.py:532
  113.2 0.7 copy-start.6
  113.9 19.6 %copy-start = (bf16[256,1536]{1,0:T(8,128)(2,1)S(1)}, bf16[256,1536]{1,0:T(8,128)(2,1)}, u32[]{:S(2)}) copy-start(bf16[256,1536]{1,0:T(8,128)(2,1)} %get-tuple-element.51.rest_0_) | copy-start | bytes 2359300
  113.9 19.6 %copy-start.2 = (s32[1,256]{1,0:T(1,128)S(1)}, s32[1,256]{1,0:T(1,128)}, u32[]{:S(2)}) copy-start(s32[1,256]{1,0:T(1,128)} %get-tuple-element.31.refs_0_.rep_ref) | copy-start | bytes 3076
  121.4 12.1 %all-to-all-start.3 = ((bf16[16,16,256]{2,1,0:T(8,128)(2,1)}), bf16[16,16,256]{2,1,0:T(8,128)(2,1)S(1)}, u32[]{:S(2)}, u32[]{:S(2)}) async-start(bf16[16,16,256]{2,1,0:T(8,128)(2,1)} %get-tuple-element.49), calls=%async_computation.3 | async-start | bytes 262144 | tf_op jit(solution)/shard_map/all_to_all | solution.py:400
  125.6 7.0 %collective-permute-start.15 = (bf16[128,512]{1,0:T(8,128)(2,1)S(1)}, bf16[128,512]{1,0:T(8,128)(2,1)S(1)}, u32[]{:S(2)}, u32[]{:S(2)}) collective-permute-start(bf16[128,512]{1,0:T(8,128)(2,1)S(1)} %pad_maximum_fusion), channel_id=1, source_target_pairs={{0,4},{2,6},{4,0},{6,2},{8,12},{10,14},{12,8},{14,10},{16,20},{18,... | collective-permute-start | bytes 393224 | tf_op jit(solution)/shard_map/ppermute | solution.py:532
  132.6 4.4 %collective-permute-start.16 = (bf16[256,512]{1,0:T(8,128)(2,1)S(1)}, bf16[256,512]{1,0:T(8,128)(2,1)S(1)}, u32[]{:S(2)}, u32[]{:S(2)}) collective-permute-start(bf16[256,512]{1,0:T(8,128)(2,1)S(1)} %constant_dynamic-update-slice_fusion.own_ref), channel_id=1, source_target_pairs={{0,2},{2,0},{4,6},{6,4},{8,10},{10,8},{12,14},{14,12},{16,18},{18,... | collective-permute-start | bytes 786440 | tf_op jit(solution)/shard_map/ppermute | solution.py:532
  133.5 1.4 %copy-start.1 = (bf16[256,3072]{1,0:T(8,128)(2,1)S(1)}, bf16[256,3072]{1,0:T(8,128)(2,1)}, u32[]{:S(2)}) copy-start(bf16[256,3072]{1,0:T(8,128)(2,1)} %get-tuple-element.50.back_ref) | copy-start | bytes 4718596
  (1 other events, 0.7 us)

commit v4 on v3

--- a/solution.py
+++ b/solution.py
@@ -45,10 +45,6 @@
     return pl.CostEstimate(flops=int(flops), bytes_accessed=int(nbytes), transcendentals=0)
 
 
-def block_of(n):
-    return next(b for b in (512, 256, 128) if n % b == 0)
-
-
 def list_tiles(blocks, count, lists, source_col, trash, low, high):
     tiles, sources, targets = lists
 
@@ -65,6 +61,23 @@
         sources[n + u] = 0
         targets[n + u] = trash
     return n
+
+
+def blocks_of(width, body, size=256):
+    size = size if width % size == 0 else 128
+
+    def step(i, _):
+        body(pl.ds(pl.multiple_of(i * size, size), size))
+        return 0
+
+    lax.fori_loop(0, width // size, step, 0)
+
+
+def clear(acc):
+    def zero(cols):
+        acc[:, cols] = jnp.zeros((acc.shape[0], cols.size), acc.dtype)
+
+    blocks_of(acc.shape[1], zero)
 
 
 def run_tiles(n, lists, values, tile_dim, x_all, acc, tile):
@@ -87,22 +100,27 @@
     return ref[:, pl.ds(at, tile)]
 
 
-def prep_kernel(nf, x_ref, replica, pull_ref, rep_ref, *halves):
+def prep_kernel(nf, x_ref, replica, pull_ref, rep_ref, *rest):
+    halves, total = rest[:nf], rest[nf]
     rep_ref[...] = jnp.concatenate(
         [replica[0, p : p + 1, :] for p in range(replica.shape[1])], axis=1
     )
     h = lax.axis_index("feat")
-    _, masters = x_ref.shape
     width = halves[0].shape[1]
-    step = block_of(masters)
-    total = None
-    for at in range(0, masters, step):
-        part = dot(x_ref[:, at : at + step], picks(rep_ref[...], at, step))
-        total = part if total is None else total + part
-    pull_ref[...] = flip(total.astype(BF)).reshape(pull_ref.shape)
+    total[...] = jnp.zeros_like(total)
+
+    def gather(cols):
+        total[...] += dot(x_ref[:, cols], picks(rep_ref[...], cols.start, cols.size))
+
+    blocks_of(x_ref.shape[1], gather, 512)
+    pull_ref[...] = flip(total[...].astype(BF)).reshape(pull_ref.shape)
     for j in range(nf):
         at = pl.multiple_of(lax.rem(h + j, nf) * width, 128)
-        halves[j][...] = x_ref[:, pl.ds(at, width)]
+
+        def take(cols, j=j, at=at):
+            halves[j][:, cols] = x_ref[:, pl.ds(pl.multiple_of(at + cols.start, 128), cols.size)]
+
+        blocks_of(width, take)
 
 
 def spread_own(tile, blocks, count, x_ref, values_ref, out_ref, acc, x, values, *rest):
@@ -114,12 +132,16 @@
     ]
     for copy in copies:
         copy.start()
-    acc[...] = jnp.zeros_like(acc)
+    clear(acc)
     n = list_tiles(blocks, count[0], lists, 0, acc.shape[1] // tile - 1, 0, masters // tile)
     for copy in copies:
         copy.wait()
     run_tiles(n, lists, values, 0, x, acc, tile)
-    out_ref[...] = acc[:, : out_ref.shape[1]].astype(BF)
+
+    def store(cols):
+        out_ref[:, cols] = acc[:, cols].astype(BF)
+
+    blocks_of(out_ref.shape[1], store)
 
 
 def spread_mirrors(nf, nc, tile, blocks, count, mirrors, values_ref, own_ref, *rest):
@@ -136,7 +158,7 @@
     ]
     for copy in copies:
         copy.start()
-    acc[...] = jnp.zeros_like(acc)
+    clear(acc)
     x[...] = flip(mirrors[...].reshape(slots, feats))
     low = masters // tile
     n = list_tiles(
@@ -150,15 +172,21 @@
         return (own[:, pl.ds(at, size)].astype(F32) + acc[:, pl.ds(at, size)]).astype(BF)
 
     part = width // nc
+
+    def store(ref, at):
+        def block(cols):
+            ref[:, cols] = total(pl.multiple_of(at + cols.start, 128), cols.size)
+
+        blocks_of(ref.shape[1], block)
+
     for j in range(1, nf):
         for c in range(nc):
-            at = pl.multiple_of(lax.rem(h + j, nf) * width + c * part, 128)
-            sends[(j - 1) * nc + c][...] = total(at, part)
+            store(sends[(j - 1) * nc + c], lax.rem(h + j, nf) * width + c * part)
     push = flip(total(masters, slots))
     push = push.reshape(push_ref.shape[0], push_ref.shape[2], feats)
     for f in range(nf):
         push_ref[:, f] = push
-    part_ref[...] = total(pl.multiple_of(h * width, 128), width)
+    store(part_ref, h * width)
 
 
 def dense_kernel(nf, nc, c, *refs):
@@ -170,7 +198,7 @@
         refs = refs[2 + nf :]
     agg_hbm, out_hbm, g_hbm, pay_ref = refs[:4]
     grads, selfs = refs[4 : 4 + nf], refs[4 + nf : 4 + 2 * nf]
-    wt, w, cot, rows, terms, out, g_all, both, in_sems, out_sems = refs[4 + 2 * nf :]
+    wt, w, cot, rows, terms, out, g_all, both, incs, pay, in_sems, out_sems = refs[4 + 2 * nf :]
     h = lax.axis_index("feat")
     feats, part = grads[0].shape
     wide = w.shape[1]
@@ -180,65 +208,72 @@
     def place(f):
         return pl.ds(pl.multiple_of(f * feats, feats), feats)
 
-    early, late = [], []
+    def place_agg(f):
+        return pl.ds(pl.multiple_of(wide + f * feats, feats), feats)
+
+    copies = []
     for j in range(nf):
         f = lax.rem(h - j + nf, nf)
         term = parts[j].at[:, chunk] if j == 0 else parts[j]
-        early.append(pltpu.make_async_copy(term, terms.at[j], in_sems.at[j]))
+        copies.append(pltpu.make_async_copy(term, terms.at[j], in_sems.at[j]))
         x = xs[j].at[:, chunk]
-        early.append(pltpu.make_async_copy(x, rows.at[place(f)], in_sems.at[nf + j]))
-    late.append(pltpu.make_async_copy(wt_hbm, wt, in_sems.at[2 * nf]))
-    late.append(pltpu.make_async_copy(cot_hbm.at[:, chunk], cot, in_sems.at[2 * nf + 1]))
-    late.append(pltpu.make_async_copy(w_hbm, w, in_sems.at[2 * nf + 2]))
-    for copy in early + late:
+        copies.append(pltpu.make_async_copy(x, rows.at[place(f)], in_sems.at[nf + j]))
+    copies.append(pltpu.make_async_copy(wt_hbm, wt, in_sems.at[2 * nf]))
+    copies.append(pltpu.make_async_copy(cot_hbm.at[:, chunk], cot, in_sems.at[2 * nf + 1]))
+    copies.append(pltpu.make_async_copy(w_hbm, w, in_sems.at[2 * nf + 2]))
+    for copy in copies:
         copy.start()
-    pick = picks(rep_ref[...], (h * nc + c) * part, part)
-    incs = [flip(inc_ref[:, lax.rem(h - j + nf, nf)].reshape(slots, feats)) for j in range(nf)]
-    adds = [dot(inc, pick, 1, 1) for inc in incs]
-    for copy in early:
+    for j in range(nf):
+        incs[j] = flip(inc_ref[:, lax.rem(h - j + nf, nf)].reshape(slots, feats))
+    pay[...] = pay_in[...].astype(F32) if c else jnp.zeros_like(pay)
+    for copy in copies:
         copy.wait()
-    for j in range(nf):
-        f = lax.rem(h - j + nf, nf)
-        total = terms[j].astype(F32) + adds[j]
-        rows[pl.ds(pl.multiple_of(wide + f * feats, feats), feats), :] = total.astype(BF)
-    out_copies = []
-
-    def put(src, dst):
-        copy = pltpu.make_async_copy(src, dst, out_sems.at[len(out_copies)])
-        copy.start()
-        out_copies.append(copy)
-
-    put(rows.at[wide:], agg_hbm)
-    for copy in late:
-        copy.wait()
-    step = 256 if part % 256 == 0 else 128
-    for b in range(0, part, step):
-        cols = slice(b, b + step)
+    size = 256 if part % 256 == 0 else 128
+
+    def outputs(b, at):
+        cols = pl.ds(at, size)
+        whole = pl.ds(pl.multiple_of(c * part + at, 128), size)
+        pairs = [
+            (rows.at[wide:, cols], agg_hbm.at[:, cols]),
+            (g_all.at[:, cols], g_hbm.at[:, cols]),
+            (out.at[:, cols], out_hbm.at[:, whole]),
+        ]
+        for j in range(nf):
+            f = lax.rem(h + j, nf)
+            pairs.append((both.at[place_agg(f), cols], grads[j].at[:, cols]))
+            pairs.append((both.at[place(f), cols], selfs[j].at[:, whole]))
+        return [
+            pltpu.make_async_copy(a, o, out_sems.at[k, b]) for k, (a, o) in enumerate(pairs)
+        ]
+
+    def step(b, _):
+        at = pl.multiple_of(b * size, size)
+        cols = pl.ds(at, size)
+        pick = picks(rep_ref[...], (h * nc + c) * part + at, size)
+        for j in range(nf):
+            total = terms[j, :, cols].astype(F32) + dot(incs[j], pick, 1, 1)
+            rows[place_agg(lax.rem(h - j + nf, nf)), cols] = total.astype(BF)
         z = dot(wt[...], rows[:, cols])
         s = 0.5 + 0.5 * jnp.tanh(0.5 * z)
         out[:, cols] = (z * s).astype(BF)
         g = (cot[:, cols].astype(F32) * (s * (1.0 + z * (1.0 - s)))).astype(BF)
         g_all[:, cols] = g
         both[:, cols] = dot(w[...], g).astype(BF)
-        for j in range(nf):
-            at = lax.rem(h + j, nf)
-            peer = pl.ds(pl.multiple_of(wide + at * feats, feats), feats)
-            put(both.at[peer, cols], grads[j].at[:, cols])
-            put(both.at[place(at), cols], selfs[j].at[:, pl.ds(c * part + b, step)])
-        put(g_all.at[:, cols], g_hbm.at[:, cols])
-        put(out.at[:, cols], out_hbm.at[:, pl.ds(c * part + b, step)])
-    pay = dot(both[wide:, :], pick)
-    if c:
-        pay = pay + pay_in[...].astype(F32)
-    pay = pay.astype(BF)
+        for copy in outputs(b, at):
+            copy.start()
+        pay[...] += dot(both[wide:, cols], pick)
+        return 0
+
+    lax.fori_loop(0, part // size, step, 0)
     if c + 1 < nc:
-        pay_ref[...] = pay
+        pay_ref[...] = pay[...].astype(BF)
     else:
         for f in range(nf):
-            mine = flip(pay[f * feats : (f + 1) * feats])
+            mine = flip(pay[f * feats : (f + 1) * feats].astype(BF))
             pay_ref[:, f] = mine.reshape(pay_ref.shape[0], pay_ref.shape[2], feats)
-    for copy in out_copies:
-        copy.wait()
+    for b in range(part // size):
+        for copy in outputs(b, b * size):
+            copy.wait()
 
 
 def weight_kernel(nf, nc, *refs):
@@ -257,20 +292,45 @@
             copies[k].start()
     xs, aggs, grads = held[:nf], held[nf : nf + nc], held[nf + nc :]
     part = grads[0].shape[1]
+    size = min(256, feats)
     for c in range(nc):
         for k in order[c]:
             copies[k].wait()
-        terms = [(pl.ds(wide, wide), aggs[c][...])]
+
+        def add(at, left, c=c):
+            term = dot(left, grads[c][...], 1, 1)
+            acc[at, :] = term if c == 0 else acc[at, :] + term
+
+        def step(i, _, c=c):
+            at = pl.multiple_of(i * size, size)
+            add(pl.ds(wide + at, size), aggs[c][pl.ds(at, size), :])
+            return 0
+
+        lax.fori_loop(0, wide // size, step, 0)
         for j in range(nf):
             at = pl.multiple_of(lax.rem(h - j + nf, nf) * feats, feats)
-            terms.append((pl.ds(at, feats), xs[j][:, c * part : (c + 1) * part]))
-        for at, left in terms:
-            term = dot(left, grads[c][...], 1, 1)
-            acc[at, :] = term if c == 0 else acc[at, :] + term
+            add(pl.ds(at, feats), xs[j][:, c * part : (c + 1) * part])
     for j in range(nf):
         at = lax.rem(h + j, nf) * feats
         keep_ref[j] = acc[pl.ds(pl.multiple_of(bit * wide + at, feats), feats), :]
         send_ref[j] = acc[pl.ds(pl.multiple_of((1 - bit) * wide + at, feats), feats), :].astype(BF)
+
+
+def combine_kernel(nf, radix, digit, keep_ref, *rest):
+    recvs, out_ref, sends = rest[: -radix], rest[-radix], rest[-radix + 1 :]
+    unit, base = digit
+    mine = lax.rem(lax.axis_index("dom") // unit, base)
+    size = out_ref.shape[1]
+    for j in range(nf):
+        for m in range(radix):
+            at = pl.ds(pl.multiple_of(jnp.bitwise_xor(mine, m) * size, size), size)
+            total = keep_ref[j, at, :]
+            for recv in recvs:
+                total = total + recv[j, at, :].astype(F32)
+            if m == 0:
+                out_ref[j] = total
+            else:
+                sends[m - 1][j] = total.astype(BF)
 
 
 def radices_of(n):
@@ -334,7 +394,7 @@
             )
     for copy in copies:
         copy.start()
-    acc[...] = jnp.zeros_like(acc)
+    clear(acc)
     total = mirrors[:, 0].astype(F32)
     for f in range(1, nf):
         total = total + mirrors[:, f].astype(F32)
@@ -345,23 +405,30 @@
     run_tiles(count[0], lists, values, 1, x_all, acc, tile)
     partial = acc[:, masters : masters + slots].astype(BF)
     push_ref[...] = flip(partial).reshape(push_ref.shape)
-    back_ref[...] = acc[:, :masters].astype(BF)
-
-
-def final_kernel(nf, nc, rep_ref, inc_ref, back_ref, *rest):
+
+    def store(cols):
+        back_ref[:, cols] = acc[:, cols].astype(BF)
+
+    blocks_of(masters, store)
+
+
+def final_kernel(nf, rep_ref, inc_ref, back_ref, *rest):
     selfs, out_ref = rest[:nf], rest[nf]
     h = lax.axis_index("feat")
     feats, width = selfs[0].shape
-    part = width // nc
     slots = rep_ref.shape[1]
     inc = flip(inc_ref[...].reshape(slots, feats))
     for j in range(nf):
-        for c in range(nc):
-            at = pl.multiple_of((lax.rem(h - j + nf, nf) * nc + c) * part, 128)
-            back = back_ref[:, pl.ds(at, part)].astype(F32)
-            back = back + dot(inc, picks(rep_ref[...], at, part), 1, 1)
-            own = selfs[j][:, c * part : (c + 1) * part].astype(F32)
-            out_ref[:, pl.ds(at, part)] = (own + back).astype(BF)
+        start = lax.rem(h - j + nf, nf) * width
+
+        def block(cols, j=j, start=start):
+            at = pl.multiple_of(start + cols.start, 128)
+            here = pl.ds(at, cols.size)
+            back = back_ref[:, here].astype(F32)
+            back = back + dot(inc, picks(rep_ref[...], at, cols.size), 1, 1)
+            out_ref[:, here] = (selfs[j][:, cols].astype(F32) + back).astype(BF)
+
+        blocks_of(width, block)
 
 
 def local(nd, nf, features, weights, tile_values, tile_blocks, tile_counts, replica, cotangent):
@@ -415,6 +482,7 @@
         [features, replica],
         [None] * 2,
         [sd((nd, per, feats), BF), sd((1, slots), jnp.int32)] + [vec] * nf,
+        [pltpu.VMEM((feats, slots), F32)],
     )
     mirrors = exchange(pull, "dom")
     x_parts = [x_halves[0]] + [to_peer(x_halves[j], j) for j in range(1, nf)]
@@ -488,8 +556,10 @@
                 pltpu.VMEM((wide, part), BF),
                 pltpu.VMEM((wide, part), BF),
                 pltpu.VMEM((2 * wide, part), BF),
+                pltpu.VMEM((nf, feats, slots), BF),
+                pltpu.VMEM((wide, slots), F32),
                 pltpu.SemaphoreType.DMA((2 * nf + 3,)),
-                pltpu.SemaphoreType.DMA((1 + (part // step) * (2 * nf + 2),)),
+                pltpu.SemaphoreType.DMA((2 * nf + 3, part // step)),
             ],
             (),
             [ANY] * 3 + [full(outs[3])] + [ANY] * (2 * nf),
@@ -534,9 +604,21 @@
     sends = [send]
     for k, r in enumerate(radices):
         unit = unit_of(radices, k)
+        recvs = [swap(sends[m - 1], m * unit) for m in range(1, r)]
+        if k + 1 < len(radices) and keep.shape[1] // radices[k + 1] % 16 == 0:
+            size = keep.shape[1] // radices[k + 1]
+            digit = unit_of(radices, k + 1), radices[k + 1]
+            keep, *sends = call(
+                functools.partial(combine_kernel, nf, radices[k + 1], digit),
+                0,
+                [keep, *recvs],
+                [None] * r,
+                [sd((nf, size, wide), F32)] + [sd((nf, size, wide), BF)] * (radices[k + 1] - 1),
+            )
+            continue
         cur = keep
-        for m in range(1, r):
-            cur = cur + swap(sends[m - 1], m * unit).astype(F32)
+        for recv in recvs:
+            cur = cur + recv.astype(F32)
         if k + 1 == len(radices):
             break
         size = cur.shape[1] // radices[k + 1]
@@ -577,7 +659,7 @@
     weight_grad = weight_grad.reshape(2, feats, wide)
 
     (feature_grad,) = call(
-        functools.partial(final_kernel, nf, nc),
+        functools.partial(final_kernel, nf),
         2 * slots * feats * masters,
         [rep, back_in, back, *selfs],
         [None] * (3 + nf),

time: 139 us -> 159 us (1.14)
  Pallas kernels: 47.1 us -> 61.1 us
  waiting for transfers between devices: 40.6 us -> 46.1 us
    pallas_call x9 -> x11, Pallas kernels: 47.1 us -> 61.1 us  [call(): pl.pallas_call(body, grid=grid, in_specs=[full(a) if p is None else p for...]
    ppermute x7, waiting for transfers between devices: 25.4 us -> 30.7 us  [to_peer(): return lax.ppermute(x, 'feat', [(i, (i + j) % nf) for i in range(nf)])]
    unnamed x27 -> x33, local copies, waits for them, and re-layouts: 4.62 us -> 6.09 us
  transfers between devices with their start and end apart: 21 -> 21, of which waited for: 7 -> 7; matrix products, arithmetic and copies ran while one was open for 1% -> 1% of each run, Pallas kernels for 21% -> 22%
where the time goes in v4:
time: 159 us; the launch traced here: 158 us
  Pallas kernels  61.1 us (38%)
  waiting for transfers between devices  46.1 us (29%)
  starting transfers between devices  40.9 us (26%)
  local copies, waits for them, and re-layouts  7.41 us (5%)
    pallas_call x11, Pallas kernels, call(): pl.pallas_call(body, grid=grid, in_specs=[full(a) if p is None else p for...  61.1 us
    ppermute x7, waiting for transfers between devices, to_peer(): return lax.ppermute(x, 'feat', [(i, (i + j) % nf) for i in range(nf)])  30.7 us
    all_to_all x4, starting transfers between devices, exchange(): return lax.all_to_all(flat, axes, 0, 0, tiled=True).reshape(x.shape)  19.4 us
    ppermute x10, waiting for transfers between devices, swap(): return lax.ppermute(x, 'dom', [(i, i ^ b) for i in range(nd)])  14.4 us
    ppermute x10, starting transfers between devices, swap(): return lax.ppermute(x, 'dom', [(i, i ^ b) for i in range(nd)])  12.2 us
    ppermute x7, starting transfers between devices, to_peer(): return lax.ppermute(x, 'feat', [(i, (i + j) % nf) for i in range(nf)])  9.27 us
    unnamed x33, local copies, waits for them, and re-layouts  6.09 us
  transfers between devices with their start and end apart: 21, of which 7 were waited for; matrix products, arithmetic and copies ran while one was open for 1% of the time, Pallas kernels for 22%

profile of v4, /device:TPU:0, one launch (start us, length us, event | category | flops | bytes accessed | tf_op | source)
XLA Modules:
  0.0 158.0 jit_solution(410698961120656236)
XLA Ops:
  0.6 4.5 %shard_map.94 = (bf16[16,16,256]{2,1,0:T(8,128)(2,1)}, s32[1,256]{1,0:T(1,128)}, bf16[256,1536]{1,0:T(8,128)(2,1)}, bf16[256,1536]{1,0:T(8,128)(2,1)}) custom-call(bf16[256,3072]{1,0:T(8,128)(2,1)} %x_ref.3, s32[1,16,16]{2,1,0:T(8,128)} %replica.1), custom_call_target="tpu_custom_call" | custom-call | flops 402653184 | bytes 1573376 | tf_op jit(solution)/shard_map/pallas_call | solution.py:450
  5.2 3.0 %collective-permute-start = (bf16[256,1536]{1,0:T(8,128)(2,1)}, bf16[256,1536]{1,0:T(8,128)(2,1)S(1)}, u32[]{:S(2)}, u32[]{:S(2)}) collective-permute-start(bf16[256,1536]{1,0:T(8,128)(2,1)} %get-tuple-element.41), channel_id=1, source_target_pairs={{0,1},{1,0},{2,3},{3,2},{4,5},{5,4},{6,7},{7,6},{8,9},{9,8},{10,11... | collective-permute-start | bytes 2359304 | tf_op jit(solution)/shard_map/ppermute | solution.py:463
  8.2 5.9 %all-to-all-start = ((bf16[16,16,256]{2,1,0:T(8,128)(2,1)}), bf16[16,16,256]{2,1,0:T(8,128)(2,1)S(1)}, u32[]{:S(2)}, u32[]{:S(2)}) async-start(bf16[16,16,256]{2,1,0:T(8,128)(2,1)} %get-tuple-element.38), calls=%async_computation | async-start | bytes 262144 | tf_op jit(solution)/shard_map/all_to_all | solution.py:467
  14.7 7.1 %shard_map.95.own_ref = bf16[256,3328]{1,0:T(8,128)(2,1)} custom-call(s32[2,72]{1,0:T(2,128)} %bitcast.26, s32[1]{0:T(128)S(6)} %copy.22.count, bf16[256,3072]{1,0:T(8,128)(2,1)} %x_ref.3, bf16[72,128,128]{2,1,0:T(8,128)(2,1)} %values_ref.5), custom_call_target="tpu_custom_call" | custom-call | flops 603979776 | bytes 3932450 | tf_op jit(solution)/shard_map/pallas_call | solution.py:450
  22.7 5.3 %shard_map.96 = (bf16[256,1536]{1,0:T(8,128)(2,1)}, bf16[16,2,16,256]{3,2,1,0:T(8,128)(2,1)}, bf16[256,768]{1,0:T(8,128)(2,1)}, bf16[256,768]{1,0:T(8,128)(2,1)}) custom-call(s32[2,72]{1,0:T(2,128)} %bitcast.27, s32[1]{0:T(128)S(6)} %copy.22.count, bf16[16,16,256]{2,1,0:T(8,128)(2,1)} %copy-done.9, bf16[72,128,128]{2,1,0:T(8,128)(2,1)} %values_ref.5, ...), custom_call_target="tpu_custom_call" | custom-call | flops 150994944 | bytes 4194594 | tf_op jit(solution)/shard_map/pallas_call | solution.py:450
  27.9 4.6 %all-to-all-start.1 = ((bf16[32,16,256]{2,1,0:T(8,128)(2,1)}), bf16[32,16,256]{2,1,0:T(8,128)(2,1)S(1)}, u32[]{:S(2)}, u32[]{:S(2)}) async-start(bf16[32,16,256]{2,1,0:T(8,128)(2,1)} %bitcast.25), calls=%async_computation.1 | async-start | bytes 524288 | tf_op jit(solution)/shard_map/all_to_all | solution.py:467
  32.5 1.8 %collective-permute-start.2 = (bf16[256,768]{1,0:T(8,128)(2,1)}, bf16[256,768]{1,0:T(8,128)(2,1)S(1)}, u32[]{:S(2)}, u32[]{:S(2)}) collective-permute-start(bf16[256,768]{1,0:T(8,128)(2,1)} %get-tuple-element.44), channel_id=1, source_target_pairs={{0,1},{1,0},{2,3},{3,2},{4,5},{5,4},{6,7},{7,6},{8,9},{9,8},{10,11... | collective-permute-start | bytes 1179656 | tf_op jit(solution)/shard_map/ppermute | solution.py:463
  34.6 1.3 copy.14.refs_2_
  35.9 11.3 %collective-permute-done.2.refs_8_ = bf16[256,768]{1,0:T(8,128)(2,1)S(1)} collective-permute-done((bf16[256,768]{1,0:T(8,128)(2,1)}, bf16[256,768]{1,0:T(8,128)(2,1)S(1)}, u32[]{:S(2)}, u32[]{:S(2)}) %collective-permute-start.2) | collective-permute-done | bytes 393248 | tf_op jit(solution)/shard_map/ppermute | solution.py:463
  48.3 10.5 %shard_map.97 = (bf16[512,768]{1,0:T(8,128)(2,1)}, bf16[512,1536]{1,0:T(8,128)(2,1)}, bf16[512,768]{1,0:T(8,128)(2,1)}, bf16[512,256]{1,0:T(8,128)(2,1)}, bf16[2...) custom-call(s32[1,256]{1,0:T(1,128)} %get-tuple-element.37.refs_0_.rep_ref, ...), custom_call_target="tpu_custom_call" | custom-call | flops 1610612736 | bytes 6685184 | tf_op jit(solution)/shard_map/pallas_call | solution.py:450
  59.6 10.6 %shard_map.98 = (bf16[512,768]{1,0:T(8,128)(2,1)}, bf16[512,1536]{1,0:T(8,128)(2,1)}, bf16[512,768]{1,0:T(8,128)(2,1)}, bf16[16,2,16,256]{3,2,1,0:T(8,128)(2,1)}...) custom-call(s32[1,256]{1,0:T(1,128)} %get-tuple-element.37.refs_0_.r, ...), custom_call_target="tpu_custom_call", output_to_operand_aliasing={{1}: (10, {}), {6}: (11, {}), {7}: (12, {})} | custom-call | flops 1610612736 | bytes 10093056 | tf_op jit(solution)/shard_map/pallas_call | solution.py:450
  70.1 6.0 %shard_map.101 = (f32[2,256,512]{2,1,0:T(8,128)}, bf16[2,256,512]{2,1,0:T(8,128)(2,1)}) custom-call(bf16[256,1536]{1,0:T(8,128)(2,1)} %get-tuple-element.40.refs_5_.refs_0_, bf16[256,1536]{1,0:T(8,128)(2,1)} %copy-done.4, bf16[512,768]{1,0:T(8,128)(2,1)} %get-tuple-element.59.refs_2_, bf16[512,768]{1,0:T(8,128)(2,1)} %get-tuple-element.60.refs_3_, ...), custom_call_target="tpu_custom_call" | custom-call | flops 1610612736 | bytes 4718592 | tf_op jit(solution)/shard_map/pallas_call | solution.py:450
  76.2 2.1 %collective-permute-done.6.rest_0_ = bf16[2,256,512]{2,1,0:T(8,128)(2,1)S(1)} collective-permute-done((bf16[2,256,512]{2,1,0:T(8,128)(2,1)}, bf16[2,256,512]{2,1,0:T(8,128)(2,1)S(1)}, u32[]{:S(2)}, u32[]{:S(2)}) %collective-permute-start.6) | collective-permute-done | bytes 524320 | tf_op jit(solution)/shard_map/ppermute | solution.py:602
  79.1 2.4 %shard_map.102 = (f32[2,128,512]{2,1,0:T(8,128)}, bf16[2,128,512]{2,1,0:T(8,128)(2,1)}) custom-call(f32[2,256,512]{2,1,0:T(8,128)} %get-tuple-element.63.keep_ref, bf16[2,256,512]{2,1,0:T(8,128)(2,1)} %copy-done.8), custom_call_target="tpu_custom_call" | custom-call | bytes 1048576 | tf_op jit(solution)/shard_map/pallas_call | solution.py:450
  81.5 1.2 collective-permute-start.7
  82.7 7.3 %collective-permute-done.7.rest_0_ = bf16[2,128,512]{2,1,0:T(8,128)(2,1)S(1)} collective-permute-done((bf16[2,128,512]{2,1,0:T(8,128)(2,1)}, bf16[2,128,512]{2,1,0:T(8,128)(2,1)S(1)}, u32[]{:S(2)}, u32[]{:S(2)}) %collective-permute-start.7) | collective-permute-done | bytes 262176 | tf_op jit(solution)/shard_map/ppermute | solution.py:602
  90.8 1.8 %shard_map.103 = (f32[2,32,512]{2,1,0:T(8,128)}, bf16[2,32,512]{2,1,0:T(8,128)(2,1)}, bf16[2,32,512]{2,1,0:T(8,128)(2,1)}, bf16[2,32,512]{2,1,0:T(8,128)(2,1)}) custom-call(f32[2,128,512]{2,1,0:T(8,128)} %get-tuple-element.65.keep_ref, bf16[2,128,512]{2,1,0:T(8,128)(2,1)} %copy-done.13), custom_call_target="tpu_custom_call" | custom-call | bytes 524288 | tf_op jit(solution)/shard_map/pallas_call | solution.py:450
  92.6 1.5 collective-permute-start.8
  94.1 2.3 %collective-permute-start.9 = (bf16[2,32,512]{2,1,0:T(8,128)(2,1)}, bf16[2,32,512]{2,1,0:T(8,128)(2,1)S(1)}, u32[]{:S(2)}, u32[]{:S(2)}) collective-permute-start(bf16[2,32,512]{2,1,0:T(8,128)(2,1)} %get-tuple-element.69), channel_id=1, source_target_pairs={{0,16},{2,18},{4,20},{6,22},{8,24},{10,26},{12,28},{14,30},{16,0},... | collective-permute-start | bytes 196616 | tf_op jit(solution)/shard_map/ppermute | solution.py:602
  97.0 4.2 %all-to-all-start.2 = ((bf16[32,16,256]{2,1,0:T(8,128)(2,1)}), bf16[32,16,256]{2,1,0:T(8,128)(2,1)S(1)}, u32[]{:S(2)}, u32[]{:S(2)}) async-start(bf16[32,16,256]{2,1,0:T(8,128)(2,1)} %bitcast.5), calls=%async_computation.2 | async-start | bytes 524288 | tf_op jit(solution)/shard_map/all_to_all | solution.py:467
  101.2 1.8 %collective-permute-start.4 = (bf16[256,768]{1,0:T(8,128)(2,1)}, bf16[256,768]{1,0:T(8,128)(2,1)S(1)}, u32[]{:S(2)}, u32[]{:S(2)}) collective-permute-start(bf16[256,768]{1,0:T(8,128)(2,1)} %get-tuple-element.54), channel_id=1, source_target_pairs={{0,1},{1,0},{2,3},{3,2},{4,5},{5,4},{6,7},{7,6},{8,9},{9,8},{10,11... | collective-permute-start | bytes 1179656 | tf_op jit(solution)/shard_map/ppermute | solution.py:463
  104.2 1.8 %collective-permute-start.11 = (f32[32,512]{1,0:T(8,128)S(1)}, f32[32,512]{1,0:T(8,128)S(1)}, u32[]{:S(2)}, u32[]{:S(2)}) collective-permute-start(f32[32,512]{1,0:T(8,128)S(1)} %slice_bitcast_fusion), channel_id=1, source_target_pairs={{0,1},{1,0},{2,3},{3,2},{4,5},{5,4},{6,7},{7,6},{8,9},{9,8},{10,11... | collective-permute-start | bytes 196616 | tf_op jit(solution)/shard_map/ppermute | solution.py:463
  106.3 19.4 %collective-permute-done.11 = f32[32,512]{1,0:T(8,128)S(1)} collective-permute-done((f32[32,512]{1,0:T(8,128)S(1)}, f32[32,512]{1,0:T(8,128)S(1)}, u32[]{:S(2)}, u32[]{:S(2)}) %collective-permute-start.11) | collective-permute-done | bytes 65568 | tf_op jit(solution)/shard_map/ppermute | solution.py:463
  125.7 3.4 %collective-permute-start.14 = (bf16[32,512]{1,0:T(8,128)(2,1)S(1)}, bf16[32,512]{1,0:T(8,128)(2,1)S(1)}, u32[]{:S(2)}, u32[]{:S(2)}) collective-permute-start(bf16[32,512]{1,0:T(8,128)(2,1)S(1)} %get-tuple-element.72), channel_id=1, source_target_pairs={{0,24},{2,26},{4,28},{6,30},{8,16},{10,18},{12,20},{14,22},{16,8},... | collective-permute-start | bytes 98312 | tf_op jit(solution)/shard_map/ppermute | solution.py:602
  129.1 1.1 collective-permute-start.12
  130.9 7.6 %shard_map.99 = (bf16[256,3072]{1,0:T(8,128)(2,1)}, bf16[16,16,256]{2,1,0:T(8,128)(2,1)}) custom-call(s32[2,72]{1,0:T(2,128)} %bitcast.28, s32[1]{0:T(128)S(6)} %copy.22.count, bf16[16,2,16,256]{3,2,1,0:T(8,128)(2,1)} %bitcast.23, bf16[72,128,128]{2,1,0:T(8,128)(2,1)} %values_ref.5, bf16[256,768]{1,0:T(8,128)(2,1)} %get-tuple-element.51.rest_0_, ...), custom_call_target="tpu_custom_call" | custom-call | flops 603979776 | bytes 4194594 | tf_op jit(solution)/shard_map/pallas_call | solution.py:450
  138.5 4.8 %all-to-all-start.3 = ((bf16[16,16,256]{2,1,0:T(8,128)(2,1)}), bf16[16,16,256]{2,1,0:T(8,128)(2,1)S(1)}, u32[]{:S(2)}, u32[]{:S(2)}) async-start(bf16[16,16,256]{2,1,0:T(8,128)(2,1)} %get-tuple-element.55), calls=%async_computation.3 | async-start | bytes 262144 | tf_op jit(solution)/shard_map/all_to_all | solution.py:467
  143.3 2.0 %collective-permute-start.15 = (bf16[128,512]{1,0:T(8,128)(2,1)S(1)}, bf16[128,512]{1,0:T(8,128)(2,1)S(1)}, u32[]{:S(2)}, u32[]{:S(2)}) collective-permute-start(bf16[128,512]{1,0:T(8,128)(2,1)S(1)} %pad_maximum_fusion), channel_id=1, source_target_pairs={{0,4},{2,6},{4,0},{6,2},{8,12},{10,14},{12,8},{14,10},{16,20},{18,... | collective-permute-start | bytes 393224 | tf_op jit(solution)/shard_map/ppermute | solution.py:602
  145.3 5.0 %collective-permute-done.15 = bf16[128,512]{1,0:T(8,128)(2,1)S(1)} collective-permute-done((bf16[128,512]{1,0:T(8,128)(2,1)S(1)}, bf16[128,512]{1,0:T(8,128)(2,1)S(1)}, u32[]{:S(2)}, u32[]{:S(2)}) %collective-permute-start.15) | collective-permute-done | bytes 131104 | tf_op jit(solution)/shard_map/ppermute | solution.py:602
  151.2 1.4 copy-done.1
  152.6 4.2 %shard_map.100 = bf16[256,3072]{1,0:T(8,128)(2,1)} custom-call(s32[1,256]{1,0:T(1,128)S(1)} %copy-done.2, bf16[16,16,256]{2,1,0:T(8,128)(2,1)S(1)} %all-to-all-done.3.inc_ref, bf16[256,3072]{1,0:T(8,128)(2,1)S(1)} %copy-done.1, bf16[256,1536]{1,0:T(8,128)(2,1)S(1)} %copy-done, bf16[256,1536]{1,0:T(8,128)(2,1)S(1)} %collective-permute-done.5.rest_1_), custom_call_target="tpu_custom_call" | custom-call | flops 402653184 | bytes 3277312 | tf_op jit(solution)/shard_map/pallas_call | solution.py:450
  156.8 1.2 shard_map.104
  (60 shorter events, 8.1 us)
Async XLA Ops:
  5.2 42.0 %collective-permute-start = (bf16[256,1536]{1,0:T(8,128)(2,1)}, bf16[256,1536]{1,0:T(8,128)(2,1)S(1)}, u32[]{:S(2)}, u32[]{:S(2)}) collective-permute-start(bf16[256,1536]{1,0:T(8,128)(2,1)} %get-tuple-element.41), channel_id=1, source_target_pairs={{0,1},{1,0},{2,3},{3,2},{4,5},{5,4},{6,7},{7,6},{8,9},{9,8},{10,11... | collective-permute-start | bytes 2359304 | tf_op jit(solution)/shard_map/ppermute | solution.py:463
  8.2 13.8 %all-to-all-start = ((bf16[16,16,256]{2,1,0:T(8,128)(2,1)}), bf16[16,16,256]{2,1,0:T(8,128)(2,1)S(1)}, u32[]{:S(2)}, u32[]{:S(2)}) async-start(bf16[16,16,256]{2,1,0:T(8,128)(2,1)} %get-tuple-element.38), calls=%async_computation | async-start | bytes 262144 | tf_op jit(solution)/shard_map/all_to_all | solution.py:467
  21.8 12.8 %copy-start.3 = (bf16[2,512,512]{2,1,0:T(8,128)(2,1)S(1)}, bf16[2,512,512]{2,1,0:T(8,128)(2,1)}, u32[]{:S(2)}) copy-start(bf16[2,512,512]{2,1,0:T(8,128)(2,1)} %param.8) | copy-start | bytes 3145732
  27.9 19.3 %all-to-all-start.1 = ((bf16[32,16,256]{2,1,0:T(8,128)(2,1)}), bf16[32,16,256]{2,1,0:T(8,128)(2,1)S(1)}, u32[]{:S(2)}, u32[]{:S(2)}) async-start(bf16[32,16,256]{2,1,0:T(8,128)(2,1)} %bitcast.25), calls=%async_computation.1 | async-start | bytes 524288 | tf_op jit(solution)/shard_map/all_to_all | solution.py:467
  32.5 14.7 %collective-permute-start.2 = (bf16[256,768]{1,0:T(8,128)(2,1)}, bf16[256,768]{1,0:T(8,128)(2,1)S(1)}, u32[]{:S(2)}, u32[]{:S(2)}) collective-permute-start(bf16[256,768]{1,0:T(8,128)(2,1)} %get-tuple-element.44), channel_id=1, source_target_pairs={{0,1},{1,0},{2,3},{3,2},{4,5},{5,4},{6,7},{7,6},{8,9},{9,8},{10,11... | collective-permute-start | bytes 1179656 | tf_op jit(solution)/shard_map/ppermute | solution.py:463
  34.3 24.5 %collective-permute-start.1 = (bf16[256,768]{1,0:T(8,128)(2,1)}, bf16[256,768]{1,0:T(8,128)(2,1)S(1)}, u32[]{:S(2)}, u32[]{:S(2)}) collective-permute-start(bf16[256,768]{1,0:T(8,128)(2,1)} %get-tuple-element.43), channel_id=1, source_target_pairs={{0,1},{1,0},{2,3},{3,2},{4,5},{5,4},{6,7},{7,6},{8,9},{9,8},{10,11... | collective-permute-start | bytes 1179656 | tf_op jit(solution)/shard_map/ppermute | solution.py:463
  47.2 0.8 copy-start.5
  47.2 1.1 copy-start.4
  58.8 0.7 copy-start.12
  76.1 26.9 %copy-start.14 = (bf16[256,768]{1,0:T(8,128)(2,1)S(1)}, bf16[256,768]{1,0:T(8,128)(2,1)}, u32[]{:S(2)}) copy-start(bf16[256,768]{1,0:T(8,128)(2,1)} %get-tuple-element.53) | copy-start | bytes 1179652
  76.1 2.2 %collective-permute-start.6 = (bf16[2,256,512]{2,1,0:T(8,128)(2,1)}, bf16[2,256,512]{2,1,0:T(8,128)(2,1)S(1)}, u32[]{:S(2)}, u32[]{:S(2)}) collective-permute-start(bf16[2,256,512]{2,1,0:T(8,128)(2,1)} %get-tuple-element.64), channel_id=1, source_target_pairs={{0,2},{2,0},{4,6},{6,4},{8,10},{10,8},{12,14},{14,12},{16,18},{18,... | collective-permute-start | bytes 1572872 | tf_op jit(solution)/shard_map/ppermute | solution.py:602
  78.3 0.8 copy-start.8
  79.1 27.0 %copy-start.7 = (bf16[256,1536]{1,0:T(8,128)(2,1)S(1)}, bf16[256,1536]{1,0:T(8,128)(2,1)}, u32[]{:S(2)}) copy-start(bf16[256,1536]{1,0:T(8,128)(2,1)} %get-tuple-element.58) | copy-start | bytes 2359300
  81.5 8.6 %collective-permute-start.7 = (bf16[2,128,512]{2,1,0:T(8,128)(2,1)}, bf16[2,128,512]{2,1,0:T(8,128)(2,1)S(1)}, u32[]{:S(2)}, u32[]{:S(2)}) collective-permute-start(bf16[2,128,512]{2,1,0:T(8,128)(2,1)} %get-tuple-element.66), channel_id=1, source_target_pairs={{0,4},{2,6},{4,0},{6,2},{8,12},{10,14},{12,8},{14,10},{16,20},{18,... | collective-permute-start | bytes 786440 | tf_op jit(solution)/shard_map/ppermute | solution.py:602
  92.6 10.7 %collective-permute-start.8 = (bf16[2,32,512]{2,1,0:T(8,128)(2,1)}, bf16[2,32,512]{2,1,0:T(8,128)(2,1)S(1)}, u32[]{:S(2)}, u32[]{:S(2)}) collective-permute-start(bf16[2,32,512]{2,1,0:T(8,128)(2,1)} %get-tuple-element.68), channel_id=1, source_target_pairs={{0,8},{2,10},{4,12},{6,14},{8,0},{10,2},{12,4},{14,6},{16,24},{18,... | collective-permute-start | bytes 196616 | tf_op jit(solution)/shard_map/ppermute | solution.py:602
  94.1 9.1 %collective-permute-start.9 = (bf16[2,32,512]{2,1,0:T(8,128)(2,1)}, bf16[2,32,512]{2,1,0:T(8,128)(2,1)S(1)}, u32[]{:S(2)}, u32[]{:S(2)}) collective-permute-start(bf16[2,32,512]{2,1,0:T(8,128)(2,1)} %get-tuple-element.69), channel_id=1, source_target_pairs={{0,16},{2,18},{4,20},{6,22},{8,24},{10,26},{12,28},{14,30},{16,0},... | collective-permute-start | bytes 196616 | tf_op jit(solution)/shard_map/ppermute | solution.py:602
  96.5 6.8 %collective-permute-start.10 = (bf16[2,32,512]{2,1,0:T(8,128)(2,1)}, bf16[2,32,512]{2,1,0:T(8,128)(2,1)S(1)}, u32[]{:S(2)}, u32[]{:S(2)}) collective-permute-start(bf16[2,32,512]{2,1,0:T(8,128)(2,1)} %get-tuple-element.70), channel_id=1, source_target_pairs={{0,24},{2,26},{4,28},{6,30},{8,16},{10,18},{12,20},{14,22},{16,8},... | collective-permute-start | bytes 196616 | tf_op jit(solution)/shard_map/ppermute | solution.py:602
  97.0 33.2 %all-to-all-start.2 = ((bf16[32,16,256]{2,1,0:T(8,128)(2,1)}), bf16[32,16,256]{2,1,0:T(8,128)(2,1)S(1)}, u32[]{:S(2)}, u32[]{:S(2)}) async-start(bf16[32,16,256]{2,1,0:T(8,128)(2,1)} %bitcast.5), calls=%async_computation.2 | async-start | bytes 524288 | tf_op jit(solution)/shard_map/all_to_all | solution.py:467
  101.2 27.9 %collective-permute-start.4 = (bf16[256,768]{1,0:T(8,128)(2,1)}, bf16[256,768]{1,0:T(8,128)(2,1)S(1)}, u32[]{:S(2)}, u32[]{:S(2)}) collective-permute-start(bf16[256,768]{1,0:T(8,128)(2,1)} %get-tuple-element.54), channel_id=1, source_target_pairs={{0,1},{1,0},{2,3},{3,2},{4,5},{5,4},{6,7},{7,6},{8,9},{9,8},{10,11... | collective-permute-start | bytes 1179656 | tf_op jit(solution)/shard_map/ppermute | solution.py:463
  103.0 27.2 %collective-permute-start.3 = (bf16[256,768]{1,0:T(8,128)(2,1)S(1)}, bf16[256,768]{1,0:T(8,128)(2,1)}, u32[]{:S(2)}, u32[]{:S(2)}) collective-permute-start(bf16[256,768]{1,0:T(8,128)(2,1)S(1)} %copy-done.14), channel_id=1, source_target_pairs={{0,1},{1,0},{2,3},{3,2},{4,5},{5,4},{6,7},{7,6},{8,9},{9,8},{10,11... | collective-permute-start | bytes 1179656 | tf_op jit(solution)/shard_map/ppermute | solution.py:463
  104.2 21.5 %collective-permute-start.11 = (f32[32,512]{1,0:T(8,128)S(1)}, f32[32,512]{1,0:T(8,128)S(1)}, u32[]{:S(2)}, u32[]{:S(2)}) collective-permute-start(f32[32,512]{1,0:T(8,128)S(1)} %slice_bitcast_fusion), channel_id=1, source_target_pairs={{0,1},{1,0},{2,3},{3,2},{4,5},{5,4},{6,7},{7,6},{8,9},{9,8},{10,11... | collective-permute-start | bytes 196616 | tf_op jit(solution)/shard_map/ppermute | solution.py:463
  106.1 45.1 %collective-permute-start.5 = (bf16[256,1536]{1,0:T(8,128)(2,1)S(1)}, bf16[256,1536]{1,0:T(8,128)(2,1)S(1)}, u32[]{:S(2)}, u32[]{:S(2)}) collective-permute-start(bf16[256,1536]{1,0:T(8,128)(2,1)S(1)} %copy-done.7), channel_id=1, source_target_pairs={{0,1},{1,0},{2,3},{3,2},{4,5},{5,4},{6,7},{7,6},{8,9},{9,8},{10,11... | collective-permute-start | bytes 2359304 | tf_op jit(solution)/shard_map/ppermute | solution.py:463
  125.7 17.6 %collective-permute-start.14 = (bf16[32,512]{1,0:T(8,128)(2,1)S(1)}, bf16[32,512]{1,0:T(8,128)(2,1)S(1)}, u32[]{:S(2)}, u32[]{:S(2)}) collective-permute-start(bf16[32,512]{1,0:T(8,128)(2,1)S(1)} %get-tuple-element.72), channel_id=1, source_target_pairs={{0,24},{2,26},{4,28},{6,30},{8,16},{10,18},{12,20},{14,22},{16,8},... | collective-permute-start | bytes 98312 | tf_op jit(solution)/shard_map/ppermute | solution.py:602
  129.1 14.2 %collective-permute-start.13 = (bf16[32,512]{1,0:T(8,128)(2,1)S(1)}, bf16[32,512]{1,0:T(8,128)(2,1)S(1)}, u32[]{:S(2)}, u32[]{:S(2)}) collective-permute-start(bf16[32,512]{1,0:T(8,128)(2,1)S(1)} %get-tuple-element.72), channel_id=1, source_target_pairs={{0,16},{2,18},{4,20},{6,22},{8,24},{10,26},{12,28},{14,30},{16,0},... | collective-permute-start | bytes 98312 | tf_op jit(solution)/shard_map/ppermute | solution.py:602
  129.1 1.1 copy-start.10
  129.1 14.2 %collective-permute-start.12 = (bf16[32,512]{1,0:T(8,128)(2,1)S(1)}, bf16[32,512]{1,0:T(8,128)(2,1)S(1)}, u32[]{:S(2)}, u32[]{:S(2)}) collective-permute-start(bf16[32,512]{1,0:T(8,128)(2,1)S(1)} %get-tuple-element.72), channel_id=1, source_target_pairs={{0,8},{2,10},{4,12},{6,14},{8,0},{10,2},{12,4},{14,6},{16,24},{18,... | collective-permute-start | bytes 98312 | tf_op jit(solution)/shard_map/ppermute | solution.py:602
  130.9 20.3 %copy-start = (bf16[256,1536]{1,0:T(8,128)(2,1)S(1)}, bf16[256,1536]{1,0:T(8,128)(2,1)}, u32[]{:S(2)}) copy-start(bf16[256,1536]{1,0:T(8,128)(2,1)} %get-tuple-element.57.rest_0_) | copy-start | bytes 2359300
  130.9 20.3 %copy-start.2 = (s32[1,256]{1,0:T(1,128)S(1)}, s32[1,256]{1,0:T(1,128)}, u32[]{:S(2)}) copy-start(s32[1,256]{1,0:T(1,128)} %get-tuple-element.37.refs_0_.rep_ref) | copy-start | bytes 3076
  138.5 12.7 %all-to-all-start.3 = ((bf16[16,16,256]{2,1,0:T(8,128)(2,1)}), bf16[16,16,256]{2,1,0:T(8,128)(2,1)S(1)}, u32[]{:S(2)}, u32[]{:S(2)}) async-start(bf16[16,16,256]{2,1,0:T(8,128)(2,1)} %get-tuple-element.55), calls=%async_computation.3 | async-start | bytes 262144 | tf_op jit(solution)/shard_map/all_to_all | solution.py:467
  143.3 7.0 %collective-permute-start.15 = (bf16[128,512]{1,0:T(8,128)(2,1)S(1)}, bf16[128,512]{1,0:T(8,128)(2,1)S(1)}, u32[]{:S(2)}, u32[]{:S(2)}) collective-permute-start(bf16[128,512]{1,0:T(8,128)(2,1)S(1)} %pad_maximum_fusion), channel_id=1, source_target_pairs={{0,4},{2,6},{4,0},{6,2},{8,12},{10,14},{12,8},{14,10},{16,20},{18,... | collective-permute-start | bytes 393224 | tf_op jit(solution)/shard_map/ppermute | solution.py:602
  150.3 6.4 %collective-permute-start.16 = (bf16[256,512]{1,0:T(8,128)(2,1)S(1)}, bf16[256,512]{1,0:T(8,128)(2,1)S(1)}, u32[]{:S(2)}, u32[]{:S(2)}) collective-permute-start(bf16[256,512]{1,0:T(8,128)(2,1)S(1)} %constant_dynamic-update-slice_fusion.own_ref), channel_id=1, source_target_pairs={{0,2},{2,0},{4,6},{6,4},{8,10},{10,8},{12,14},{14,12},{16,18},{18,... | collective-permute-start | bytes 786440 | tf_op jit(solution)/shard_map/ppermute | solution.py:602
  151.2 1.4 copy-start.1
  (4 other events, 2.8 us)

commit v5 on v3

--- a/solution.py
+++ b/solution.py
@@ -9,7 +9,7 @@
 
 BF = jnp.bfloat16
 F32 = jnp.float32
-GROUP = 8
+GROUP = 16
 SMALL = 24 * 1024 * 1024
 
 
@@ -125,9 +125,16 @@
 def spread_mirrors(nf, nc, tile, blocks, count, mirrors, values_ref, own_ref, *rest):
     part_ref, push_ref = rest[:2]
     sends = rest[2 : 2 + (nf - 1) * nc]
-    acc, own, x, values, *lists, sems = rest[2 + (nf - 1) * nc :]
+    acc, own, x, values, *lists, sems, held_part, held_push = rest[2 + (nf - 1) * nc :][:10]
+    held_sends = rest[2 + (nf - 1) * nc :][10:]
     h = lax.axis_index("feat")
     feats, width = part_ref.shape
+    outs = []
+
+    def put(src, dst):
+        outs.append(pltpu.make_async_copy(src, dst, sems.at[2 + len(outs)]))
+        outs[-1].start()
+
     slots = x.shape[1]
     masters = own.shape[1] - slots
     copies = [
@@ -153,24 +160,41 @@
     for j in range(1, nf):
         for c in range(nc):
             at = pl.multiple_of(lax.rem(h + j, nf) * width + c * part, 128)
-            sends[(j - 1) * nc + c][...] = total(at, part)
+            held_sends[(j - 1) * nc + c][...] = total(at, part)
+            put(held_sends[(j - 1) * nc + c], sends[(j - 1) * nc + c])
     push = flip(total(masters, slots))
     push = push.reshape(push_ref.shape[0], push_ref.shape[2], feats)
     for f in range(nf):
-        push_ref[:, f] = push
-    part_ref[...] = total(pl.multiple_of(h * width, 128), width)
+        held_push[:, f] = push
+    put(held_push, push_ref)
+    held_part[...] = total(pl.multiple_of(h * width, 128), width)
+    put(held_part, part_ref)
+    for copy in outs:
+        copy.wait()
+
+
+def own_term_kernel(nf, wt_ref, *refs):
+    xs, out_ref, rows = refs[:nf], refs[nf], refs[nf + 1]
+    h = lax.axis_index("feat")
+    feats, width = xs[0].shape
+    for j in range(nf):
+        f = lax.rem(h - j + nf, nf)
+        rows[pl.ds(pl.multiple_of(f * feats, feats), feats), :] = xs[j][...]
+    step = 512 if width % 512 == 0 else 128
+    for b in range(0, width, step):
+        out_ref[:, b : b + step] = dot(wt_ref[...], rows[:, b : b + step])
 
 
 def dense_kernel(nf, nc, c, *refs):
-    rep_ref, inc_ref, wt_hbm, w_hbm, cot_hbm = refs[:5]
-    xs, parts = refs[5 : 5 + nf], refs[5 + nf : 5 + 2 * nf]
-    refs = refs[5 + 2 * nf :]
+    rep_ref, inc_ref, wt_hbm, w_hbm, cot_hbm, z_hbm = refs[:6]
+    parts = refs[6 : 6 + nf]
+    refs = refs[6 + nf :]
     if c:
         pay_in = refs[0]
         refs = refs[2 + nf :]
     agg_hbm, out_hbm, g_hbm, pay_ref = refs[:4]
     grads, selfs = refs[4 : 4 + nf], refs[4 + nf : 4 + 2 * nf]
-    wt, w, cot, rows, terms, out, g_all, both, in_sems, out_sems = refs[4 + 2 * nf :]
+    wt, w, cot, z_own, rows, terms, out, g_all, both, held_pay, in_sems, out_sems = refs[4 + 2 * nf :]
     h = lax.axis_index("feat")
     feats, part = grads[0].shape
     wide = w.shape[1]
@@ -182,14 +206,12 @@
 
     early, late = [], []
     for j in range(nf):
-        f = lax.rem(h - j + nf, nf)
         term = parts[j].at[:, chunk] if j == 0 else parts[j]
         early.append(pltpu.make_async_copy(term, terms.at[j], in_sems.at[j]))
-        x = xs[j].at[:, chunk]
-        early.append(pltpu.make_async_copy(x, rows.at[place(f)], in_sems.at[nf + j]))
-    late.append(pltpu.make_async_copy(wt_hbm, wt, in_sems.at[2 * nf]))
-    late.append(pltpu.make_async_copy(cot_hbm.at[:, chunk], cot, in_sems.at[2 * nf + 1]))
-    late.append(pltpu.make_async_copy(w_hbm, w, in_sems.at[2 * nf + 2]))
+    late.append(pltpu.make_async_copy(wt_hbm, wt, in_sems.at[nf]))
+    late.append(pltpu.make_async_copy(z_hbm.at[:, chunk], z_own, in_sems.at[nf + 1]))
+    late.append(pltpu.make_async_copy(cot_hbm.at[:, chunk], cot, in_sems.at[nf + 2]))
+    late.append(pltpu.make_async_copy(w_hbm, w, in_sems.at[nf + 3]))
     for copy in early + late:
         copy.start()
     pick = picks(rep_ref[...], (h * nc + c) * part, part)
@@ -200,7 +222,7 @@
     for j in range(nf):
         f = lax.rem(h - j + nf, nf)
         total = terms[j].astype(F32) + adds[j]
-        rows[pl.ds(pl.multiple_of(wide + f * feats, feats), feats), :] = total.astype(BF)
+        rows[place(f), :] = total.astype(BF)
     out_copies = []
 
     def put(src, dst):
@@ -208,13 +230,13 @@
         copy.start()
         out_copies.append(copy)
 
-    put(rows.at[wide:], agg_hbm)
+    put(rows, agg_hbm)
     for copy in late:
         copy.wait()
     step = 256 if part % 256 == 0 else 128
     for b in range(0, part, step):
         cols = slice(b, b + step)
-        z = dot(wt[...], rows[:, cols])
+        z = z_own[:, cols] + dot(wt[...], rows[:, cols])
         s = 0.5 + 0.5 * jnp.tanh(0.5 * z)
         out[:, cols] = (z * s).astype(BF)
         g = (cot[:, cols].astype(F32) * (s * (1.0 + z * (1.0 - s)))).astype(BF)
@@ -232,11 +254,12 @@
         pay = pay + pay_in[...].astype(F32)
     pay = pay.astype(BF)
     if c + 1 < nc:
-        pay_ref[...] = pay
+        held_pay[...] = pay
     else:
         for f in range(nf):
             mine = flip(pay[f * feats : (f + 1) * feats])
-            pay_ref[:, f] = mine.reshape(pay_ref.shape[0], pay_ref.shape[2], feats)
+            held_pay[:, f] = mine.reshape(pay_ref.shape[0], pay_ref.shape[2], feats)
+    put(held_pay, pay_ref)
     for copy in out_copies:
         copy.wait()
 
@@ -318,7 +341,8 @@
 
 def back_kernel(nf, nc, tile, blocks, count, mirrors, values_ref, *rest):
     grads = rest[: nf * nc]
-    back_ref, push_ref, acc, x_all, values, tiles, sources, targets, sems = rest[nf * nc :]
+    back_ref, push_ref, acc, x_all, values, tiles, sources, targets, sems = rest[nf * nc : -2]
+    held_back, held_push = rest[-2:]
     lists = (tiles, sources, targets)
     h = lax.axis_index("feat")
     feats, masters = back_ref.shape
@@ -344,8 +368,14 @@
         copy.wait()
     run_tiles(count[0], lists, values, 1, x_all, acc, tile)
     partial = acc[:, masters : masters + slots].astype(BF)
-    push_ref[...] = flip(partial).reshape(push_ref.shape)
-    back_ref[...] = acc[:, :masters].astype(BF)
+    held_push[...] = flip(partial).reshape(push_ref.shape)
+    outs = [pltpu.make_async_copy(held_push, push_ref, sems.at[nf * nc + 1])]
+    outs[0].start()
+    held_back[...] = acc[:, :masters].astype(BF)
+    outs.append(pltpu.make_async_copy(held_back, back_ref, sems.at[nf * nc + 2]))
+    outs[1].start()
+    for copy in outs:
+        copy.wait()
 
 
 def final_kernel(nf, nc, rep_ref, inc_ref, back_ref, *rest):
@@ -444,8 +474,12 @@
             pltpu.VMEM((feats, slots), BF),
             all_values,
             *lists,
-            pair,
-        ],
+            pltpu.SemaphoreType.DMA((4 + (nf - 1) * nc,)),
+            pltpu.VMEM((feats, width), BF),
+            pltpu.VMEM((nd, nf, per, feats), BF),
+        ]
+        + [pltpu.VMEM((feats, part), BF)] * ((nf - 1) * nc),
+        out_specs=[ANY] * (2 + (nf - 1) * nc),
     )
     part_recv = [
         [to_peer(part_sends[(j - 1) * nc + c], j) for j in range(1, nf)]
@@ -454,12 +488,20 @@
     incoming = exchange(push, ("dom", "feat"))
 
     flat_w = weights.reshape(2 * wide, wide)
-    wt = flat_w.T
+    wt = [weights[0].T, weights[1].T]
+    (z_own,) = call(
+        functools.partial(own_term_kernel, nf),
+        2 * wide * wide * width,
+        [wt[0], *x_parts],
+        [None] * (nf + 1),
+        [sd((wide, width), F32)],
+        [pltpu.VMEM((wide, width), BF)],
+    )
     rows, grads, grad_own, grad_recv = [], [], [], []
     step = 256 if part % 256 == 0 else 128
     for c in range(nc):
         last = c + 1 == nc
-        args = [rep, incoming, wt, flat_w, cotangent, *x_parts, own_part, *part_recv[c]]
+        args = [rep, incoming, wt[1], flat_w, cotangent, z_own, own_part, *part_recv[c]]
         specs = [None] * 2 + [ANY] * (len(args) - 2)
         alias = {}
         if c:
@@ -480,19 +522,21 @@
             specs,
             outs,
             [
-                pltpu.VMEM((wide, 2 * wide), BF),
+                pltpu.VMEM((wide, wide), BF),
                 pltpu.VMEM((2 * wide, wide), BF),
                 pltpu.VMEM((wide, part), BF),
-                pltpu.VMEM((2 * wide, part), BF),
+                pltpu.VMEM((wide, part), F32),
+                pltpu.VMEM((wide, part), BF),
                 pltpu.VMEM((nf, feats, part), BF),
                 pltpu.VMEM((wide, part), BF),
                 pltpu.VMEM((wide, part), BF),
                 pltpu.VMEM((2 * wide, part), BF),
-                pltpu.SemaphoreType.DMA((2 * nf + 3,)),
-                pltpu.SemaphoreType.DMA((1 + (part // step) * (2 * nf + 2),)),
+                pltpu.VMEM(outs[3].shape, BF),
+                pltpu.SemaphoreType.DMA((nf + 4,)),
+                pltpu.SemaphoreType.DMA((2 + (part // step) * (2 * nf + 2),)),
             ],
             (),
-            [ANY] * 3 + [full(outs[3])] + [ANY] * (2 * nf),
+            [ANY] * len(outs),
             alias,
         )
         rows.append(rows_c)
@@ -522,7 +566,9 @@
         [blocks, tile_counts, grad_mirrors, tile_values, *flat_grads],
         [SMEM, SMEM, None, ANY] + [ANY] * (nf * nc),
         [sd((feats, masters), BF), sd((nd, per, feats), BF)],
-        tile_scratch(nf * nc + 1),
+        tile_scratch(nf * nc + 3)
+        + [pltpu.VMEM((feats, masters), BF), pltpu.VMEM((nd, per, feats), BF)],
+        out_specs=[ANY] * 2,
     )
     back_in = exchange(push, "dom")
 

time: 139 us -> 137 us (0.986)
  waiting for transfers between devices: 40.6 us -> 34.1 us
  Pallas kernels: 47.1 us -> 49.5 us
    ppermute x7, waiting for transfers between devices: 25.4 us -> 18.8 us  [to_peer(): return lax.ppermute(x, 'feat', [(i, (i + j) % nf) for i in range(nf)])]
    unnamed x27, local copies, waits for them, and re-layouts: 4.62 us -> 7.13 us
    pallas_call x9 -> x10, Pallas kernels: 47.1 us -> 49.5 us  [call(): pl.pallas_call(body, grid=grid, in_specs=[full(a) if p is None else p for...]
  transfers between devices with their start and end apart: 21 -> 21, of which waited for: 7 -> 7; matrix products, arithmetic and copies ran while one was open for 1% -> 2% of each run, Pallas kernels for 21% -> 24%
where the time goes in v5:
time: 137 us; the launch traced here: 136 us
  Pallas kernels  49.5 us (36%)
  starting transfers between devices  42.3 us (31%)
  waiting for transfers between devices  34.1 us (25%)
  local copies, waits for them, and re-layouts  7.3 us (5%)
  between operations  1.56 us (1%)
  other arithmetic  1.51 us (1%)
    pallas_call x10, Pallas kernels, call(): pl.pallas_call(body, grid=grid, in_specs=[full(a) if p is None else p for...  49.5 us
    all_to_all x4, starting transfers between devices, exchange(): return lax.all_to_all(flat, axes, 0, 0, tiled=True).reshape(x.shape)  19.5 us
    ppermute x7, waiting for transfers between devices, to_peer(): return lax.ppermute(x, 'feat', [(i, (i + j) % nf) for i in range(nf)])  18.8 us
    ppermute x10, waiting for transfers between devices, swap(): return lax.ppermute(x, 'dom', [(i, i ^ b) for i in range(nd)])  14 us
    ppermute x10, starting transfers between devices, swap(): return lax.ppermute(x, 'dom', [(i, i ^ b) for i in range(nd)])  12.6 us
    ppermute x7, starting transfers between devices, to_peer(): return lax.ppermute(x, 'feat', [(i, (i + j) % nf) for i in range(nf)])  10.2 us
    unnamed x27, local copies, waits for them, and re-layouts  7.13 us
  transfers between devices with their start and end apart: 21, of which 7 were waited for; matrix products, arithmetic and copies ran while one was open for 2% of the time, Pallas kernels for 24%

profile of v5, /device:TPU:0, one launch (start us, length us, event | category | flops | bytes accessed | tf_op | source)
XLA Modules:
  0.0 136.2 jit_solution(9259900621018251392)
XLA Ops:
  0.6 3.5 %shard_map.94 = (bf16[16,16,256]{2,1,0:T(8,128)(2,1)}, s32[1,256]{1,0:T(1,128)}, bf16[256,1536]{1,0:T(8,128)(2,1)}, bf16[256,1536]{1,0:T(8,128)(2,1)}) custom-call(bf16[256,3072]{1,0:T(8,128)(2,1)} %x_ref.3, s32[1,16,16]{2,1,0:T(8,128)} %replica.1), custom_call_target="tpu_custom_call" | custom-call | flops 402653184 | bytes 1573376 | tf_op jit(solution)/shard_map/pallas_call | solution.py:413
  4.1 3.0 %collective-permute-start = (bf16[256,1536]{1,0:T(8,128)(2,1)}, bf16[256,1536]{1,0:T(8,128)(2,1)S(1)}, u32[]{:S(2)}, u32[]{:S(2)}) collective-permute-start(bf16[256,1536]{1,0:T(8,128)(2,1)} %get-tuple-element.35), channel_id=1, source_target_pairs={{0,1},{1,0},{2,3},{3,2},{4,5},{5,4},{6,7},{7,6},{8,9},{9,8},{10,11... | collective-permute-start | bytes 2359304 | tf_op jit(solution)/shard_map/ppermute | solution.py:426
  7.1 5.9 %all-to-all-start = ((bf16[16,16,256]{2,1,0:T(8,128)(2,1)}), bf16[16,16,256]{2,1,0:T(8,128)(2,1)S(1)}, u32[]{:S(2)}, u32[]{:S(2)}) async-start(bf16[16,16,256]{2,1,0:T(8,128)(2,1)} %get-tuple-element.32), calls=%async_computation | async-start | bytes 262144 | tf_op jit(solution)/shard_map/all_to_all | solution.py:430
  13.7 6.8 %shard_map.95.own_ref = bf16[256,3328]{1,0:T(8,128)(2,1)} custom-call(s32[2,72]{1,0:T(2,128)} %bitcast.33, s32[1]{0:T(128)S(6)} %copy.24.count, bf16[256,3072]{1,0:T(8,128)(2,1)} %x_ref.3, bf16[72,128,128]{2,1,0:T(8,128)(2,1)} %values_ref.5), custom_call_target="tpu_custom_call" | custom-call | flops 603979776 | bytes 3932450 | tf_op jit(solution)/shard_map/pallas_call | solution.py:413
  21.6 5.2 %shard_map.96 = (bf16[256,1536]{1,0:T(8,128)(2,1)}, bf16[16,2,16,256]{3,2,1,0:T(8,128)(2,1)}, bf16[256,768]{1,0:T(8,128)(2,1)}, bf16[256,768]{1,0:T(8,128)(2,1)}) custom-call(s32[2,72]{1,0:T(2,128)} %bitcast.34, s32[1]{0:T(128)S(6)} %copy.24.count, bf16[16,16,256]{2,1,0:T(8,128)(2,1)} %copy-done.8, bf16[72,128,128]{2,1,0:T(8,128)(2,1)} %values_ref.5, ...), custom_call_target="tpu_custom_call" | custom-call | flops 150994944 | bytes 4194594 | tf_op jit(solution)/shard_map/pallas_call | solution.py:413
  26.8 4.2 %all-to-all-start.1 = ((bf16[32,16,256]{2,1,0:T(8,128)(2,1)}), bf16[32,16,256]{2,1,0:T(8,128)(2,1)S(1)}, u32[]{:S(2)}, u32[]{:S(2)}) async-start(bf16[32,16,256]{2,1,0:T(8,128)(2,1)} %bitcast.32), calls=%async_computation.1 | async-start | bytes 524288 | tf_op jit(solution)/shard_map/all_to_all | solution.py:430
  31.1 1.7 %collective-permute-start.2 = (bf16[256,768]{1,0:T(8,128)(2,1)}, bf16[256,768]{1,0:T(8,128)(2,1)}, u32[]{:S(2)}, u32[]{:S(2)}) collective-permute-start(bf16[256,768]{1,0:T(8,128)(2,1)} %get-tuple-element.38), channel_id=1, source_target_pairs={{0,1},{1,0},{2,3},{3,2},{4,5},{5,4},{6,7},{7,6},{8,9},{9,8},{10,11... | collective-permute-start | bytes 1179656 | tf_op jit(solution)/shard_map/ppermute | solution.py:426
  34.2 1.0 copy.15
  36.1 4.2 %shard_map.97.refs_5_ = f32[512,1536]{1,0:T(8,128)} custom-call(bf16[512,512]{1,0:T(8,128)(2,1)} %bitcast.28, bf16[256,1536]{1,0:T(8,128)(2,1)} %get-tuple-element.34.refs_0_, bf16[256,1536]{1,0:T(8,128)(2,1)} %copy-done.6), custom_call_target="tpu_custom_call" | custom-call | flops 805306368 | bytes 2097152 | tf_op jit(solution)/shard_map/pallas_call | solution.py:413
  40.3 5.4 %collective-permute-done.2.refs_7_ = bf16[256,768]{1,0:T(8,128)(2,1)} collective-permute-done((bf16[256,768]{1,0:T(8,128)(2,1)}, bf16[256,768]{1,0:T(8,128)(2,1)}, u32[]{:S(2)}, u32[]{:S(2)}) %collective-permute-start.2) | collective-permute-done | bytes 393248 | tf_op jit(solution)/shard_map/ppermute | solution.py:426
  46.4 7.0 %shard_map.98 = (bf16[512,768]{1,0:T(8,128)(2,1)}, bf16[512,1536]{1,0:T(8,128)(2,1)}, bf16[512,768]{1,0:T(8,128)(2,1)}, bf16[512,256]{1,0:T(8,128)(2,1)}, bf16[2...) custom-call(s32[1,256]{1,0:T(1,128)} %get-tuple-element.31.refs_0_.rep_ref, ...), custom_call_target="tpu_custom_call" | custom-call | flops 1610612736 | bytes 6160896 | tf_op jit(solution)/shard_map/pallas_call | solution.py:413
  54.2 7.1 %shard_map.99 = (bf16[512,768]{1,0:T(8,128)(2,1)}, bf16[512,1536]{1,0:T(8,128)(2,1)}, bf16[512,768]{1,0:T(8,128)(2,1)}, bf16[16,2,16,256]{3,2,1,0:T(8,128)(2,1)}...) custom-call(s32[1,256]{1,0:T(1,128)} %get-tuple-element.31.refs_0_.r, ...), custom_call_target="tpu_custom_call", output_to_operand_aliasing={{1}: (9, {}), {6}: (10, {}), {7}: (11, {})} | custom-call | flops 1610612736 | bytes 9568768 | tf_op jit(solution)/shard_map/pallas_call | solution.py:413
  61.3 5.3 %shard_map.102 = (f32[2,256,512]{2,1,0:T(8,128)}, bf16[2,256,512]{2,1,0:T(8,128)(2,1)}) custom-call(bf16[256,1536]{1,0:T(8,128)(2,1)} %get-tuple-element.34.refs_0_, bf16[256,1536]{1,0:T(8,128)(2,1)} %copy-done.6, bf16[512,768]{1,0:T(8,128)(2,1)} %get-tuple-element.53.refs_2_, bf16[512,768]{1,0:T(8,128)(2,1)} %get-tuple-element.54.refs_3_, ...), custom_call_target="tpu_custom_call" | custom-call | flops 1610612736 | bytes 4718592 | tf_op jit(solution)/shard_map/pallas_call | solution.py:413
  66.7 2.1 %collective-permute-done.6 = bf16[2,256,512]{2,1,0:T(8,128)(2,1)S(1)} collective-permute-done((bf16[2,256,512]{2,1,0:T(8,128)(2,1)}, bf16[2,256,512]{2,1,0:T(8,128)(2,1)S(1)}, u32[]{:S(2)}, u32[]{:S(2)}) %collective-permute-start.6) | collective-permute-done | bytes 524320 | tf_op jit(solution)/shard_map/ppermute | solution.py:578
  68.8 1.4 %convert_add_fusion = f32[2,256,512]{2,1,0:T(8,128)S(1)} fusion(f32[2,256,512]{2,1,0:T(8,128)} %get-tuple-element.57, bf16[2,256,512]{2,1,0:T(8,128)(2,1)S(1)} %collective-permute-done.6), kind=kLoop, calls=%fused_computation | loop fusion | flops 524288 | bytes 2621440 | tf_op jit(solution)/shard_map/add | solution.py:585
  70.2 1.5 %collective-permute-start.7 = (bf16[2,128,512]{2,1,0:T(8,128)(2,1)S(1)}, bf16[2,128,512]{2,1,0:T(8,128)(2,1)S(1)}, u32[]{:S(2)}, u32[]{:S(2)}) collective-permute-start(bf16[2,128,512]{2,1,0:T(8,128)(2,1)S(1)} %dynamic-slice_convert_fusion), channel_id=1, source_target_pairs={{0,4},{2,6},{4,0},{6,2},{8,12},{10,14},{12,8},{14,10},{16,20},{18,... | collective-permute-start | bytes 786440 | tf_op jit(solution)/shard_map/ppermute | solution.py:578
  71.8 6.9 %collective-permute-done.7 = bf16[2,128,512]{2,1,0:T(8,128)(2,1)S(1)} collective-permute-done((bf16[2,128,512]{2,1,0:T(8,128)(2,1)S(1)}, bf16[2,128,512]{2,1,0:T(8,128)(2,1)S(1)}, u32[]{:S(2)}, u32[]{:S(2)}) %collective-permute-start.7) | collective-permute-done | bytes 262176 | tf_op jit(solution)/shard_map/ppermute | solution.py:578
  78.8 3.6 %collective-permute-start.10 = (bf16[2,32,512]{2,1,0:T(8,128)(2,1)S(1)}, bf16[2,32,512]{2,1,0:T(8,128)(2,1)S(1)}, u32[]{:S(2)}, u32[]{:S(2)}) collective-permute-start(bf16[2,32,512]{2,1,0:T(8,128)(2,1)S(1)} %get-tuple-element.64), channel_id=1, source_target_pairs={{0,24},{2,26},{4,28},{6,30},{8,16},{10,18},{12,20},{14,22},{16,8},... | collective-permute-start | bytes 196616 | tf_op jit(solution)/shard_map/ppermute | solution.py:578
  83.2 1.2 collective-permute-start.4
  84.4 4.7 %all-to-all-start.2 = ((bf16[32,16,256]{2,1,0:T(8,128)(2,1)}), bf16[32,16,256]{2,1,0:T(8,128)(2,1)S(1)}, u32[]{:S(2)}, u32[]{:S(2)}) async-start(bf16[32,16,256]{2,1,0:T(8,128)(2,1)} %bitcast.31), calls=%async_computation.2 | async-start | bytes 524288 | tf_op jit(solution)/shard_map/all_to_all | solution.py:430
  89.1 1.8 %collective-permute-start.3 = (bf16[256,768]{1,0:T(8,128)(2,1)}, bf16[256,768]{1,0:T(8,128)(2,1)}, u32[]{:S(2)}, u32[]{:S(2)}) collective-permute-start(bf16[256,768]{1,0:T(8,128)(2,1)} %get-tuple-element.47), channel_id=1, source_target_pairs={{0,1},{1,0},{2,3},{3,2},{4,5},{5,4},{6,7},{7,6},{8,9},{9,8},{10,11... | collective-permute-start | bytes 1179656 | tf_op jit(solution)/shard_map/ppermute | solution.py:426
  91.3 1.8 %collective-permute-start.5 = (bf16[256,1536]{1,0:T(8,128)(2,1)S(1)}, bf16[256,1536]{1,0:T(8,128)(2,1)S(1)}, u32[]{:S(2)}, u32[]{:S(2)}) collective-permute-start(bf16[256,1536]{1,0:T(8,128)(2,1)S(1)} %copy-done.7), channel_id=1, source_target_pairs={{0,1},{1,0},{2,3},{3,2},{4,5},{5,4},{6,7},{7,6},{8,9},{9,8},{10,11... | collective-permute-start | bytes 2359304 | tf_op jit(solution)/shard_map/ppermute | solution.py:426
  93.1 13.4 %collective-permute-done.11 = f32[32,512]{1,0:T(8,128)S(1)} collective-permute-done((f32[32,512]{1,0:T(8,128)S(1)}, f32[32,512]{1,0:T(8,128)S(1)}, u32[]{:S(2)}, u32[]{:S(2)}) %collective-permute-start.11) | collective-permute-done | bytes 65568 | tf_op jit(solution)/shard_map/ppermute | solution.py:426
  106.6 1.3 collective-permute-start.12
  107.8 2.9 %collective-permute-start.13 = (bf16[32,512]{1,0:T(8,128)(2,1)S(1)}, bf16[32,512]{1,0:T(8,128)(2,1)S(1)}, u32[]{:S(2)}, u32[]{:S(2)}) collective-permute-start(bf16[32,512]{1,0:T(8,128)(2,1)S(1)} %get-tuple-element.60), channel_id=1, source_target_pairs={{0,16},{2,18},{4,20},{6,22},{8,24},{10,26},{12,28},{14,30},{16,0},... | collective-permute-start | bytes 98312 | tf_op jit(solution)/shard_map/ppermute | solution.py:578
  111.7 7.1 %shard_map.100 = (bf16[256,3072]{1,0:T(8,128)(2,1)}, bf16[16,16,256]{2,1,0:T(8,128)(2,1)}) custom-call(s32[2,72]{1,0:T(2,128)} %bitcast.35, s32[1]{0:T(128)S(6)} %copy.24.count, bf16[16,2,16,256]{3,2,1,0:T(8,128)(2,1)} %bitcast.29, bf16[72,128,128]{2,1,0:T(8,128)(2,1)} %values_ref.5, bf16[256,768]{1,0:T(8,128)(2,1)} %get-tuple-element.45.rest_0_, ...), custom_call_target="tpu_custom_call" | custom-call | flops 603979776 | bytes 4194594 | tf_op jit(solution)/shard_map/pallas_call | solution.py:413
  118.8 4.7 %all-to-all-start.3 = ((bf16[16,16,256]{2,1,0:T(8,128)(2,1)}), bf16[16,16,256]{2,1,0:T(8,128)(2,1)S(1)}, u32[]{:S(2)}, u32[]{:S(2)}) async-start(bf16[16,16,256]{2,1,0:T(8,128)(2,1)} %get-tuple-element.49), calls=%async_computation.3 | async-start | bytes 262144 | tf_op jit(solution)/shard_map/all_to_all | solution.py:430
  123.6 2.0 %collective-permute-start.15 = (bf16[128,512]{1,0:T(8,128)(2,1)S(1)}, bf16[128,512]{1,0:T(8,128)(2,1)S(1)}, u32[]{:S(2)}, u32[]{:S(2)}) collective-permute-start(bf16[128,512]{1,0:T(8,128)(2,1)S(1)} %pad_maximum_fusion), channel_id=1, source_target_pairs={{0,4},{2,6},{4,0},{6,2},{8,12},{10,14},{12,8},{14,10},{16,20},{18,... | collective-permute-start | bytes 393224 | tf_op jit(solution)/shard_map/ppermute | solution.py:578
  125.6 5.0 %collective-permute-done.15 = bf16[128,512]{1,0:T(8,128)(2,1)S(1)} collective-permute-done((bf16[128,512]{1,0:T(8,128)(2,1)S(1)}, bf16[128,512]{1,0:T(8,128)(2,1)S(1)}, u32[]{:S(2)}, u32[]{:S(2)}) %collective-permute-start.15) | collective-permute-done | bytes 131104 | tf_op jit(solution)/shard_map/ppermute | solution.py:578
  131.5 1.4 %copy-done.1 = bf16[256,3072]{1,0:T(8,128)(2,1)S(1)} copy-done((bf16[256,3072]{1,0:T(8,128)(2,1)S(1)}, bf16[256,3072]{1,0:T(8,128)(2,1)}, u32[]{:S(2)}) %copy-start.1) | copy-done | bytes 1572888
  132.8 2.1 %shard_map.101 = bf16[256,3072]{1,0:T(8,128)(2,1)} custom-call(s32[1,256]{1,0:T(1,128)S(1)} %copy-done.2, bf16[16,16,256]{2,1,0:T(8,128)(2,1)S(1)} %all-to-all-done.3.inc_ref, bf16[256,3072]{1,0:T(8,128)(2,1)S(1)} %copy-done.1, bf16[256,1536]{1,0:T(8,128)(2,1)S(1)} %copy-done, bf16[256,1536]{1,0:T(8,128)(2,1)S(1)} %collective-permute-done.5.rest_1_), custom_call_target="tpu_custom_call" | custom-call | flops 402653184 | bytes 3277312 | tf_op jit(solution)/shard_map/pallas_call | solution.py:413
  135.0 1.2 shard_map.103
  (57 shorter events, 8.4 us)
Async XLA Ops:
  4.1 31.1 %collective-permute-start = (bf16[256,1536]{1,0:T(8,128)(2,1)}, bf16[256,1536]{1,0:T(8,128)(2,1)S(1)}, u32[]{:S(2)}, u32[]{:S(2)}) collective-permute-start(bf16[256,1536]{1,0:T(8,128)(2,1)} %get-tuple-element.35), channel_id=1, source_target_pairs={{0,1},{1,0},{2,3},{3,2},{4,5},{5,4},{6,7},{7,6},{8,9},{9,8},{10,11... | collective-permute-start | bytes 2359304 | tf_op jit(solution)/shard_map/ppermute | solution.py:426
  7.1 13.8 %all-to-all-start = ((bf16[16,16,256]{2,1,0:T(8,128)(2,1)}), bf16[16,16,256]{2,1,0:T(8,128)(2,1)S(1)}, u32[]{:S(2)}, u32[]{:S(2)}) async-start(bf16[16,16,256]{2,1,0:T(8,128)(2,1)} %get-tuple-element.32), calls=%async_computation | async-start | bytes 262144 | tf_op jit(solution)/shard_map/all_to_all | solution.py:430
  20.5 12.7 %copy-start.3 = (bf16[2,512,512]{2,1,0:T(8,128)(2,1)S(1)}, bf16[2,512,512]{2,1,0:T(8,128)(2,1)}, u32[]{:S(2)}) copy-start(bf16[2,512,512]{2,1,0:T(8,128)(2,1)} %param.8) | copy-start | bytes 3145732
  20.9 0.7 copy-start.8
  26.8 18.9 %all-to-all-start.1 = ((bf16[32,16,256]{2,1,0:T(8,128)(2,1)}), bf16[32,16,256]{2,1,0:T(8,128)(2,1)S(1)}, u32[]{:S(2)}, u32[]{:S(2)}) async-start(bf16[32,16,256]{2,1,0:T(8,128)(2,1)} %bitcast.32), calls=%async_computation.1 | async-start | bytes 524288 | tf_op jit(solution)/shard_map/all_to_all | solution.py:430
  31.1 14.7 %collective-permute-start.2 = (bf16[256,768]{1,0:T(8,128)(2,1)}, bf16[256,768]{1,0:T(8,128)(2,1)}, u32[]{:S(2)}, u32[]{:S(2)}) collective-permute-start(bf16[256,768]{1,0:T(8,128)(2,1)} %get-tuple-element.38), channel_id=1, source_target_pairs={{0,1},{1,0},{2,3},{3,2},{4,5},{5,4},{6,7},{7,6},{8,9},{9,8},{10,11... | collective-permute-start | bytes 1179656 | tf_op jit(solution)/shard_map/ppermute | solution.py:426
  32.7 20.8 %collective-permute-start.1 = (bf16[256,768]{1,0:T(8,128)(2,1)}, bf16[256,768]{1,0:T(8,128)(2,1)S(1)}, u32[]{:S(2)}, u32[]{:S(2)}) collective-permute-start(bf16[256,768]{1,0:T(8,128)(2,1)} %get-tuple-element.37), channel_id=1, source_target_pairs={{0,1},{1,0},{2,3},{3,2},{4,5},{5,4},{6,7},{7,6},{8,9},{9,8},{10,11... | collective-permute-start | bytes 1179656 | tf_op jit(solution)/shard_map/ppermute | solution.py:426
  35.2 0.9 copy-start.6
  45.7 0.7 copy-start.4
  53.5 0.7 copy-start.9
  66.6 2.2 %collective-permute-start.6 = (bf16[2,256,512]{2,1,0:T(8,128)(2,1)}, bf16[2,256,512]{2,1,0:T(8,128)(2,1)S(1)}, u32[]{:S(2)}, u32[]{:S(2)}) collective-permute-start(bf16[2,256,512]{2,1,0:T(8,128)(2,1)} %get-tuple-element.58), channel_id=1, source_target_pairs={{0,2},{2,0},{4,6},{6,4},{8,10},{10,8},{12,14},{14,12},{16,18},{18,... | collective-permute-start | bytes 1572872 | tf_op jit(solution)/shard_map/ppermute | solution.py:578
  70.2 21.1 %copy-start.7 = (bf16[256,1536]{1,0:T(8,128)(2,1)S(1)}, bf16[256,1536]{1,0:T(8,128)(2,1)}, u32[]{:S(2)}) copy-start(bf16[256,1536]{1,0:T(8,128)(2,1)} %get-tuple-element.52) | copy-start | bytes 2359300
  70.2 8.4 %collective-permute-start.7 = (bf16[2,128,512]{2,1,0:T(8,128)(2,1)S(1)}, bf16[2,128,512]{2,1,0:T(8,128)(2,1)S(1)}, u32[]{:S(2)}, u32[]{:S(2)}) collective-permute-start(bf16[2,128,512]{2,1,0:T(8,128)(2,1)S(1)} %dynamic-slice_convert_fusion), channel_id=1, source_target_pairs={{0,4},{2,6},{4,0},{6,2},{8,12},{10,14},{12,8},{14,10},{16,20},{18,... | collective-permute-start | bytes 786440 | tf_op jit(solution)/shard_map/ppermute | solution.py:578
  78.8 12.2 %collective-permute-start.10 = (bf16[2,32,512]{2,1,0:T(8,128)(2,1)S(1)}, bf16[2,32,512]{2,1,0:T(8,128)(2,1)S(1)}, u32[]{:S(2)}, u32[]{:S(2)}) collective-permute-start(bf16[2,32,512]{2,1,0:T(8,128)(2,1)S(1)} %get-tuple-element.64), channel_id=1, source_target_pairs={{0,24},{2,26},{4,28},{6,30},{8,16},{10,18},{12,20},{14,22},{16,8},... | collective-permute-start | bytes 196616 | tf_op jit(solution)/shard_map/ppermute | solution.py:578
  82.3 8.6 %collective-permute-start.8 = (bf16[2,32,512]{2,1,0:T(8,128)(2,1)S(1)}, bf16[2,32,512]{2,1,0:T(8,128)(2,1)S(1)}, u32[]{:S(2)}, u32[]{:S(2)}) collective-permute-start(bf16[2,32,512]{2,1,0:T(8,128)(2,1)S(1)} %get-tuple-element.63), channel_id=1, source_target_pairs={{0,8},{2,10},{4,12},{6,14},{8,0},{10,2},{12,4},{14,6},{16,24},{18,... | collective-permute-start | bytes 196616 | tf_op jit(solution)/shard_map/ppermute | solution.py:578
  82.3 8.6 %collective-permute-start.9 = (bf16[2,32,512]{2,1,0:T(8,128)(2,1)S(1)}, bf16[2,32,512]{2,1,0:T(8,128)(2,1)S(1)}, u32[]{:S(2)}, u32[]{:S(2)}) collective-permute-start(bf16[2,32,512]{2,1,0:T(8,128)(2,1)S(1)} %get-tuple-element.65), channel_id=1, source_target_pairs={{0,16},{2,18},{4,20},{6,22},{8,24},{10,26},{12,28},{14,30},{16,0},... | collective-permute-start | bytes 196616 | tf_op jit(solution)/shard_map/ppermute | solution.py:578
  83.2 27.5 %collective-permute-start.4 = (bf16[256,768]{1,0:T(8,128)(2,1)}, bf16[256,768]{1,0:T(8,128)(2,1)S(1)}, u32[]{:S(2)}, u32[]{:S(2)}) collective-permute-start(bf16[256,768]{1,0:T(8,128)(2,1)} %get-tuple-element.48), channel_id=1, source_target_pairs={{0,1},{1,0},{2,3},{3,2},{4,5},{5,4},{6,7},{7,6},{8,9},{9,8},{10,11... | collective-permute-start | bytes 1179656 | tf_op jit(solution)/shard_map/ppermute | solution.py:426
  84.4 26.6 %all-to-all-start.2 = ((bf16[32,16,256]{2,1,0:T(8,128)(2,1)}), bf16[32,16,256]{2,1,0:T(8,128)(2,1)S(1)}, u32[]{:S(2)}, u32[]{:S(2)}) async-start(bf16[32,16,256]{2,1,0:T(8,128)(2,1)} %bitcast.31), calls=%async_computation.2 | async-start | bytes 524288 | tf_op jit(solution)/shard_map/all_to_all | solution.py:430
  89.1 21.9 %collective-permute-start.3 = (bf16[256,768]{1,0:T(8,128)(2,1)}, bf16[256,768]{1,0:T(8,128)(2,1)}, u32[]{:S(2)}, u32[]{:S(2)}) collective-permute-start(bf16[256,768]{1,0:T(8,128)(2,1)} %get-tuple-element.47), channel_id=1, source_target_pairs={{0,1},{1,0},{2,3},{3,2},{4,5},{5,4},{6,7},{7,6},{8,9},{9,8},{10,11... | collective-permute-start | bytes 1179656 | tf_op jit(solution)/shard_map/ppermute | solution.py:426
  91.0 15.5 %collective-permute-start.11 = (f32[32,512]{1,0:T(8,128)S(1)}, f32[32,512]{1,0:T(8,128)S(1)}, u32[]{:S(2)}, u32[]{:S(2)}) collective-permute-start(f32[32,512]{1,0:T(8,128)S(1)} %slice_bitcast_fusion), channel_id=1, source_target_pairs={{0,1},{1,0},{2,3},{3,2},{4,5},{5,4},{6,7},{7,6},{8,9},{9,8},{10,11... | collective-permute-start | bytes 196616 | tf_op jit(solution)/shard_map/ppermute | solution.py:426
  91.3 40.1 %collective-permute-start.5 = (bf16[256,1536]{1,0:T(8,128)(2,1)S(1)}, bf16[256,1536]{1,0:T(8,128)(2,1)S(1)}, u32[]{:S(2)}, u32[]{:S(2)}) collective-permute-start(bf16[256,1536]{1,0:T(8,128)(2,1)S(1)} %copy-done.7), channel_id=1, source_target_pairs={{0,1},{1,0},{2,3},{3,2},{4,5},{5,4},{6,7},{7,6},{8,9},{9,8},{10,11... | collective-permute-start | bytes 2359304 | tf_op jit(solution)/shard_map/ppermute | solution.py:426
  106.6 17.0 %collective-permute-start.12 = (bf16[32,512]{1,0:T(8,128)(2,1)S(1)}, bf16[32,512]{1,0:T(8,128)(2,1)S(1)}, u32[]{:S(2)}, u32[]{:S(2)}) collective-permute-start(bf16[32,512]{1,0:T(8,128)(2,1)S(1)} %get-tuple-element.60), channel_id=1, source_target_pairs={{0,8},{2,10},{4,12},{6,14},{8,0},{10,2},{12,4},{14,6},{16,24},{18,... | collective-permute-start | bytes 98312 | tf_op jit(solution)/shard_map/ppermute | solution.py:578
  107.8 15.7 %collective-permute-start.13 = (bf16[32,512]{1,0:T(8,128)(2,1)S(1)}, bf16[32,512]{1,0:T(8,128)(2,1)S(1)}, u32[]{:S(2)}, u32[]{:S(2)}) collective-permute-start(bf16[32,512]{1,0:T(8,128)(2,1)S(1)} %get-tuple-element.60), channel_id=1, source_target_pairs={{0,16},{2,18},{4,20},{6,22},{8,24},{10,26},{12,28},{14,30},{16,0},... | collective-permute-start | bytes 98312 | tf_op jit(solution)/shard_map/ppermute | solution.py:578
  110.7 0.7 copy-start.10
  110.7 12.9 %collective-permute-start.14 = (bf16[32,512]{1,0:T(8,128)(2,1)S(1)}, bf16[32,512]{1,0:T(8,128)(2,1)S(1)}, u32[]{:S(2)}, u32[]{:S(2)}) collective-permute-start(bf16[32,512]{1,0:T(8,128)(2,1)S(1)} %get-tuple-element.60), channel_id=1, source_target_pairs={{0,24},{2,26},{4,28},{6,30},{8,16},{10,18},{12,20},{14,22},{16,8},... | collective-permute-start | bytes 98312 | tf_op jit(solution)/shard_map/ppermute | solution.py:578
  111.0 0.7 copy-start.5
  111.7 19.7 %copy-start = (bf16[256,1536]{1,0:T(8,128)(2,1)S(1)}, bf16[256,1536]{1,0:T(8,128)(2,1)}, u32[]{:S(2)}) copy-start(bf16[256,1536]{1,0:T(8,128)(2,1)} %get-tuple-element.51.rest_0_) | copy-start | bytes 2359300
  111.7 19.7 %copy-start.2 = (s32[1,256]{1,0:T(1,128)S(1)}, s32[1,256]{1,0:T(1,128)}, u32[]{:S(2)}) copy-start(s32[1,256]{1,0:T(1,128)} %get-tuple-element.31.refs_0_.rep_ref) | copy-start | bytes 3076
  118.8 12.6 %all-to-all-start.3 = ((bf16[16,16,256]{2,1,0:T(8,128)(2,1)}), bf16[16,16,256]{2,1,0:T(8,128)(2,1)S(1)}, u32[]{:S(2)}, u32[]{:S(2)}) async-start(bf16[16,16,256]{2,1,0:T(8,128)(2,1)} %get-tuple-element.49), calls=%async_computation.3 | async-start | bytes 262144 | tf_op jit(solution)/shard_map/all_to_all | solution.py:430
  123.6 7.0 %collective-permute-start.15 = (bf16[128,512]{1,0:T(8,128)(2,1)S(1)}, bf16[128,512]{1,0:T(8,128)(2,1)S(1)}, u32[]{:S(2)}, u32[]{:S(2)}) collective-permute-start(bf16[128,512]{1,0:T(8,128)(2,1)S(1)} %pad_maximum_fusion), channel_id=1, source_target_pairs={{0,4},{2,6},{4,0},{6,2},{8,12},{10,14},{12,8},{14,10},{16,20},{18,... | collective-permute-start | bytes 393224 | tf_op jit(solution)/shard_map/ppermute | solution.py:578
  130.6 4.4 %collective-permute-start.16 = (bf16[256,512]{1,0:T(8,128)(2,1)S(1)}, bf16[256,512]{1,0:T(8,128)(2,1)S(1)}, u32[]{:S(2)}, u32[]{:S(2)}) collective-permute-start(bf16[256,512]{1,0:T(8,128)(2,1)S(1)} %constant_dynamic-update-slice_fusion.own_ref), channel_id=1, source_target_pairs={{0,2},{2,0},{4,6},{6,4},{8,10},{10,8},{12,14},{14,12},{16,18},{18,... | collective-permute-start | bytes 786440 | tf_op jit(solution)/shard_map/ppermute | solution.py:578
  131.4 1.4 %copy-start.1 = (bf16[256,3072]{1,0:T(8,128)(2,1)S(1)}, bf16[256,3072]{1,0:T(8,128)(2,1)}, u32[]{:S(2)}) copy-start(bf16[256,3072]{1,0:T(8,128)(2,1)} %get-tuple-element.50.back_ref) | copy-start | bytes 4718596

commit v6 on v5

--- a/solution.py
+++ b/solution.py
@@ -182,7 +182,7 @@
         rows[pl.ds(pl.multiple_of(f * feats, feats), feats), :] = xs[j][...]
     step = 512 if width % 512 == 0 else 128
     for b in range(0, width, step):
-        out_ref[:, b : b + step] = dot(wt_ref[...], rows[:, b : b + step])
+        out_ref[:, b : b + step] = dot(wt_ref[:, : rows.shape[0]], rows[:, b : b + step])
 
 
 def dense_kernel(nf, nc, c, *refs):
@@ -208,7 +208,7 @@
     for j in range(nf):
         term = parts[j].at[:, chunk] if j == 0 else parts[j]
         early.append(pltpu.make_async_copy(term, terms.at[j], in_sems.at[j]))
-    late.append(pltpu.make_async_copy(wt_hbm, wt, in_sems.at[nf]))
+    late.append(pltpu.make_async_copy(wt_hbm.at[:, wide:], wt, in_sems.at[nf]))
     late.append(pltpu.make_async_copy(z_hbm.at[:, chunk], z_own, in_sems.at[nf + 1]))
     late.append(pltpu.make_async_copy(cot_hbm.at[:, chunk], cot, in_sems.at[nf + 2]))
     late.append(pltpu.make_async_copy(w_hbm, w, in_sems.at[nf + 3]))
@@ -488,11 +488,11 @@
     incoming = exchange(push, ("dom", "feat"))
 
     flat_w = weights.reshape(2 * wide, wide)
-    wt = [weights[0].T, weights[1].T]
+    wt = flat_w.T
     (z_own,) = call(
         functools.partial(own_term_kernel, nf),
         2 * wide * wide * width,
-        [wt[0], *x_parts],
+        [wt, *x_parts],
         [None] * (nf + 1),
         [sd((wide, width), F32)],
         [pltpu.VMEM((wide, width), BF)],
@@ -501,7 +501,7 @@
     step = 256 if part % 256 == 0 else 128
     for c in range(nc):
         last = c + 1 == nc
-        args = [rep, incoming, wt[1], flat_w, cotangent, z_own, own_part, *part_recv[c]]
+        args = [rep, incoming, wt, flat_w, cotangent, z_own, own_part, *part_recv[c]]
         specs = [None] * 2 + [ANY] * (len(args) - 2)
         alias = {}
         if c:
@@ -594,7 +594,7 @@
         keep, sends = pieces[0], [piece.astype(BF) for piece in pieces[1:]]
     total = cur[0]
     for j in range(1, nf):
-        total = total + to_peer(cur[j], j)
+        total = total + to_peer(cur[j].astype(BF), j).astype(F32)
     total = total.astype(BF)
     for k in reversed(range(1, len(radices))):
         unit = unit_of(radices, k)

time: 137 us -> 136 us (level)
    unnamed x27, local copies, waits for them, and re-layouts: 7.13 us -> 5.22 us
  transfers between devices with their start and end apart: 21 -> 21, of which waited for: 7 -> 7; matrix products, arithmetic and copies ran while one was open for 2% -> 1% of each run, Pallas kernels for 24% -> 24%
where the time goes in v6:
time: 136 us; the launch traced here: 135 us
  Pallas kernels  49.7 us (37%)
  starting transfers between devices  42.2 us (31%)
  waiting for transfers between devices  33.9 us (25%)
  local copies, waits for them, and re-layouts  6.62 us (5%)
  between operations  1.57 us (1%)
  other arithmetic  1.51 us (1%)
    pallas_call x10, Pallas kernels, call(): pl.pallas_call(body, grid=grid, in_specs=[full(a) if p is None else p for...  49.7 us
    all_to_all x4, starting transfers between devices, exchange(): return lax.all_to_all(flat, axes, 0, 0, tiled=True).reshape(x.shape)  19.5 us
    ppermute x7, waiting for transfers between devices, to_peer(): return lax.ppermute(x, 'feat', [(i, (i + j) % nf) for i in range(nf)])  18.7 us
    ppermute x10, waiting for transfers between devices, swap(): return lax.ppermute(x, 'dom', [(i, i ^ b) for i in range(nd)])  14 us
    ppermute x10, starting transfers between devices, swap(): return lax.ppermute(x, 'dom', [(i, i ^ b) for i in range(nd)])  12.5 us
    ppermute x7, starting transfers between devices, to_peer(): return lax.ppermute(x, 'feat', [(i, (i + j) % nf) for i in range(nf)])  10.2 us
    unnamed x27, local copies, waits for them, and re-layouts  5.22 us
  transfers between devices with their start and end apart: 21, of which 7 were waited for; matrix products, arithmetic and copies ran while one was open for 1% of the time, Pallas kernels for 24%

profile of v6, /device:TPU:0, one launch (start us, length us, event | category | flops | bytes accessed | tf_op | source)
XLA Modules:
  0.0 135.5 jit_solution(10013377806078760900)
XLA Ops:
  0.6 3.5 %shard_map.94 = (bf16[16,16,256]{2,1,0:T(8,128)(2,1)}, s32[1,256]{1,0:T(1,128)}, bf16[256,1536]{1,0:T(8,128)(2,1)}, bf16[256,1536]{1,0:T(8,128)(2,1)}) custom-call(bf16[256,3072]{1,0:T(8,128)(2,1)} %x_ref.3, s32[1,16,16]{2,1,0:T(8,128)} %replica.1), custom_call_target="tpu_custom_call" | custom-call | flops 402653184 | bytes 1573376 | tf_op jit(solution)/shard_map/pallas_call | solution.py:413
  4.1 3.0 %collective-permute-start = (bf16[256,1536]{1,0:T(8,128)(2,1)}, bf16[256,1536]{1,0:T(8,128)(2,1)S(1)}, u32[]{:S(2)}, u32[]{:S(2)}) collective-permute-start(bf16[256,1536]{1,0:T(8,128)(2,1)} %get-tuple-element.35), channel_id=1, source_target_pairs={{0,1},{1,0},{2,3},{3,2},{4,5},{5,4},{6,7},{7,6},{8,9},{9,8},{10,11... | collective-permute-start | bytes 2359304 | tf_op jit(solution)/shard_map/ppermute | solution.py:426
  7.1 5.9 %all-to-all-start = ((bf16[16,16,256]{2,1,0:T(8,128)(2,1)}), bf16[16,16,256]{2,1,0:T(8,128)(2,1)S(1)}, u32[]{:S(2)}, u32[]{:S(2)}) async-start(bf16[16,16,256]{2,1,0:T(8,128)(2,1)} %get-tuple-element.32), calls=%async_computation | async-start | bytes 262144 | tf_op jit(solution)/shard_map/all_to_all | solution.py:430
  13.7 6.8 %shard_map.95.own_ref = bf16[256,3328]{1,0:T(8,128)(2,1)} custom-call(s32[2,72]{1,0:T(2,128)} %bitcast.27, s32[1]{0:T(128)S(6)} %copy.23.count, bf16[256,3072]{1,0:T(8,128)(2,1)} %x_ref.3, bf16[72,128,128]{2,1,0:T(8,128)(2,1)} %values_ref.5), custom_call_target="tpu_custom_call" | custom-call | flops 603979776 | bytes 3932450 | tf_op jit(solution)/shard_map/pallas_call | solution.py:413
  21.6 5.2 %shard_map.96 = (bf16[256,1536]{1,0:T(8,128)(2,1)}, bf16[16,2,16,256]{3,2,1,0:T(8,128)(2,1)}, bf16[256,768]{1,0:T(8,128)(2,1)}, bf16[256,768]{1,0:T(8,128)(2,1)}) custom-call(s32[2,72]{1,0:T(2,128)} %bitcast.28, s32[1]{0:T(128)S(6)} %copy.23.count, bf16[16,16,256]{2,1,0:T(8,128)(2,1)} %copy-done.8, bf16[72,128,128]{2,1,0:T(8,128)(2,1)} %values_ref.5, ...), custom_call_target="tpu_custom_call" | custom-call | flops 150994944 | bytes 4194594 | tf_op jit(solution)/shard_map/pallas_call | solution.py:413
  26.8 4.2 %all-to-all-start.1 = ((bf16[32,16,256]{2,1,0:T(8,128)(2,1)}), bf16[32,16,256]{2,1,0:T(8,128)(2,1)S(1)}, u32[]{:S(2)}, u32[]{:S(2)}) async-start(bf16[32,16,256]{2,1,0:T(8,128)(2,1)} %bitcast.26), calls=%async_computation.1 | async-start | bytes 524288 | tf_op jit(solution)/shard_map/all_to_all | solution.py:430
  31.1 1.7 %collective-permute-start.2 = (bf16[256,768]{1,0:T(8,128)(2,1)}, bf16[256,768]{1,0:T(8,128)(2,1)S(1)}, u32[]{:S(2)}, u32[]{:S(2)}) collective-permute-start(bf16[256,768]{1,0:T(8,128)(2,1)} %get-tuple-element.38), channel_id=1, source_target_pairs={{0,1},{1,0},{2,3},{3,2},{4,5},{5,4},{6,7},{7,6},{8,9},{9,8},{10,11... | collective-permute-start | bytes 1179656 | tf_op jit(solution)/shard_map/ppermute | solution.py:426
  33.1 1.3 copy.15.wt_ref.refs_2_
  35.3 4.4 %shard_map.97.refs_5_ = f32[512,1536]{1,0:T(8,128)} custom-call(bf16[512,1024]{1,0:T(8,128)(2,1)} %copy.15.wt_ref.refs_2_, bf16[256,1536]{1,0:T(8,128)(2,1)} %get-tuple-element.34.refs_0_, bf16[256,1536]{1,0:T(8,128)(2,1)} %copy-done.7), custom_call_target="tpu_custom_call" | custom-call | flops 805306368 | bytes 2621440 | tf_op jit(solution)/shard_map/pallas_call | solution.py:413
  39.7 5.9 %collective-permute-done.2.refs_7_ = bf16[256,768]{1,0:T(8,128)(2,1)S(1)} collective-permute-done((bf16[256,768]{1,0:T(8,128)(2,1)}, bf16[256,768]{1,0:T(8,128)(2,1)S(1)}, u32[]{:S(2)}, u32[]{:S(2)}) %collective-permute-start.2) | collective-permute-done | bytes 393248 | tf_op jit(solution)/shard_map/ppermute | solution.py:426
  46.4 7.1 %shard_map.98 = (bf16[512,768]{1,0:T(8,128)(2,1)}, bf16[512,1536]{1,0:T(8,128)(2,1)}, bf16[512,768]{1,0:T(8,128)(2,1)}, bf16[512,256]{1,0:T(8,128)(2,1)}, bf16[2...) custom-call(s32[1,256]{1,0:T(1,128)} %get-tuple-element.31.refs_0_.rep_ref, ...), custom_call_target="tpu_custom_call" | custom-call | flops 1610612736 | bytes 6685184 | tf_op jit(solution)/shard_map/pallas_call | solution.py:413
  54.2 7.1 %shard_map.99 = (bf16[512,768]{1,0:T(8,128)(2,1)}, bf16[512,1536]{1,0:T(8,128)(2,1)}, bf16[512,768]{1,0:T(8,128)(2,1)}, bf16[16,2,16,256]{3,2,1,0:T(8,128)(2,1)}...) custom-call(s32[1,256]{1,0:T(1,128)} %get-tuple-element.31.refs_0_.r, ...), custom_call_target="tpu_custom_call", output_to_operand_aliasing={{1}: (9, {}), {6}: (10, {}), {7}: (11, {})} | custom-call | flops 1610612736 | bytes 10093056 | tf_op jit(solution)/shard_map/pallas_call | solution.py:413
  61.3 5.3 %shard_map.102 = (f32[2,256,512]{2,1,0:T(8,128)}, bf16[2,256,512]{2,1,0:T(8,128)(2,1)}) custom-call(bf16[256,1536]{1,0:T(8,128)(2,1)} %get-tuple-element.34.refs_0_, bf16[256,1536]{1,0:T(8,128)(2,1)} %copy-done.7, bf16[512,768]{1,0:T(8,128)(2,1)} %get-tuple-element.53.refs_2_, bf16[512,768]{1,0:T(8,128)(2,1)} %get-tuple-element.54.refs_3_, ...), custom_call_target="tpu_custom_call" | custom-call | flops 1610612736 | bytes 4718592 | tf_op jit(solution)/shard_map/pallas_call | solution.py:413
  66.7 2.1 %collective-permute-done.6 = bf16[2,256,512]{2,1,0:T(8,128)(2,1)S(1)} collective-permute-done((bf16[2,256,512]{2,1,0:T(8,128)(2,1)}, bf16[2,256,512]{2,1,0:T(8,128)(2,1)S(1)}, u32[]{:S(2)}, u32[]{:S(2)}) %collective-permute-start.6) | collective-permute-done | bytes 524320 | tf_op jit(solution)/shard_map/ppermute | solution.py:578
  68.8 1.4 %convert_add_fusion = f32[2,256,512]{2,1,0:T(8,128)S(1)} fusion(f32[2,256,512]{2,1,0:T(8,128)} %get-tuple-element.57, bf16[2,256,512]{2,1,0:T(8,128)(2,1)S(1)} %collective-permute-done.6), kind=kLoop, calls=%fused_computation | loop fusion | flops 524288 | bytes 2621440 | tf_op jit(solution)/shard_map/add | solution.py:585
  70.2 1.5 %collective-permute-start.7 = (bf16[2,128,512]{2,1,0:T(8,128)(2,1)S(1)}, bf16[2,128,512]{2,1,0:T(8,128)(2,1)S(1)}, u32[]{:S(2)}, u32[]{:S(2)}) collective-permute-start(bf16[2,128,512]{2,1,0:T(8,128)(2,1)S(1)} %dynamic-slice_convert_fusion), channel_id=1, source_target_pairs={{0,4},{2,6},{4,0},{6,2},{8,12},{10,14},{12,8},{14,10},{16,20},{18,... | collective-permute-start | bytes 786440 | tf_op jit(solution)/shard_map/ppermute | solution.py:578
  71.7 6.9 %collective-permute-done.7 = bf16[2,128,512]{2,1,0:T(8,128)(2,1)S(1)} collective-permute-done((bf16[2,128,512]{2,1,0:T(8,128)(2,1)S(1)}, bf16[2,128,512]{2,1,0:T(8,128)(2,1)S(1)}, u32[]{:S(2)}, u32[]{:S(2)}) %collective-permute-start.7) | collective-permute-done | bytes 262176 | tf_op jit(solution)/shard_map/ppermute | solution.py:578
  78.8 3.6 %collective-permute-start.10 = (bf16[2,32,512]{2,1,0:T(8,128)(2,1)S(1)}, bf16[2,32,512]{2,1,0:T(8,128)(2,1)S(1)}, u32[]{:S(2)}, u32[]{:S(2)}) collective-permute-start(bf16[2,32,512]{2,1,0:T(8,128)(2,1)S(1)} %get-tuple-element.62), channel_id=1, source_target_pairs={{0,24},{2,26},{4,28},{6,30},{8,16},{10,18},{12,20},{14,22},{16,8},... | collective-permute-start | bytes 196616 | tf_op jit(solution)/shard_map/ppermute | solution.py:578
  83.2 1.2 collective-permute-start.4
  84.4 4.7 %all-to-all-start.2 = ((bf16[32,16,256]{2,1,0:T(8,128)(2,1)}), bf16[32,16,256]{2,1,0:T(8,128)(2,1)S(1)}, u32[]{:S(2)}, u32[]{:S(2)}) async-start(bf16[32,16,256]{2,1,0:T(8,128)(2,1)} %bitcast.25), calls=%async_computation.2 | async-start | bytes 524288 | tf_op jit(solution)/shard_map/all_to_all | solution.py:430
  89.1 1.8 %collective-permute-start.3 = (bf16[256,768]{1,0:T(8,128)(2,1)}, bf16[256,768]{1,0:T(8,128)(2,1)}, u32[]{:S(2)}, u32[]{:S(2)}) collective-permute-start(bf16[256,768]{1,0:T(8,128)(2,1)} %get-tuple-element.47), channel_id=1, source_target_pairs={{0,1},{1,0},{2,3},{3,2},{4,5},{5,4},{6,7},{7,6},{8,9},{9,8},{10,11... | collective-permute-start | bytes 1179656 | tf_op jit(solution)/shard_map/ppermute | solution.py:426
  91.3 1.8 %collective-permute-start.5 = (bf16[256,1536]{1,0:T(8,128)(2,1)S(1)}, bf16[256,1536]{1,0:T(8,128)(2,1)S(1)}, u32[]{:S(2)}, u32[]{:S(2)}) collective-permute-start(bf16[256,1536]{1,0:T(8,128)(2,1)S(1)} %copy-done.6), channel_id=1, source_target_pairs={{0,1},{1,0},{2,3},{3,2},{4,5},{5,4},{6,7},{7,6},{8,9},{9,8},{10,11... | collective-permute-start | bytes 2359304 | tf_op jit(solution)/shard_map/ppermute | solution.py:426
  93.1 12.8 %collective-permute-done.11 = bf16[32,512]{1,0:T(8,128)(2,1)S(1)} collective-permute-done((bf16[32,512]{1,0:T(8,128)(2,1)S(1)}, bf16[32,512]{1,0:T(8,128)(2,1)S(1)}, u32[]{:S(2)}, u32[]{:S(2)}) %collective-permute-start.11) | collective-permute-done | bytes 32800 | tf_op jit(solution)/shard_map/ppermute | solution.py:426
  105.9 1.3 collective-permute-start.12
  107.1 2.9 %collective-permute-start.13 = (bf16[32,512]{1,0:T(8,128)(2,1)S(1)}, bf16[32,512]{1,0:T(8,128)(2,1)S(1)}, u32[]{:S(2)}, u32[]{:S(2)}) collective-permute-start(bf16[32,512]{1,0:T(8,128)(2,1)S(1)} %get-tuple-element.60), channel_id=1, source_target_pairs={{0,16},{2,18},{4,20},{6,22},{8,24},{10,26},{12,28},{14,30},{16,0},... | collective-permute-start | bytes 98312 | tf_op jit(solution)/shard_map/ppermute | solution.py:578
  111.1 7.1 %shard_map.100 = (bf16[256,3072]{1,0:T(8,128)(2,1)}, bf16[16,16,256]{2,1,0:T(8,128)(2,1)}) custom-call(s32[2,72]{1,0:T(2,128)} %bitcast.29, s32[1]{0:T(128)S(6)} %copy.23.count, bf16[16,2,16,256]{3,2,1,0:T(8,128)(2,1)} %bitcast.23, bf16[72,128,128]{2,1,0:T(8,128)(2,1)} %values_ref.5, bf16[256,768]{1,0:T(8,128)(2,1)} %get-tuple-element.45.rest_0_, ...), custom_call_target="tpu_custom_call" | custom-call | flops 603979776 | bytes 4194594 | tf_op jit(solution)/shard_map/pallas_call | solution.py:413
  118.1 4.7 %all-to-all-start.3 = ((bf16[16,16,256]{2,1,0:T(8,128)(2,1)}), bf16[16,16,256]{2,1,0:T(8,128)(2,1)S(1)}, u32[]{:S(2)}, u32[]{:S(2)}) async-start(bf16[16,16,256]{2,1,0:T(8,128)(2,1)} %get-tuple-element.49), calls=%async_computation.3 | async-start | bytes 262144 | tf_op jit(solution)/shard_map/all_to_all | solution.py:430
  122.9 2.0 %collective-permute-start.15 = (bf16[128,512]{1,0:T(8,128)(2,1)S(1)}, bf16[128,512]{1,0:T(8,128)(2,1)S(1)}, u32[]{:S(2)}, u32[]{:S(2)}) collective-permute-start(bf16[128,512]{1,0:T(8,128)(2,1)S(1)} %pad_maximum_fusion), channel_id=1, source_target_pairs={{0,4},{2,6},{4,0},{6,2},{8,12},{10,14},{12,8},{14,10},{16,20},{18,... | collective-permute-start | bytes 393224 | tf_op jit(solution)/shard_map/ppermute | solution.py:578
  124.9 5.0 %collective-permute-done.15 = bf16[128,512]{1,0:T(8,128)(2,1)S(1)} collective-permute-done((bf16[128,512]{1,0:T(8,128)(2,1)S(1)}, bf16[128,512]{1,0:T(8,128)(2,1)S(1)}, u32[]{:S(2)}, u32[]{:S(2)}) %collective-permute-start.15) | collective-permute-done | bytes 131104 | tf_op jit(solution)/shard_map/ppermute | solution.py:578
  130.7 1.4 %copy-done.1 = bf16[256,3072]{1,0:T(8,128)(2,1)S(1)} copy-done((bf16[256,3072]{1,0:T(8,128)(2,1)S(1)}, bf16[256,3072]{1,0:T(8,128)(2,1)}, u32[]{:S(2)}) %copy-start.1) | copy-done | bytes 1572888
  132.1 2.1 %shard_map.101 = bf16[256,3072]{1,0:T(8,128)(2,1)} custom-call(s32[1,256]{1,0:T(1,128)S(1)} %copy-done.2, bf16[16,16,256]{2,1,0:T(8,128)(2,1)S(1)} %all-to-all-done.3.inc_ref, bf16[256,3072]{1,0:T(8,128)(2,1)S(1)} %copy-done.1, bf16[256,1536]{1,0:T(8,128)(2,1)S(1)} %copy-done, bf16[256,1536]{1,0:T(8,128)(2,1)S(1)} %collective-permute-done.5.rest_1_), custom_call_target="tpu_custom_call" | custom-call | flops 402653184 | bytes 3277312 | tf_op jit(solution)/shard_map/pallas_call | solution.py:413
  134.3 1.2 shard_map.103
  (57 shorter events, 7.4 us)
Async XLA Ops:
  4.1 30.3 %collective-permute-start = (bf16[256,1536]{1,0:T(8,128)(2,1)}, bf16[256,1536]{1,0:T(8,128)(2,1)S(1)}, u32[]{:S(2)}, u32[]{:S(2)}) collective-permute-start(bf16[256,1536]{1,0:T(8,128)(2,1)} %get-tuple-element.35), channel_id=1, source_target_pairs={{0,1},{1,0},{2,3},{3,2},{4,5},{5,4},{6,7},{7,6},{8,9},{9,8},{10,11... | collective-permute-start | bytes 2359304 | tf_op jit(solution)/shard_map/ppermute | solution.py:426
  7.1 13.8 %all-to-all-start = ((bf16[16,16,256]{2,1,0:T(8,128)(2,1)}), bf16[16,16,256]{2,1,0:T(8,128)(2,1)S(1)}, u32[]{:S(2)}, u32[]{:S(2)}) async-start(bf16[16,16,256]{2,1,0:T(8,128)(2,1)} %get-tuple-element.32), calls=%async_computation | async-start | bytes 262144 | tf_op jit(solution)/shard_map/all_to_all | solution.py:430
  20.5 12.7 %copy-start.3 = (bf16[2,512,512]{2,1,0:T(8,128)(2,1)S(1)}, bf16[2,512,512]{2,1,0:T(8,128)(2,1)}, u32[]{:S(2)}) copy-start(bf16[2,512,512]{2,1,0:T(8,128)(2,1)} %param.8) | copy-start | bytes 3145732
  26.8 18.8 %all-to-all-start.1 = ((bf16[32,16,256]{2,1,0:T(8,128)(2,1)}), bf16[32,16,256]{2,1,0:T(8,128)(2,1)S(1)}, u32[]{:S(2)}, u32[]{:S(2)}) async-start(bf16[32,16,256]{2,1,0:T(8,128)(2,1)} %bitcast.26), calls=%async_computation.1 | async-start | bytes 524288 | tf_op jit(solution)/shard_map/all_to_all | solution.py:430
  31.1 14.5 %collective-permute-start.2 = (bf16[256,768]{1,0:T(8,128)(2,1)}, bf16[256,768]{1,0:T(8,128)(2,1)S(1)}, u32[]{:S(2)}, u32[]{:S(2)}) collective-permute-start(bf16[256,768]{1,0:T(8,128)(2,1)} %get-tuple-element.38), channel_id=1, source_target_pairs={{0,1},{1,0},{2,3},{3,2},{4,5},{5,4},{6,7},{7,6},{8,9},{9,8},{10,11... | collective-permute-start | bytes 1179656 | tf_op jit(solution)/shard_map/ppermute | solution.py:426
  32.7 20.8 %collective-permute-start.1 = (bf16[256,768]{1,0:T(8,128)(2,1)}, bf16[256,768]{1,0:T(8,128)(2,1)S(1)}, u32[]{:S(2)}, u32[]{:S(2)}) collective-permute-start(bf16[256,768]{1,0:T(8,128)(2,1)} %get-tuple-element.37), channel_id=1, source_target_pairs={{0,1},{1,0},{2,3},{3,2},{4,5},{5,4},{6,7},{7,6},{8,9},{9,8},{10,11... | collective-permute-start | bytes 1179656 | tf_op jit(solution)/shard_map/ppermute | solution.py:426
  34.5 0.9 copy-start.7
  45.6 0.8 copy-start.10
  45.6 0.8 copy-start.4
  53.5 0.7 copy-start.9
  66.6 2.2 %collective-permute-start.6 = (bf16[2,256,512]{2,1,0:T(8,128)(2,1)}, bf16[2,256,512]{2,1,0:T(8,128)(2,1)S(1)}, u32[]{:S(2)}, u32[]{:S(2)}) collective-permute-start(bf16[2,256,512]{2,1,0:T(8,128)(2,1)} %get-tuple-element.58), channel_id=1, source_target_pairs={{0,2},{2,0},{4,6},{6,4},{8,10},{10,8},{12,14},{14,12},{16,18},{18,... | collective-permute-start | bytes 1572872 | tf_op jit(solution)/shard_map/ppermute | solution.py:578
  70.2 21.2 %copy-start.6 = (bf16[256,1536]{1,0:T(8,128)(2,1)S(1)}, bf16[256,1536]{1,0:T(8,128)(2,1)}, u32[]{:S(2)}) copy-start(bf16[256,1536]{1,0:T(8,128)(2,1)} %get-tuple-element.52) | copy-start | bytes 2359300
  70.2 8.4 %collective-permute-start.7 = (bf16[2,128,512]{2,1,0:T(8,128)(2,1)S(1)}, bf16[2,128,512]{2,1,0:T(8,128)(2,1)S(1)}, u32[]{:S(2)}, u32[]{:S(2)}) collective-permute-start(bf16[2,128,512]{2,1,0:T(8,128)(2,1)S(1)} %dynamic-slice_convert_fusion), channel_id=1, source_target_pairs={{0,4},{2,6},{4,0},{6,2},{8,12},{10,14},{12,8},{14,10},{16,20},{18,... | collective-permute-start | bytes 786440 | tf_op jit(solution)/shard_map/ppermute | solution.py:578
  78.8 12.2 %collective-permute-start.10 = (bf16[2,32,512]{2,1,0:T(8,128)(2,1)S(1)}, bf16[2,32,512]{2,1,0:T(8,128)(2,1)S(1)}, u32[]{:S(2)}, u32[]{:S(2)}) collective-permute-start(bf16[2,32,512]{2,1,0:T(8,128)(2,1)S(1)} %get-tuple-element.62), channel_id=1, source_target_pairs={{0,24},{2,26},{4,28},{6,30},{8,16},{10,18},{12,20},{14,22},{16,8},... | collective-permute-start | bytes 196616 | tf_op jit(solution)/shard_map/ppermute | solution.py:578
  82.3 8.6 %collective-permute-start.8 = (bf16[2,32,512]{2,1,0:T(8,128)(2,1)S(1)}, bf16[2,32,512]{2,1,0:T(8,128)(2,1)S(1)}, u32[]{:S(2)}, u32[]{:S(2)}) collective-permute-start(bf16[2,32,512]{2,1,0:T(8,128)(2,1)S(1)} %get-tuple-element.61), channel_id=1, source_target_pairs={{0,8},{2,10},{4,12},{6,14},{8,0},{10,2},{12,4},{14,6},{16,24},{18,... | collective-permute-start | bytes 196616 | tf_op jit(solution)/shard_map/ppermute | solution.py:578
  82.3 8.6 %collective-permute-start.9 = (bf16[2,32,512]{2,1,0:T(8,128)(2,1)S(1)}, bf16[2,32,512]{2,1,0:T(8,128)(2,1)S(1)}, u32[]{:S(2)}, u32[]{:S(2)}) collective-permute-start(bf16[2,32,512]{2,1,0:T(8,128)(2,1)S(1)} %get-tuple-element.63), channel_id=1, source_target_pairs={{0,16},{2,18},{4,20},{6,22},{8,24},{10,26},{12,28},{14,30},{16,0},... | collective-permute-start | bytes 196616 | tf_op jit(solution)/shard_map/ppermute | solution.py:578
  83.2 26.8 %collective-permute-start.4 = (bf16[256,768]{1,0:T(8,128)(2,1)}, bf16[256,768]{1,0:T(8,128)(2,1)S(1)}, u32[]{:S(2)}, u32[]{:S(2)}) collective-permute-start(bf16[256,768]{1,0:T(8,128)(2,1)} %get-tuple-element.48), channel_id=1, source_target_pairs={{0,1},{1,0},{2,3},{3,2},{4,5},{5,4},{6,7},{7,6},{8,9},{9,8},{10,11... | collective-permute-start | bytes 1179656 | tf_op jit(solution)/shard_map/ppermute | solution.py:426
  84.4 25.9 %all-to-all-start.2 = ((bf16[32,16,256]{2,1,0:T(8,128)(2,1)}), bf16[32,16,256]{2,1,0:T(8,128)(2,1)S(1)}, u32[]{:S(2)}, u32[]{:S(2)}) async-start(bf16[32,16,256]{2,1,0:T(8,128)(2,1)} %bitcast.25), calls=%async_computation.2 | async-start | bytes 524288 | tf_op jit(solution)/shard_map/all_to_all | solution.py:430
  89.1 21.2 %collective-permute-start.3 = (bf16[256,768]{1,0:T(8,128)(2,1)}, bf16[256,768]{1,0:T(8,128)(2,1)}, u32[]{:S(2)}, u32[]{:S(2)}) collective-permute-start(bf16[256,768]{1,0:T(8,128)(2,1)} %get-tuple-element.47), channel_id=1, source_target_pairs={{0,1},{1,0},{2,3},{3,2},{4,5},{5,4},{6,7},{7,6},{8,9},{9,8},{10,11... | collective-permute-start | bytes 1179656 | tf_op jit(solution)/shard_map/ppermute | solution.py:426
  91.0 14.9 %collective-permute-start.11 = (bf16[32,512]{1,0:T(8,128)(2,1)S(1)}, bf16[32,512]{1,0:T(8,128)(2,1)S(1)}, u32[]{:S(2)}, u32[]{:S(2)}) collective-permute-start(bf16[32,512]{1,0:T(8,128)(2,1)S(1)} %fusion.2), channel_id=1, source_target_pairs={{0,1},{1,0},{2,3},{3,2},{4,5},{5,4},{6,7},{7,6},{8,9},{9,8},{10,11... | collective-permute-start | bytes 98312 | tf_op jit(solution)/shard_map/ppermute | solution.py:426
  91.3 39.4 %collective-permute-start.5 = (bf16[256,1536]{1,0:T(8,128)(2,1)S(1)}, bf16[256,1536]{1,0:T(8,128)(2,1)S(1)}, u32[]{:S(2)}, u32[]{:S(2)}) collective-permute-start(bf16[256,1536]{1,0:T(8,128)(2,1)S(1)} %copy-done.6), channel_id=1, source_target_pairs={{0,1},{1,0},{2,3},{3,2},{4,5},{5,4},{6,7},{7,6},{8,9},{9,8},{10,11... | collective-permute-start | bytes 2359304 | tf_op jit(solution)/shard_map/ppermute | solution.py:426
  105.9 16.9 %collective-permute-start.12 = (bf16[32,512]{1,0:T(8,128)(2,1)S(1)}, bf16[32,512]{1,0:T(8,128)(2,1)S(1)}, u32[]{:S(2)}, u32[]{:S(2)}) collective-permute-start(bf16[32,512]{1,0:T(8,128)(2,1)S(1)} %get-tuple-element.60), channel_id=1, source_target_pairs={{0,8},{2,10},{4,12},{6,14},{8,0},{10,2},{12,4},{14,6},{16,24},{18,... | collective-permute-start | bytes 98312 | tf_op jit(solution)/shard_map/ppermute | solution.py:578
  107.1 15.7 %collective-permute-start.13 = (bf16[32,512]{1,0:T(8,128)(2,1)S(1)}, bf16[32,512]{1,0:T(8,128)(2,1)S(1)}, u32[]{:S(2)}, u32[]{:S(2)}) collective-permute-start(bf16[32,512]{1,0:T(8,128)(2,1)S(1)} %get-tuple-element.60), channel_id=1, source_target_pairs={{0,16},{2,18},{4,20},{6,22},{8,24},{10,26},{12,28},{14,30},{16,0},... | collective-permute-start | bytes 98312 | tf_op jit(solution)/shard_map/ppermute | solution.py:578
  110.0 0.7 copy-start.11
  110.0 12.8 %collective-permute-start.14 = (bf16[32,512]{1,0:T(8,128)(2,1)S(1)}, bf16[32,512]{1,0:T(8,128)(2,1)S(1)}, u32[]{:S(2)}, u32[]{:S(2)}) collective-permute-start(bf16[32,512]{1,0:T(8,128)(2,1)S(1)} %get-tuple-element.60), channel_id=1, source_target_pairs={{0,24},{2,26},{4,28},{6,30},{8,16},{10,18},{12,20},{14,22},{16,8},... | collective-permute-start | bytes 98312 | tf_op jit(solution)/shard_map/ppermute | solution.py:578
  110.4 0.7 copy-start.5
  111.1 19.7 %copy-start = (bf16[256,1536]{1,0:T(8,128)(2,1)S(1)}, bf16[256,1536]{1,0:T(8,128)(2,1)}, u32[]{:S(2)}) copy-start(bf16[256,1536]{1,0:T(8,128)(2,1)} %get-tuple-element.51.rest_0_) | copy-start | bytes 2359300
  111.1 19.7 %copy-start.2 = (s32[1,256]{1,0:T(1,128)S(1)}, s32[1,256]{1,0:T(1,128)}, u32[]{:S(2)}) copy-start(s32[1,256]{1,0:T(1,128)} %get-tuple-element.31.refs_0_.rep_ref) | copy-start | bytes 3076
  118.1 12.6 %all-to-all-start.3 = ((bf16[16,16,256]{2,1,0:T(8,128)(2,1)}), bf16[16,16,256]{2,1,0:T(8,128)(2,1)S(1)}, u32[]{:S(2)}, u32[]{:S(2)}) async-start(bf16[16,16,256]{2,1,0:T(8,128)(2,1)} %get-tuple-element.49), calls=%async_computation.3 | async-start | bytes 262144 | tf_op jit(solution)/shard_map/all_to_all | solution.py:430
  122.9 7.0 %collective-permute-start.15 = (bf16[128,512]{1,0:T(8,128)(2,1)S(1)}, bf16[128,512]{1,0:T(8,128)(2,1)S(1)}, u32[]{:S(2)}, u32[]{:S(2)}) collective-permute-start(bf16[128,512]{1,0:T(8,128)(2,1)S(1)} %pad_maximum_fusion), channel_id=1, source_target_pairs={{0,4},{2,6},{4,0},{6,2},{8,12},{10,14},{12,8},{14,10},{16,20},{18,... | collective-permute-start | bytes 393224 | tf_op jit(solution)/shard_map/ppermute | solution.py:578
  129.9 4.4 %collective-permute-start.16 = (bf16[256,512]{1,0:T(8,128)(2,1)S(1)}, bf16[256,512]{1,0:T(8,128)(2,1)S(1)}, u32[]{:S(2)}, u32[]{:S(2)}) collective-permute-start(bf16[256,512]{1,0:T(8,128)(2,1)S(1)} %constant_dynamic-update-slice_fusion.own_ref), channel_id=1, source_target_pairs={{0,2},{2,0},{4,6},{6,4},{8,10},{10,8},{12,14},{14,12},{16,18},{18,... | collective-permute-start | bytes 786440 | tf_op jit(solution)/shard_map/ppermute | solution.py:578
  130.7 1.4 %copy-start.1 = (bf16[256,3072]{1,0:T(8,128)(2,1)S(1)}, bf16[256,3072]{1,0:T(8,128)(2,1)}, u32[]{:S(2)}) copy-start(bf16[256,3072]{1,0:T(8,128)(2,1)} %get-tuple-element.50.back_ref) | copy-start | bytes 4718596
  (1 other events, 0.7 us)

commit v7 on v6

--- a/solution.py
+++ b/solution.py
@@ -580,18 +580,17 @@
     sends = [send]
     for k, r in enumerate(radices):
         unit = unit_of(radices, k)
-        cur = keep
-        for m in range(1, r):
-            cur = cur + swap(sends[m - 1], m * unit).astype(F32)
+        terms = [keep] + [swap(sends[m - 1], m * unit) for m in range(1, r)]
         if k + 1 == len(radices):
             break
-        size = cur.shape[1] // radices[k + 1]
+        size = keep.shape[1] // radices[k + 1]
         digit = lax.rem(d // unit_of(radices, k + 1), radices[k + 1])
-        pieces = [
-            lax.dynamic_slice_in_dim(cur, (digit ^ m) * size, size, 1)
-            for m in range(radices[k + 1])
-        ]
+        pieces = []
+        for m in range(radices[k + 1]):
+            cuts = [lax.dynamic_slice_in_dim(t, (digit ^ m) * size, size, 1) for t in terms]
+            pieces.append(sum(cut.astype(F32) for cut in cuts))
         keep, sends = pieces[0], [piece.astype(BF) for piece in pieces[1:]]
+    cur = sum(term.astype(F32) for term in terms)
     total = cur[0]
     for j in range(1, nf):
         total = total + to_peer(cur[j].astype(BF), j).astype(F32)

time: 136 us -> 136 us (level)
    convert_element_type x0 -> x2, other arithmetic: none -> 1.45 us  [local(): keep, sends = (pieces[0], [piece.astype(BF) for piece in pieces[1:]])]
    add x3 -> x1, other arithmetic: 1.49 us -> 0.05 us  [local(): cur = sum((term.astype(F32) for term in terms))]
    unnamed x27 -> x29, local copies, waits for them, and re-layouts: 5.22 us -> 5.27 us
where the time goes in v7:
time: 136 us; the launch traced here: 135 us
  Pallas kernels  49.7 us (37%)
  starting transfers between devices  42.2 us (31%)
  waiting for transfers between devices  33.9 us (25%)
  local copies, waits for them, and re-layouts  6.6 us (5%)
  between operations  1.56 us (1%)
  other arithmetic  1.52 us (1%)
    pallas_call x10, Pallas kernels, call(): pl.pallas_call(body, grid=grid, in_specs=[full(a) if p is None else p for...  49.7 us
    all_to_all x4, starting transfers between devices, exchange(): return lax.all_to_all(flat, axes, 0, 0, tiled=True).reshape(x.shape)  19.5 us
    ppermute x7, waiting for transfers between devices, to_peer(): return lax.ppermute(x, 'feat', [(i, (i + j) % nf) for i in range(nf)])  18.6 us
    ppermute x10, waiting for transfers between devices, swap(): return lax.ppermute(x, 'dom', [(i, i ^ b) for i in range(nd)])  14 us
    ppermute x10, starting transfers between devices, swap(): return lax.ppermute(x, 'dom', [(i, i ^ b) for i in range(nd)])  12.5 us
    ppermute x7, starting transfers between devices, to_peer(): return lax.ppermute(x, 'feat', [(i, (i + j) % nf) for i in range(nf)])  10.2 us
    unnamed x29, local copies, waits for them, and re-layouts  5.27 us
  transfers between devices with their start and end apart: 21, of which 7 were waited for; matrix products, arithmetic and copies ran while one was open for 1% of the time, Pallas kernels for 24%

profile of v7, /device:TPU:0, one launch (start us, length us, event | category | flops | bytes accessed | tf_op | source)
XLA Modules:
  0.0 135.4 jit_solution(1686911829937654969)
XLA Ops:
  0.6 3.5 %shard_map.94 = (bf16[16,16,256]{2,1,0:T(8,128)(2,1)}, s32[1,256]{1,0:T(1,128)}, bf16[256,1536]{1,0:T(8,128)(2,1)}, bf16[256,1536]{1,0:T(8,128)(2,1)}) custom-call(bf16[256,3072]{1,0:T(8,128)(2,1)} %x_ref.3, s32[1,16,16]{2,1,0:T(8,128)} %replica.1), custom_call_target="tpu_custom_call" | custom-call | flops 402653184 | bytes 1573376 | tf_op jit(solution)/shard_map/pallas_call | solution.py:413
  4.1 3.0 %collective-permute-start = (bf16[256,1536]{1,0:T(8,128)(2,1)}, bf16[256,1536]{1,0:T(8,128)(2,1)S(1)}, u32[]{:S(2)}, u32[]{:S(2)}) collective-permute-start(bf16[256,1536]{1,0:T(8,128)(2,1)} %get-tuple-element.35), channel_id=1, source_target_pairs={{0,1},{1,0},{2,3},{3,2},{4,5},{5,4},{6,7},{7,6},{8,9},{9,8},{10,11... | collective-permute-start | bytes 2359304 | tf_op jit(solution)/shard_map/ppermute | solution.py:426
  7.1 5.9 %all-to-all-start = ((bf16[16,16,256]{2,1,0:T(8,128)(2,1)}), bf16[16,16,256]{2,1,0:T(8,128)(2,1)S(1)}, u32[]{:S(2)}, u32[]{:S(2)}) async-start(bf16[16,16,256]{2,1,0:T(8,128)(2,1)} %get-tuple-element.32), calls=%async_computation | async-start | bytes 262144 | tf_op jit(solution)/shard_map/all_to_all | solution.py:430
  13.7 6.8 %shard_map.95.own_ref = bf16[256,3328]{1,0:T(8,128)(2,1)} custom-call(s32[2,72]{1,0:T(2,128)} %bitcast.26, s32[1]{0:T(128)S(6)} %copy.23.count, bf16[256,3072]{1,0:T(8,128)(2,1)} %x_ref.3, bf16[72,128,128]{2,1,0:T(8,128)(2,1)} %values_ref.5), custom_call_target="tpu_custom_call" | custom-call | flops 603979776 | bytes 3932450 | tf_op jit(solution)/shard_map/pallas_call | solution.py:413
  21.6 5.2 %shard_map.96 = (bf16[256,1536]{1,0:T(8,128)(2,1)}, bf16[16,2,16,256]{3,2,1,0:T(8,128)(2,1)}, bf16[256,768]{1,0:T(8,128)(2,1)}, bf16[256,768]{1,0:T(8,128)(2,1)}) custom-call(s32[2,72]{1,0:T(2,128)} %bitcast.27, s32[1]{0:T(128)S(6)} %copy.23.count, bf16[16,16,256]{2,1,0:T(8,128)(2,1)} %copy-done.8, bf16[72,128,128]{2,1,0:T(8,128)(2,1)} %values_ref.5, ...), custom_call_target="tpu_custom_call" | custom-call | flops 150994944 | bytes 4194594 | tf_op jit(solution)/shard_map/pallas_call | solution.py:413
  26.8 4.2 %all-to-all-start.1 = ((bf16[32,16,256]{2,1,0:T(8,128)(2,1)}), bf16[32,16,256]{2,1,0:T(8,128)(2,1)S(1)}, u32[]{:S(2)}, u32[]{:S(2)}) async-start(bf16[32,16,256]{2,1,0:T(8,128)(2,1)} %bitcast.25), calls=%async_computation.1 | async-start | bytes 524288 | tf_op jit(solution)/shard_map/all_to_all | solution.py:430
  31.1 1.7 %collective-permute-start.2 = (bf16[256,768]{1,0:T(8,128)(2,1)}, bf16[256,768]{1,0:T(8,128)(2,1)S(1)}, u32[]{:S(2)}, u32[]{:S(2)}) collective-permute-start(bf16[256,768]{1,0:T(8,128)(2,1)} %get-tuple-element.38), channel_id=1, source_target_pairs={{0,1},{1,0},{2,3},{3,2},{4,5},{5,4},{6,7},{7,6},{8,9},{9,8},{10,11... | collective-permute-start | bytes 1179656 | tf_op jit(solution)/shard_map/ppermute | solution.py:426
  33.1 1.3 copy.15.wt_ref.refs_2_
  35.3 4.4 %shard_map.97.refs_5_ = f32[512,1536]{1,0:T(8,128)} custom-call(bf16[512,1024]{1,0:T(8,128)(2,1)} %copy.15.wt_ref.refs_2_, bf16[256,1536]{1,0:T(8,128)(2,1)} %get-tuple-element.34.refs_0_, bf16[256,1536]{1,0:T(8,128)(2,1)} %copy-done.7), custom_call_target="tpu_custom_call" | custom-call | flops 805306368 | bytes 2621440 | tf_op jit(solution)/shard_map/pallas_call | solution.py:413
  39.7 5.9 %collective-permute-done.2.refs_7_ = bf16[256,768]{1,0:T(8,128)(2,1)S(1)} collective-permute-done((bf16[256,768]{1,0:T(8,128)(2,1)}, bf16[256,768]{1,0:T(8,128)(2,1)S(1)}, u32[]{:S(2)}, u32[]{:S(2)}) %collective-permute-start.2) | collective-permute-done | bytes 393248 | tf_op jit(solution)/shard_map/ppermute | solution.py:426
  46.5 7.0 %shard_map.98 = (bf16[512,768]{1,0:T(8,128)(2,1)}, bf16[512,1536]{1,0:T(8,128)(2,1)}, bf16[512,768]{1,0:T(8,128)(2,1)}, bf16[512,256]{1,0:T(8,128)(2,1)}, bf16[2...) custom-call(s32[1,256]{1,0:T(1,128)} %get-tuple-element.31.refs_0_.rep_ref, ...), custom_call_target="tpu_custom_call" | custom-call | flops 1610612736 | bytes 6685184 | tf_op jit(solution)/shard_map/pallas_call | solution.py:413
  54.3 7.1 %shard_map.99 = (bf16[512,768]{1,0:T(8,128)(2,1)}, bf16[512,1536]{1,0:T(8,128)(2,1)}, bf16[512,768]{1,0:T(8,128)(2,1)}, bf16[16,2,16,256]{3,2,1,0:T(8,128)(2,1)}...) custom-call(s32[1,256]{1,0:T(1,128)} %get-tuple-element.31.refs_0_.r, ...), custom_call_target="tpu_custom_call", output_to_operand_aliasing={{1}: (9, {}), {6}: (10, {}), {7}: (11, {})} | custom-call | flops 1610612736 | bytes 10093056 | tf_op jit(solution)/shard_map/pallas_call | solution.py:413
  61.3 5.3 %shard_map.102 = (f32[2,256,512]{2,1,0:T(8,128)}, bf16[2,256,512]{2,1,0:T(8,128)(2,1)}) custom-call(bf16[256,1536]{1,0:T(8,128)(2,1)} %get-tuple-element.34.refs_0_, bf16[256,1536]{1,0:T(8,128)(2,1)} %copy-done.7, bf16[512,768]{1,0:T(8,128)(2,1)} %get-tuple-element.53.refs_2_, bf16[512,768]{1,0:T(8,128)(2,1)} %get-tuple-element.54.refs_3_, ...), custom_call_target="tpu_custom_call" | custom-call | flops 1610612736 | bytes 4718592 | tf_op jit(solution)/shard_map/pallas_call | solution.py:413
  66.7 2.1 %collective-permute-done.6 = bf16[2,256,512]{2,1,0:T(8,128)(2,1)S(1)} collective-permute-done((bf16[2,256,512]{2,1,0:T(8,128)(2,1)}, bf16[2,256,512]{2,1,0:T(8,128)(2,1)S(1)}, u32[]{:S(2)}, u32[]{:S(2)}) %collective-permute-start.6) | collective-permute-done | bytes 524320 | tf_op jit(solution)/shard_map/ppermute | solution.py:578
  68.8 1.4 %add_convert_fusion = (bf16[2,128,512]{2,1,0:T(8,128)(2,1)S(1)}, f32[2,128,512]{2,1,0:T(8,128)S(1)}) fusion(f32[2,256,512]{2,1,0:T(8,128)} %get-tuple-element.57, s32[]{:T(128)S(6)} %select_n.36, bf16[2,256,512]{2,1,0:T(8,128)(2,1)S(1)} %collective-permute-done.6, s32[]{:T(128)S(6)} %select_n.33), kind=kLoop, calls=%fused_computation | loop fusion | flops 655360 | bytes 2359304 | tf_op jit(solution)/shard_map/convert_element_type | solution.py:592
  70.2 1.5 %collective-permute-start.7 = (bf16[2,128,512]{2,1,0:T(8,128)(2,1)S(1)}, bf16[2,128,512]{2,1,0:T(8,128)(2,1)S(1)}, u32[]{:S(2)}, u32[]{:S(2)}) collective-permute-start(bf16[2,128,512]{2,1,0:T(8,128)(2,1)S(1)} %get-tuple-element.61), channel_id=1, source_target_pairs={{0,4},{2,6},{4,0},{6,2},{8,12},{10,14},{12,8},{14,10},{16,20},{18,... | collective-permute-start | bytes 786440 | tf_op jit(solution)/shard_map/ppermute | solution.py:578
  71.7 6.9 %collective-permute-done.7 = bf16[2,128,512]{2,1,0:T(8,128)(2,1)S(1)} collective-permute-done((bf16[2,128,512]{2,1,0:T(8,128)(2,1)S(1)}, bf16[2,128,512]{2,1,0:T(8,128)(2,1)S(1)}, u32[]{:S(2)}, u32[]{:S(2)}) %collective-permute-start.7) | collective-permute-done | bytes 262176 | tf_op jit(solution)/shard_map/ppermute | solution.py:578
  78.7 3.5 %collective-permute-start.10 = (bf16[2,32,512]{2,1,0:T(8,128)(2,1)S(1)}, bf16[2,32,512]{2,1,0:T(8,128)(2,1)S(1)}, u32[]{:S(2)}, u32[]{:S(2)}) collective-permute-start(bf16[2,32,512]{2,1,0:T(8,128)(2,1)S(1)} %get-tuple-element.64), channel_id=1, source_target_pairs={{0,24},{2,26},{4,28},{6,30},{8,16},{10,18},{12,20},{14,22},{16,8},... | collective-permute-start | bytes 196616 | tf_op jit(solution)/shard_map/ppermute | solution.py:578
  83.1 1.1 collective-permute-start.4
  84.3 4.7 %all-to-all-start.2 = ((bf16[32,16,256]{2,1,0:T(8,128)(2,1)}), bf16[32,16,256]{2,1,0:T(8,128)(2,1)S(1)}, u32[]{:S(2)}, u32[]{:S(2)}) async-start(bf16[32,16,256]{2,1,0:T(8,128)(2,1)} %bitcast.5), calls=%async_computation.2 | async-start | bytes 524288 | tf_op jit(solution)/shard_map/all_to_all | solution.py:430
  89.0 1.8 %collective-permute-start.3 = (bf16[256,768]{1,0:T(8,128)(2,1)S(1)}, bf16[256,768]{1,0:T(8,128)(2,1)}, u32[]{:S(2)}, u32[]{:S(2)}) collective-permute-start(bf16[256,768]{1,0:T(8,128)(2,1)S(1)} %copy-done.12), channel_id=1, source_target_pairs={{0,1},{1,0},{2,3},{3,2},{4,5},{5,4},{6,7},{7,6},{8,9},{9,8},{10,11... | collective-permute-start | bytes 1179656 | tf_op jit(solution)/shard_map/ppermute | solution.py:426
  91.3 1.8 %collective-permute-start.5 = (bf16[256,1536]{1,0:T(8,128)(2,1)S(1)}, bf16[256,1536]{1,0:T(8,128)(2,1)S(1)}, u32[]{:S(2)}, u32[]{:S(2)}) collective-permute-start(bf16[256,1536]{1,0:T(8,128)(2,1)S(1)} %copy-done.6), channel_id=1, source_target_pairs={{0,1},{1,0},{2,3},{3,2},{4,5},{5,4},{6,7},{7,6},{8,9},{9,8},{10,11... | collective-permute-start | bytes 2359304 | tf_op jit(solution)/shard_map/ppermute | solution.py:426
  93.0 12.7 %collective-permute-done.11 = bf16[32,512]{1,0:T(8,128)(2,1)S(1)} collective-permute-done((bf16[32,512]{1,0:T(8,128)(2,1)S(1)}, bf16[32,512]{1,0:T(8,128)(2,1)S(1)}, u32[]{:S(2)}, u32[]{:S(2)}) %collective-permute-start.11) | collective-permute-done | bytes 32800 | tf_op jit(solution)/shard_map/ppermute | solution.py:426
  105.8 1.3 collective-permute-start.12
  107.1 2.8 %collective-permute-start.13 = (bf16[32,512]{1,0:T(8,128)(2,1)S(1)}, bf16[32,512]{1,0:T(8,128)(2,1)S(1)}, u32[]{:S(2)}, u32[]{:S(2)}) collective-permute-start(bf16[32,512]{1,0:T(8,128)(2,1)S(1)} %get-tuple-element.60), channel_id=1, source_target_pairs={{0,16},{2,18},{4,20},{6,22},{8,24},{10,26},{12,28},{14,30},{16,0},... | collective-permute-start | bytes 98312 | tf_op jit(solution)/shard_map/ppermute | solution.py:578
  110.9 7.1 %shard_map.100 = (bf16[256,3072]{1,0:T(8,128)(2,1)}, bf16[16,16,256]{2,1,0:T(8,128)(2,1)}) custom-call(s32[2,72]{1,0:T(2,128)} %bitcast.28, s32[1]{0:T(128)S(6)} %copy.23.count, bf16[16,2,16,256]{3,2,1,0:T(8,128)(2,1)} %bitcast.23, bf16[72,128,128]{2,1,0:T(8,128)(2,1)} %values_ref.5, bf16[256,768]{1,0:T(8,128)(2,1)} %get-tuple-element.45.rest_0_, ...), custom_call_target="tpu_custom_call" | custom-call | flops 603979776 | bytes 4194594 | tf_op jit(solution)/shard_map/pallas_call | solution.py:413
  118.0 4.7 %all-to-all-start.3 = ((bf16[16,16,256]{2,1,0:T(8,128)(2,1)}), bf16[16,16,256]{2,1,0:T(8,128)(2,1)S(1)}, u32[]{:S(2)}, u32[]{:S(2)}) async-start(bf16[16,16,256]{2,1,0:T(8,128)(2,1)} %get-tuple-element.49), calls=%async_computation.3 | async-start | bytes 262144 | tf_op jit(solution)/shard_map/all_to_all | solution.py:430
  122.8 2.0 %collective-permute-start.15 = (bf16[128,512]{1,0:T(8,128)(2,1)S(1)}, bf16[128,512]{1,0:T(8,128)(2,1)S(1)}, u32[]{:S(2)}, u32[]{:S(2)}) collective-permute-start(bf16[128,512]{1,0:T(8,128)(2,1)S(1)} %pad_maximum_fusion), channel_id=1, source_target_pairs={{0,4},{2,6},{4,0},{6,2},{8,12},{10,14},{12,8},{14,10},{16,20},{18,... | collective-permute-start | bytes 393224 | tf_op jit(solution)/shard_map/ppermute | solution.py:578
  124.8 5.0 %collective-permute-done.15 = bf16[128,512]{1,0:T(8,128)(2,1)S(1)} collective-permute-done((bf16[128,512]{1,0:T(8,128)(2,1)S(1)}, bf16[128,512]{1,0:T(8,128)(2,1)S(1)}, u32[]{:S(2)}, u32[]{:S(2)}) %collective-permute-start.15) | collective-permute-done | bytes 131104 | tf_op jit(solution)/shard_map/ppermute | solution.py:578
  130.6 1.4 %copy-done.1 = bf16[256,3072]{1,0:T(8,128)(2,1)S(1)} copy-done((bf16[256,3072]{1,0:T(8,128)(2,1)S(1)}, bf16[256,3072]{1,0:T(8,128)(2,1)}, u32[]{:S(2)}) %copy-start.1) | copy-done | bytes 1572888
  132.0 2.2 %shard_map.101 = bf16[256,3072]{1,0:T(8,128)(2,1)} custom-call(s32[1,256]{1,0:T(1,128)S(1)} %copy-done.2, bf16[16,16,256]{2,1,0:T(8,128)(2,1)S(1)} %all-to-all-done.3.inc_ref, bf16[256,3072]{1,0:T(8,128)(2,1)S(1)} %copy-done.1, bf16[256,1536]{1,0:T(8,128)(2,1)S(1)} %copy-done, bf16[256,1536]{1,0:T(8,128)(2,1)S(1)} %collective-permute-done.5.rest_1_), custom_call_target="tpu_custom_call" | custom-call | flops 402653184 | bytes 3277312 | tf_op jit(solution)/shard_map/pallas_call | solution.py:413
  134.2 1.2 shard_map.103
  (57 shorter events, 7.4 us)
Async XLA Ops:
  4.1 30.3 %collective-permute-start = (bf16[256,1536]{1,0:T(8,128)(2,1)}, bf16[256,1536]{1,0:T(8,128)(2,1)S(1)}, u32[]{:S(2)}, u32[]{:S(2)}) collective-permute-start(bf16[256,1536]{1,0:T(8,128)(2,1)} %get-tuple-element.35), channel_id=1, source_target_pairs={{0,1},{1,0},{2,3},{3,2},{4,5},{5,4},{6,7},{7,6},{8,9},{9,8},{10,11... | collective-permute-start | bytes 2359304 | tf_op jit(solution)/shard_map/ppermute | solution.py:426
  7.1 13.8 %all-to-all-start = ((bf16[16,16,256]{2,1,0:T(8,128)(2,1)}), bf16[16,16,256]{2,1,0:T(8,128)(2,1)S(1)}, u32[]{:S(2)}, u32[]{:S(2)}) async-start(bf16[16,16,256]{2,1,0:T(8,128)(2,1)} %get-tuple-element.32), calls=%async_computation | async-start | bytes 262144 | tf_op jit(solution)/shard_map/all_to_all | solution.py:430
  20.4 12.7 %copy-start.3 = (bf16[2,512,512]{2,1,0:T(8,128)(2,1)S(1)}, bf16[2,512,512]{2,1,0:T(8,128)(2,1)}, u32[]{:S(2)}) copy-start(bf16[2,512,512]{2,1,0:T(8,128)(2,1)} %param.8) | copy-start | bytes 3145732
  26.8 18.8 %all-to-all-start.1 = ((bf16[32,16,256]{2,1,0:T(8,128)(2,1)}), bf16[32,16,256]{2,1,0:T(8,128)(2,1)S(1)}, u32[]{:S(2)}, u32[]{:S(2)}) async-start(bf16[32,16,256]{2,1,0:T(8,128)(2,1)} %bitcast.25), calls=%async_computation.1 | async-start | bytes 524288 | tf_op jit(solution)/shard_map/all_to_all | solution.py:430
  31.1 14.5 %collective-permute-start.2 = (bf16[256,768]{1,0:T(8,128)(2,1)}, bf16[256,768]{1,0:T(8,128)(2,1)S(1)}, u32[]{:S(2)}, u32[]{:S(2)}) collective-permute-start(bf16[256,768]{1,0:T(8,128)(2,1)} %get-tuple-element.38), channel_id=1, source_target_pairs={{0,1},{1,0},{2,3},{3,2},{4,5},{5,4},{6,7},{7,6},{8,9},{9,8},{10,11... | collective-permute-start | bytes 1179656 | tf_op jit(solution)/shard_map/ppermute | solution.py:426
  32.7 20.8 %collective-permute-start.1 = (bf16[256,768]{1,0:T(8,128)(2,1)}, bf16[256,768]{1,0:T(8,128)(2,1)S(1)}, u32[]{:S(2)}, u32[]{:S(2)}) collective-permute-start(bf16[256,768]{1,0:T(8,128)(2,1)} %get-tuple-element.37), channel_id=1, source_target_pairs={{0,1},{1,0},{2,3},{3,2},{4,5},{5,4},{6,7},{7,6},{8,9},{9,8},{10,11... | collective-permute-start | bytes 1179656 | tf_op jit(solution)/shard_map/ppermute | solution.py:426
  34.5 0.9 copy-start.7
  45.6 0.8 copy-start.10
  45.6 0.9 copy-start.4
  53.5 0.7 copy-start.9
  66.6 2.2 %collective-permute-start.6 = (bf16[2,256,512]{2,1,0:T(8,128)(2,1)}, bf16[2,256,512]{2,1,0:T(8,128)(2,1)S(1)}, u32[]{:S(2)}, u32[]{:S(2)}) collective-permute-start(bf16[2,256,512]{2,1,0:T(8,128)(2,1)} %get-tuple-element.58), channel_id=1, source_target_pairs={{0,2},{2,0},{4,6},{6,4},{8,10},{10,8},{12,14},{14,12},{16,18},{18,... | collective-permute-start | bytes 1572872 | tf_op jit(solution)/shard_map/ppermute | solution.py:578
  68.8 20.2 %copy-start.12 = (bf16[256,768]{1,0:T(8,128)(2,1)S(1)}, bf16[256,768]{1,0:T(8,128)(2,1)}, u32[]{:S(2)}) copy-start(bf16[256,768]{1,0:T(8,128)(2,1)} %get-tuple-element.47) | copy-start | bytes 1179652
  70.2 21.0 %copy-start.6 = (bf16[256,1536]{1,0:T(8,128)(2,1)S(1)}, bf16[256,1536]{1,0:T(8,128)(2,1)}, u32[]{:S(2)}) copy-start(bf16[256,1536]{1,0:T(8,128)(2,1)} %get-tuple-element.52) | copy-start | bytes 2359300
  70.2 8.4 %collective-permute-start.7 = (bf16[2,128,512]{2,1,0:T(8,128)(2,1)S(1)}, bf16[2,128,512]{2,1,0:T(8,128)(2,1)S(1)}, u32[]{:S(2)}, u32[]{:S(2)}) collective-permute-start(bf16[2,128,512]{2,1,0:T(8,128)(2,1)S(1)} %get-tuple-element.61), channel_id=1, source_target_pairs={{0,4},{2,6},{4,0},{6,2},{8,12},{10,14},{12,8},{14,10},{16,20},{18,... | collective-permute-start | bytes 786440 | tf_op jit(solution)/shard_map/ppermute | solution.py:578
  78.7 12.2 %collective-permute-start.10 = (bf16[2,32,512]{2,1,0:T(8,128)(2,1)S(1)}, bf16[2,32,512]{2,1,0:T(8,128)(2,1)S(1)}, u32[]{:S(2)}, u32[]{:S(2)}) collective-permute-start(bf16[2,32,512]{2,1,0:T(8,128)(2,1)S(1)} %get-tuple-element.64), channel_id=1, source_target_pairs={{0,24},{2,26},{4,28},{6,30},{8,16},{10,18},{12,20},{14,22},{16,8},... | collective-permute-start | bytes 196616 | tf_op jit(solution)/shard_map/ppermute | solution.py:578
  82.2 8.7 %collective-permute-start.8 = (bf16[2,32,512]{2,1,0:T(8,128)(2,1)S(1)}, bf16[2,32,512]{2,1,0:T(8,128)(2,1)S(1)}, u32[]{:S(2)}, u32[]{:S(2)}) collective-permute-start(bf16[2,32,512]{2,1,0:T(8,128)(2,1)S(1)} %get-tuple-element.63), channel_id=1, source_target_pairs={{0,8},{2,10},{4,12},{6,14},{8,0},{10,2},{12,4},{14,6},{16,24},{18,... | collective-permute-start | bytes 196616 | tf_op jit(solution)/shard_map/ppermute | solution.py:578
  82.2 8.7 %collective-permute-start.9 = (bf16[2,32,512]{2,1,0:T(8,128)(2,1)S(1)}, bf16[2,32,512]{2,1,0:T(8,128)(2,1)S(1)}, u32[]{:S(2)}, u32[]{:S(2)}) collective-permute-start(bf16[2,32,512]{2,1,0:T(8,128)(2,1)S(1)} %get-tuple-element.65), channel_id=1, source_target_pairs={{0,16},{2,18},{4,20},{6,22},{8,24},{10,26},{12,28},{14,30},{16,0},... | collective-permute-start | bytes 196616 | tf_op jit(solution)/shard_map/ppermute | solution.py:578
  83.1 26.8 %collective-permute-start.4 = (bf16[256,768]{1,0:T(8,128)(2,1)}, bf16[256,768]{1,0:T(8,128)(2,1)S(1)}, u32[]{:S(2)}, u32[]{:S(2)}) collective-permute-start(bf16[256,768]{1,0:T(8,128)(2,1)} %get-tuple-element.48), channel_id=1, source_target_pairs={{0,1},{1,0},{2,3},{3,2},{4,5},{5,4},{6,7},{7,6},{8,9},{9,8},{10,11... | collective-permute-start | bytes 1179656 | tf_op jit(solution)/shard_map/ppermute | solution.py:426
  84.3 25.9 %all-to-all-start.2 = ((bf16[32,16,256]{2,1,0:T(8,128)(2,1)}), bf16[32,16,256]{2,1,0:T(8,128)(2,1)S(1)}, u32[]{:S(2)}, u32[]{:S(2)}) async-start(bf16[32,16,256]{2,1,0:T(8,128)(2,1)} %bitcast.5), calls=%async_computation.2 | async-start | bytes 524288 | tf_op jit(solution)/shard_map/all_to_all | solution.py:430
  89.0 21.2 %collective-permute-start.3 = (bf16[256,768]{1,0:T(8,128)(2,1)S(1)}, bf16[256,768]{1,0:T(8,128)(2,1)}, u32[]{:S(2)}, u32[]{:S(2)}) collective-permute-start(bf16[256,768]{1,0:T(8,128)(2,1)S(1)} %copy-done.12), channel_id=1, source_target_pairs={{0,1},{1,0},{2,3},{3,2},{4,5},{5,4},{6,7},{7,6},{8,9},{9,8},{10,11... | collective-permute-start | bytes 1179656 | tf_op jit(solution)/shard_map/ppermute | solution.py:426
  90.9 14.8 %collective-permute-start.11 = (bf16[32,512]{1,0:T(8,128)(2,1)S(1)}, bf16[32,512]{1,0:T(8,128)(2,1)S(1)}, u32[]{:S(2)}, u32[]{:S(2)}) collective-permute-start(bf16[32,512]{1,0:T(8,128)(2,1)S(1)} %fusion.2), channel_id=1, source_target_pairs={{0,1},{1,0},{2,3},{3,2},{4,5},{5,4},{6,7},{7,6},{8,9},{9,8},{10,11... | collective-permute-start | bytes 98312 | tf_op jit(solution)/shard_map/ppermute | solution.py:426
  91.3 39.3 %collective-permute-start.5 = (bf16[256,1536]{1,0:T(8,128)(2,1)S(1)}, bf16[256,1536]{1,0:T(8,128)(2,1)S(1)}, u32[]{:S(2)}, u32[]{:S(2)}) collective-permute-start(bf16[256,1536]{1,0:T(8,128)(2,1)S(1)} %copy-done.6), channel_id=1, source_target_pairs={{0,1},{1,0},{2,3},{3,2},{4,5},{5,4},{6,7},{7,6},{8,9},{9,8},{10,11... | collective-permute-start | bytes 2359304 | tf_op jit(solution)/shard_map/ppermute | solution.py:426
  105.8 16.9 %collective-permute-start.12 = (bf16[32,512]{1,0:T(8,128)(2,1)S(1)}, bf16[32,512]{1,0:T(8,128)(2,1)S(1)}, u32[]{:S(2)}, u32[]{:S(2)}) collective-permute-start(bf16[32,512]{1,0:T(8,128)(2,1)S(1)} %get-tuple-element.60), channel_id=1, source_target_pairs={{0,8},{2,10},{4,12},{6,14},{8,0},{10,2},{12,4},{14,6},{16,24},{18,... | collective-permute-start | bytes 98312 | tf_op jit(solution)/shard_map/ppermute | solution.py:578
  107.1 15.6 %collective-permute-start.13 = (bf16[32,512]{1,0:T(8,128)(2,1)S(1)}, bf16[32,512]{1,0:T(8,128)(2,1)S(1)}, u32[]{:S(2)}, u32[]{:S(2)}) collective-permute-start(bf16[32,512]{1,0:T(8,128)(2,1)S(1)} %get-tuple-element.60), channel_id=1, source_target_pairs={{0,16},{2,18},{4,20},{6,22},{8,24},{10,26},{12,28},{14,30},{16,0},... | collective-permute-start | bytes 98312 | tf_op jit(solution)/shard_map/ppermute | solution.py:578
  109.9 0.7 copy-start.11
  109.9 12.8 %collective-permute-start.14 = (bf16[32,512]{1,0:T(8,128)(2,1)S(1)}, bf16[32,512]{1,0:T(8,128)(2,1)S(1)}, u32[]{:S(2)}, u32[]{:S(2)}) collective-permute-start(bf16[32,512]{1,0:T(8,128)(2,1)S(1)} %get-tuple-element.60), channel_id=1, source_target_pairs={{0,24},{2,26},{4,28},{6,30},{8,16},{10,18},{12,20},{14,22},{16,8},... | collective-permute-start | bytes 98312 | tf_op jit(solution)/shard_map/ppermute | solution.py:578
  110.9 19.7 %copy-start = (bf16[256,1536]{1,0:T(8,128)(2,1)S(1)}, bf16[256,1536]{1,0:T(8,128)(2,1)}, u32[]{:S(2)}) copy-start(bf16[256,1536]{1,0:T(8,128)(2,1)} %get-tuple-element.51.rest_0_) | copy-start | bytes 2359300
  110.9 19.7 %copy-start.2 = (s32[1,256]{1,0:T(1,128)S(1)}, s32[1,256]{1,0:T(1,128)}, u32[]{:S(2)}) copy-start(s32[1,256]{1,0:T(1,128)} %get-tuple-element.31.refs_0_.rep_ref) | copy-start | bytes 3076
  118.0 12.6 %all-to-all-start.3 = ((bf16[16,16,256]{2,1,0:T(8,128)(2,1)}), bf16[16,16,256]{2,1,0:T(8,128)(2,1)S(1)}, u32[]{:S(2)}, u32[]{:S(2)}) async-start(bf16[16,16,256]{2,1,0:T(8,128)(2,1)} %get-tuple-element.49), calls=%async_computation.3 | async-start | bytes 262144 | tf_op jit(solution)/shard_map/all_to_all | solution.py:430
  122.8 7.0 %collective-permute-start.15 = (bf16[128,512]{1,0:T(8,128)(2,1)S(1)}, bf16[128,512]{1,0:T(8,128)(2,1)S(1)}, u32[]{:S(2)}, u32[]{:S(2)}) collective-permute-start(bf16[128,512]{1,0:T(8,128)(2,1)S(1)} %pad_maximum_fusion), channel_id=1, source_target_pairs={{0,4},{2,6},{4,0},{6,2},{8,12},{10,14},{12,8},{14,10},{16,20},{18,... | collective-permute-start | bytes 393224 | tf_op jit(solution)/shard_map/ppermute | solution.py:578
  129.8 4.4 %collective-permute-start.16 = (bf16[256,512]{1,0:T(8,128)(2,1)S(1)}, bf16[256,512]{1,0:T(8,128)(2,1)S(1)}, u32[]{:S(2)}, u32[]{:S(2)}) collective-permute-start(bf16[256,512]{1,0:T(8,128)(2,1)S(1)} %constant_dynamic-update-slice_fusion.own_ref), channel_id=1, source_target_pairs={{0,2},{2,0},{4,6},{6,4},{8,10},{10,8},{12,14},{14,12},{16,18},{18,... | collective-permute-start | bytes 786440 | tf_op jit(solution)/shard_map/ppermute | solution.py:578
  130.6 1.4 %copy-start.1 = (bf16[256,3072]{1,0:T(8,128)(2,1)S(1)}, bf16[256,3072]{1,0:T(8,128)(2,1)}, u32[]{:S(2)}) copy-start(bf16[256,3072]{1,0:T(8,128)(2,1)} %get-tuple-element.50.back_ref) | copy-start | bytes 4718596
  (2 other events, 1.4 us)
